TPU v7x, 32 devices: a whole 2x2x4 slice. The times are simulated.
32 devices in a mesh: gx: 4 (over z), gy: 8 (over y, x, core).
Axes of the slice: x: 2, y: 2, z: 4, core: 2. Of those that a mesh axis runs over, the one named last changes fastest.
Arguments:
- right_side: float32 [512, 2048], P('gx', 'gy'), may hold values from -1.2 to 1.2
- shift: float32 [512, 2048], P('gx', 'gy'), may hold values from 0.0001 to 0.004
Outputs:
- solution: float32 [512, 2048], P('gx', 'gy')
- residual: float32 [512, 2048], P('gx', 'gy')
All inputs are finite; a program needn't handle non-finite values.
Results may differ from a plain program's by a relative error of at most 0.0003.
Values sent between devices are 32-bit elements; how exact they have to be, the bound alone decides.
No kernel may reach another device: no remote copies, remote signals or barrier semaphores. Data moves between devices by JAX's collectives and lax.ppermute only.
A program may use at most 128 MiB of HBM per device.

v0:
```python
import jax
import jax.numpy as jnp
from jax import lax
from jax.sharding import PartitionSpec as P

LEVELS = 4
COARSE_SWEEPS = 6


damping = 0.8


def padded_2(cells, sides, width):
    for axis, dim in sides:
        count = lax.axis_size(axis)
        ends = count - 1
        head = lax.slice_in_dim(cells, 0, width, axis=dim)
        tail = lax.slice_in_dim(cells, cells.shape[dim] - width, cells.shape[dim], axis=dim)
        cells = jnp.concatenate(
            [
                lax.ppermute(tail, axis, [(i, (i + 1) % count) for i in range(ends)]),
                cells,
                lax.ppermute(head, axis, [((i + 1) % count, i) for i in range(ends)]),
            ],
            axis=dim,
        )
    return cells


def restrict(values):
    rows, columns = values.shape
    blocks = values.reshape(rows // 2, 2, columns // 2, 2)
    return 0.25 * (
        blocks[:, 0, :, 0] + blocks[:, 1, :, 0] + blocks[:, 0, :, 1] + blocks[:, 1, :, 1]
    )


def prolong(values):
    rows, columns = values.shape
    copies = jnp.broadcast_to(values[:, None, :, None], (rows, 2, columns, 2))
    return copies.reshape(2 * rows, 2 * columns)


def operate_padded(padded, shifts, level):
    centre = padded[1:-1, 1:-1]
    beside = padded[2:, 1:-1] + padded[:-2, 1:-1] + padded[1:-1, 2:] + padded[1:-1, :-2]
    return 4.0 ** (-level) * (4.0 * centre - beside) + shifts * centre


def with_rim(field):
    return padded_2(field, (("gx", 0), ("gy", 1)), 1)


def build_levels(shift):
    levels = []
    shifts = shift
    for level in range(LEVELS + 1):
        diagonal = 4.0 ** (1 - level) + shifts
        outer_shift = None
        inside = None
        levels.append((shifts, diagonal, outer_shift, inside))
        if level < LEVELS:
            shifts = restrict(shifts)
    return levels


def sweep_once(iterate, source, section, level):
    shifts, diagonal = (section[0], section[1])
    if iterate is None:
        return damping * source / diagonal
    return (
        iterate + damping * (source - operate_padded(with_rim(iterate), shifts, level)) / diagonal
    )


def smooth_two(iterate, source, section, level):
    iterate = sweep_once(iterate, source, section, level)
    return sweep_once(iterate, source, section, level)


def residual_of(iterate, source, section, level):
    return source - operate_padded(with_rim(iterate), section[0], level)


def gather_early(field):
    row_band = lax.all_gather(field, "gy", axis=1, tiled=True)
    return lax.all_gather(row_band, "gx", axis=0, tiled=True)


def local_sweeps(iterate, source, shifts, level, count):
    diagonal = 4.0 ** (1 - level) + shifts
    for turn in range(count):
        if iterate is None:
            iterate = damping * source / diagonal
        else:
            iterate = (
                iterate
                + damping * (source - operate_padded(jnp.pad(iterate, 1), shifts, level)) / diagonal
            )
    return iterate


def local_coarse(iterate, source, shifts):
    unit_total = jnp.sum(operate_padded(jnp.pad(jnp.ones_like(source), 1), shifts, LEVELS))
    if iterate is None:
        left = jnp.sum(source)
        iterate = jnp.zeros_like(source) + left / unit_total
    else:
        left = jnp.sum(source - operate_padded(jnp.pad(iterate, 1), shifts, LEVELS))
        iterate = iterate + left / unit_total
    return local_sweeps(iterate, source, shifts, LEVELS, COARSE_SWEEPS)


def local_vcycle(level, iterate, source, shift_table):
    shifts = shift_table[level]
    if level == LEVELS:
        return local_coarse(iterate, source, shifts)
    iterate = local_sweeps(iterate, source, shifts, level, 2)
    coarse_rhs = restrict(source - operate_padded(jnp.pad(iterate, 1), shifts, level))
    iterate = iterate + prolong(local_vcycle(level + 1, None, coarse_rhs, shift_table))
    return local_sweeps(iterate, source, shifts, level, 2)


def local_fcycle(level, source, shift_table):
    shifts = shift_table[level]
    if level == LEVELS:
        return local_coarse(None, source, shifts)
    iterate = local_sweeps(None, source, shifts, level, 2)
    coarse_rhs = restrict(source - operate_padded(jnp.pad(iterate, 1), shifts, level))
    correction = local_fcycle(level + 1, coarse_rhs, shift_table)
    correction = local_vcycle(level + 1, correction, coarse_rhs, shift_table)
    iterate = iterate + prolong(correction)
    return local_sweeps(iterate, source, shifts, level, 2)


def own_block(whole, rows, columns):
    return lax.dynamic_slice(
        whole, (lax.axis_index("gx") * rows, lax.axis_index("gy") * columns), (rows, columns)
    )


def early_solve(coarse_rhs, shift_table, full):
    whole_rhs = gather_early(coarse_rhs)
    if full:
        whole = local_fcycle(LEVELS - 1, whole_rhs, shift_table)
        whole = local_vcycle(LEVELS - 1, whole, whole_rhs, shift_table)
    else:
        whole = local_vcycle(LEVELS - 1, None, whole_rhs, shift_table)
    return own_block(whole, coarse_rhs.shape[0], coarse_rhs.shape[1])


def vcycle(level, iterate, source, levels, shift_whole):
    section = levels[level]
    iterate = smooth_two(iterate, source, section, level)
    coarse_rhs = restrict(residual_of(iterate, source, section, level))
    if level + 1 == LEVELS - 1:
        correction = early_solve(coarse_rhs, shift_whole, False)
    else:
        correction = vcycle(level + 1, None, coarse_rhs, levels, shift_whole)
    iterate = iterate + prolong(correction)
    return smooth_two(iterate, source, section, level)


def fcycle(level, source, levels, shift_whole):
    section = levels[level]
    iterate = smooth_two(None, source, section, level)
    coarse_rhs = restrict(residual_of(iterate, source, section, level))
    if level + 1 == LEVELS - 1:
        correction = early_solve(coarse_rhs, shift_whole, True)
    else:
        correction = fcycle(level + 1, coarse_rhs, levels, shift_whole)
        correction = vcycle(level + 1, correction, coarse_rhs, levels, shift_whole)
    iterate = iterate + prolong(correction)
    return smooth_two(iterate, source, section, level)


def body(right_side, shift):
    levels = build_levels(shift)
    upper = gather_early(levels[LEVELS - 1][0])
    shift_whole = {LEVELS - 1: upper, LEVELS: restrict(upper)}
    solution = fcycle(0, right_side, levels, shift_whole)
    residual = residual_of(solution, right_side, levels[0], 0)
    return (solution, residual)


def solution(mesh):
    in_specs = (P("gx", "gy"), P("gx", "gy"))
    out_specs = (P("gx", "gy"), P("gx", "gy"))
    return jax.shard_map(body, mesh=mesh, in_specs=in_specs, out_specs=out_specs, check_vma=False)
```

profile of v0, /device:TPU:28, one launch (start us, length us, event | category | flops | bytes accessed | tf_op | source)
XLA Modules:
  0.0 715.0 jit_solution(5198619085677997498)
XLA Ops:
  5.3 10.5 %reshape.185 = f32[64,2,128,2]{3,2,1,0:T(8,128)} reshape(f32[128,256]{1,0:T(8,128)} %param.3) | data formatting | bytes 262144 | tf_op jit(solution)/shard_map/reshape | solution.py:32
  20.4 8.0 %fusion.1 = f32[64,128]{1,0:T(8,128)S(1)} fusion(f32[64,2,128,2]{3,2,1,0:T(8,128)} %reshape.185), kind=kLoop, calls=%fused_computation.2 | loop fusion | flops 32768 | bytes 163840 | tf_op jit(solution)/shard_map/mul | solution.py:33
  30.7 4.5 collective-permute-start.4
  46.0 4.4 collective-permute-done.7
  50.5 9.8 %reshape.184 = f32[64,2,128,2]{3,2,1,0:T(8,128)} reshape(f32[128,256]{1,0:T(8,128)S(1)} %fusion.39) | data formatting | bytes 262144 | tf_op jit(solution)/shard_map/reshape | solution.py:32
  60.3 8.5 %multiply_reduce_fusion = (f32[64,128]{1,0:T(8,128)S(1)}, f32[64,128]{1,0:T(8,128)S(1)}) fusion(f32[64,2,128,2]{3,2,1,0:T(8,128)} %reshape.184), kind=kLoop, calls=%fused_computation.8 | loop fusion | flops 40960 | bytes 196608 | tf_op jit(solution)/shard_map/mul | solution.py:33
  72.8 14.8 %all-gather.2 = f32[16,1,256,1]{3,2,1,0:T(8,128)S(1)} all-gather(f32[16,1,32,1]{3,2,1,0:T(8,128)S(1)} %fusion.10), channel_id=4, replica_groups=mesh['gx'=4,'gy'=8] {'gy'}, dimensions={2}, use_global_device_ids=true | all-gather | bytes 18432 | tf_op jit(solution)/shard_map/all_gather | solution.py:86
  93.7 13.6 %all-gather.3 = f32[64,1,256,1]{2,3,1,0:T(1,128)S(1)} all-gather(f32[16,1,256,1]{2,3,1,0:T(1,128)S(1)} %copy.135), channel_id=5, replica_groups=mesh['gx'=4,'gy'=8] {'gx'}, dimensions={0}, use_global_device_ids=true | all-gather | bytes 81920 | tf_op jit(solution)/shard_map/all_gather | solution.py:87
  111.4 5.6 reshape.189
  128.6 4.5 collective-permute-start.16
  163.9 14.8 %all-gather = f32[16,1,256,1]{3,2,1,0:T(8,128)S(1)} all-gather(f32[16,1,32,1]{3,2,1,0:T(8,128)S(1)} %fusion.11), channel_id=2, replica_groups=mesh['gx'=4,'gy'=8] {'gy'}, dimensions={2}, use_global_device_ids=true | all-gather | bytes 18432 | tf_op jit(solution)/shard_map/all_gather | solution.py:86
  179.3 13.1 %all-gather.1 = f32[64,1,256,1]{2,3,1,0:T(1,128)S(1)} all-gather(f32[16,1,256,1]{2,3,1,0:T(1,128)S(1)} %copy.134), channel_id=3, replica_groups=mesh['gx'=4,'gy'=8] {'gx'}, dimensions={0}, use_global_device_ids=true | all-gather | bytes 81920 | tf_op jit(solution)/shard_map/all_gather | solution.py:87
  192.7 5.6 reshape.188
  198.3 8.6 %multiply_reduce_fusion.6 = (f32[32,128]{1,0:T(8,128)S(1)}, f32[32,1,128,1]{3,2,1,0:T(8,128)S(1)}, f32[]{:T(128)}, f32[32,128]{1,0:T(8,128)S(1)}) fusion(f32[32,2,128,2]{3,2,1,0:T(8,128)} %reshape.189, f32[32,2,128,2]{3,2,1,0:T(8,128)} %reshape.188), kind=kLoop, calls=%fused_computation.33 | loop fusion | flops 36863 | bytes 180228 | tf_op jit(solution)/shard_map/mul | solution.py:33
  220.0 5.6 reshape.191
  225.6 5.8 fusion.727
  241.3 10.9 %collective-permute-start.24 = (f32[1,64]{1,0:T(1,128)S(1)}, f32[1,64]{1,0:T(1,128)S(1)}, u32[]{:S(2)}, u32[]{:S(2)}) collective-permute-start(f32[1,64]{1,0:T(1,128)S(1)} %get-tuple-element.123), channel_id=1, source_target_pairs={{8,0},{16,8},{24,16},{9,1},{17,9},{25,17},{10,2},{18,10},{26,18},{... | collective-permute-start | bytes 776 | tf_op jit(solution)/shard_map/ppermute | solution.py:23
  269.9 4.2 collective-permute-done.29
  331.4 15.1 %all-gather.4 = f32[16,1,256,1]{3,2,1,0:T(8,128)} all-gather(f32[16,1,32,1]{3,2,1,0:T(8,128)S(1)} %fusion.9), channel_id=6, replica_groups=mesh['gx'=4,'gy'=8] {'gy'}, dimensions={2}, use_global_device_ids=true | all-gather | bytes 18432 | tf_op jit(solution)/shard_map/all_gather | solution.py:86
  348.7 13.1 %all-gather.5 = f32[64,1,256,1]{2,3,1,0:T(1,128)S(1)} all-gather(f32[16,1,256,1]{2,3,1,0:T(1,128)S(1)} %copy.136), channel_id=7, replica_groups=mesh['gx'=4,'gy'=8] {'gx'}, dimensions={0}, use_global_device_ids=true | all-gather | bytes 81920 | tf_op jit(solution)/shard_map/all_gather | solution.py:87
  362.1 5.6 reshape.195
  367.7 5.8 fusion.726
  423.2 4.2 collective-permute-done.53
  537.2 15.1 %all-gather.6 = f32[16,1,256,1]{3,2,1,0:T(8,128)} all-gather(f32[16,1,32,1]{3,2,1,0:T(8,128)S(1)} %fusion.8), channel_id=8, replica_groups=mesh['gx'=4,'gy'=8] {'gy'}, dimensions={2}, use_global_device_ids=true | all-gather | bytes 18432 | tf_op jit(solution)/shard_map/all_gather | solution.py:86
  554.5 13.1 %all-gather.7 = f32[64,1,256,1]{2,3,1,0:T(1,128)S(1)} all-gather(f32[16,1,256,1]{2,3,1,0:T(1,128)S(1)} %copy.137), channel_id=9, replica_groups=mesh['gx'=4,'gy'=8] {'gx'}, dimensions={0}, use_global_device_ids=true | all-gather | bytes 81920 | tf_op jit(solution)/shard_map/all_gather | solution.py:87
  567.9 5.6 reshape.201
  573.4 5.8 fusion.725
  626.3 4.2 collective-permute-done.89
  658.5 6.9 reshape.205
  668.7 4.2 collective-permute-done.97
  684.8 4.2 collective-permute-done.101
  701.0 4.2 collective-permute-done.105
  (441 shorter events, 445.1 us)
Async XLA Ops:
  1.6 14.2 %collective-permute-start = (f32[1,256]{1,0:T(1,128)S(1)}, f32[1,256]{1,0:T(1,128)S(1)}, u32[]{:S(2)}, u32[]{:S(2)}) collective-permute-start(f32[1,256]{1,0:T(1,128)S(1)} %get-tuple-element.37), channel_id=1, source_target_pairs={{8,0},{16,8},{24,16},{9,1},{17,9},{25,17},{10,2},{18,10},{26,18},{... | collective-permute-start | bytes 3080 | tf_op jit(solution)/shard_map/ppermute | solution.py:23
  4.0 11.8 %collective-permute-start.1 = (f32[1,256]{1,0:T(1,128)S(1)}, f32[1,256]{1,0:T(1,128)S(1)}, u32[]{:S(2)}, u32[]{:S(2)}) collective-permute-start(f32[1,256]{1,0:T(1,128)S(1)} %get-tuple-element.36), channel_id=1, source_target_pairs={{0,8},{8,16},{16,24},{1,9},{9,17},{17,25},{2,10},{10,18},{18,26},{... | collective-permute-start | bytes 3080 | tf_op jit(solution)/shard_map/ppermute | solution.py:21
  16.0 14.6 %collective-permute-start.2 = (f32[130,1]{1,0:T(8,128)S(1)}, f32[130,1]{1,0:T(8,128)S(1)}, u32[]{:S(2)}, u32[]{:S(2)}) collective-permute-start(f32[130,1]{1,0:T(8,128)S(1)} %get-tuple-element.26), channel_id=1, source_target_pairs={{1,0},{2,1},{3,2},{4,3},{5,4},{6,5},{7,6},{9,8},{10,9},{11,10},{12... | collective-permute-start | bytes 1568 | tf_op jit(solution)/shard_map/ppermute | solution.py:23
  18.5 12.1 %collective-permute-start.3 = (f32[130,1]{1,0:T(8,128)S(1)}, f32[130,1]{1,0:T(8,128)S(1)}, u32[]{:S(2)}, u32[]{:S(2)}) collective-permute-start(f32[130,1]{1,0:T(8,128)S(1)} %get-tuple-element.27), channel_id=1, source_target_pairs={{0,1},{1,2},{2,3},{3,4},{4,5},{5,6},{6,7},{8,9},{9,10},{10,11},{11... | collective-permute-start | bytes 1568 | tf_op jit(solution)/shard_map/ppermute | solution.py:21
  30.7 7.2 %collective-permute-start.4 = (f32[1,256]{1,0:T(1,128)S(1)}, f32[1,256]{1,0:T(1,128)S(1)}, u32[]{:S(2)}, u32[]{:S(2)}) collective-permute-start(f32[1,256]{1,0:T(1,128)S(1)} %get-tuple-element.35), channel_id=1, source_target_pairs={{8,0},{16,8},{24,16},{9,1},{17,9},{25,17},{10,2},{18,10},{26,18},{... | collective-permute-start | bytes 3080 | tf_op jit(solution)/shard_map/ppermute | solution.py:23
  43.8 6.5 collective-permute-start.7
  68.9 19.4 %collective-permute-start.8 = (f32[1,128]{1,0:T(1,128)S(1)}, f32[1,128]{1,0:T(1,128)S(1)}, u32[]{:S(2)}, u32[]{:S(2)}) collective-permute-start(f32[1,128]{1,0:T(1,128)S(1)} %get-tuple-element.75), channel_id=1, source_target_pairs={{8,0},{16,8},{24,16},{9,1},{17,9},{25,17},{10,2},{18,10},{26,18},{... | collective-permute-start | bytes 1544 | tf_op jit(solution)/shard_map/ppermute | solution.py:23
  71.5 16.8 %collective-permute-start.9 = (f32[1,128]{1,0:T(1,128)S(1)}, f32[1,128]{1,0:T(1,128)S(1)}, u32[]{:S(2)}, u32[]{:S(2)}) collective-permute-start(f32[1,128]{1,0:T(1,128)S(1)} %get-tuple-element.74), channel_id=1, source_target_pairs={{0,8},{8,16},{16,24},{1,9},{9,17},{17,25},{2,10},{10,18},{18,26},{... | collective-permute-start | bytes 1544 | tf_op jit(solution)/shard_map/ppermute | solution.py:21
  88.4 18.9 %collective-permute-start.10 = (f32[66,1]{1,0:T(8,128)S(1)}, f32[66,1]{1,0:T(8,128)S(1)}, u32[]{:S(2)}, u32[]{:S(2)}) collective-permute-start(f32[66,1]{1,0:T(8,128)S(1)} %get-tuple-element.56), channel_id=1, source_target_pairs={{1,0},{2,1},{3,2},{4,3},{5,4},{6,5},{7,6},{9,8},{10,9},{11,10},{12... | collective-permute-start | bytes 800 | tf_op jit(solution)/shard_map/ppermute | solution.py:23
  91.7 15.5 %collective-permute-start.11 = (f32[66,1]{1,0:T(8,128)S(1)}, f32[66,1]{1,0:T(8,128)S(1)}, u32[]{:S(2)}, u32[]{:S(2)}) collective-permute-start(f32[66,1]{1,0:T(8,128)S(1)} %get-tuple-element.57), channel_id=1, source_target_pairs={{0,1},{1,2},{2,3},{3,4},{4,5},{5,6},{6,7},{8,9},{9,10},{10,11},{11... | collective-permute-start | bytes 800 | tf_op jit(solution)/shard_map/ppermute | solution.py:21
  107.4 9.6 %collective-permute-start.12 = (f32[1,128]{1,0:T(1,128)S(1)}, f32[1,128]{1,0:T(1,128)S(1)}, u32[]{:S(2)}, u32[]{:S(2)}) collective-permute-start(f32[1,128]{1,0:T(1,128)S(1)} %get-tuple-element.73), channel_id=1, source_target_pairs={{8,0},{16,8},{24,16},{9,1},{17,9},{25,17},{10,2},{18,10},{26,18},{... | collective-permute-start | bytes 1544 | tf_op jit(solution)/shard_map/ppermute | solution.py:23
  110.0 7.0 collective-permute-start.13
  119.0 6.2 collective-permute-start.15
  140.6 6.0 collective-permute-start.19
  157.0 6.0 collective-permute-start.23
  241.3 12.2 %collective-permute-start.24 = (f32[1,64]{1,0:T(1,128)S(1)}, f32[1,64]{1,0:T(1,128)S(1)}, u32[]{:S(2)}, u32[]{:S(2)}) collective-permute-start(f32[1,64]{1,0:T(1,128)S(1)} %get-tuple-element.123), channel_id=1, source_target_pairs={{8,0},{16,8},{24,16},{9,1},{17,9},{25,17},{10,2},{18,10},{26,18},{... | collective-permute-start | bytes 776 | tf_op jit(solution)/shard_map/ppermute | solution.py:23
  259.7 6.0 collective-permute-start.27
  276.0 6.0 collective-permute-start.31
  293.5 6.0 collective-permute-start.35
  392.2 6.0 collective-permute-start.47
  429.3 6.2 collective-permute-start.55
  445.0 6.2 collective-permute-start.59
  460.9 6.2 collective-permute-start.63
  476.7 6.2 collective-permute-start.67
  492.4 6.2 collective-permute-start.71
  514.8 6.0 collective-permute-start.75
  615.4 6.0 collective-permute-start.87
  632.5 6.2 collective-permute-start.91
  648.2 6.2 collective-permute-start.95
  674.9 6.5 collective-permute-start.99
  691.0 6.5 collective-permute-start.103
  707.2 6.5 collective-permute-start.107
  (79 other events, 371.7 us)
where the time goes:
time: 727 us; the launch traced here: 715 us
  starting transfers between devices  227 us (31%)
  waiting for transfers between devices  192 us (26%)
  blocking collectives  113 us (16%)
  local copies, waits for them, and re-layouts  110 us (15%)
  other arithmetic  62.6 us (9%)
  between operations  10.1 us (1%)
    ppermute x54, waiting for transfers between devices, padded_2(): lax.ppermute(tail, axis, [(i, (i + 1) % count) for i in range(ends)])  191 us
    ppermute x54, starting transfers between devices, padded_2(): lax.ppermute(head, axis, [((i + 1) % count, i) for i in range(ends)])  129 us
    ppermute x54, starting transfers between devices, padded_2(): lax.ppermute(tail, axis, [(i, (i + 1) % count) for i in range(ends)])  98.4 us
    all_gather x4, blocking collectives, gather_early(): row_band = lax.all_gather(field, 'gy', axis=1, tiled=True)  59.9 us
    reshape x12, local copies, waits for them, and re-layouts, restrict(): blocks = values.reshape(rows // 2, 2, columns // 2, 2)  55.2 us
    all_gather x4, blocking collectives, gather_early(): return lax.all_gather(row_band, 'gx', axis=0, tiled=True)  53 us
    mul x13, other arithmetic, restrict(): 0.25 * (blocks[:, 0, :, 0] + blocks[:, 1, :, 0] + blocks[:, 0, :, 1] + bl...  48.9 us
    reshape x10, local copies, waits for them, and re-layouts, prolong(): return copies.reshape(2 * rows, 2 * columns)  27.8 us
  transfers between devices with their start and end apart: 108, of which 49 were waited for; matrix products, arithmetic and copies ran while one was open for 4% of the time, Pallas kernels for 0%

commit v1 on v0

v1 whole, which is shorter than its diff:
```python
import numpy as np
import jax
import jax.numpy as jnp
from jax import lax
from jax.experimental import pallas as pl
from jax.experimental.pallas import tpu as pltpu
from jax.sharding import PartitionSpec as P

LEVELS = 4
COARSE_SWEEPS = 6
DAMPING = 0.8
HALO = 24


def f32dot_right(values, onehot):
    high = values.astype(jnp.bfloat16)
    rest = values - high.astype(jnp.float32)
    middle = rest.astype(jnp.bfloat16)
    low = (rest - middle.astype(jnp.float32)).astype(jnp.bfloat16)
    rows = values.shape[0]
    stacked = jnp.concatenate([high, middle, low], axis=0)
    out = jnp.dot(stacked, onehot, preferred_element_type=jnp.float32)
    return (out[2 * rows :] + out[rows : 2 * rows]) + out[:rows]


def f32dot_left(onehot, values):
    high = values.astype(jnp.bfloat16)
    rest = values - high.astype(jnp.float32)
    middle = rest.astype(jnp.bfloat16)
    low = (rest - middle.astype(jnp.float32)).astype(jnp.bfloat16)
    total = jnp.dot(onehot, low, preferred_element_type=jnp.float32)
    total = total + jnp.dot(onehot, middle, preferred_element_type=jnp.float32)
    return total + jnp.dot(onehot, high, preferred_element_type=jnp.float32)


def around(v):
    rows, columns = v.shape
    up = pltpu.roll(v, 1, 0)
    down = pltpu.roll(v, rows - 1, 0)
    left = pltpu.roll(v, 1, 1)
    right = pltpu.roll(v, columns - 1, 1)
    return (up + down) + (left + right)


def sweep(v, g, w):
    return (1.0 - DAMPING) * v + w * (g + around(v))


class Sizes:
    def __init__(self, rows, columns, nx, ny):
        self.rows, self.columns, self.nx, self.ny = rows, columns, nx, ny
        self.p, self.q = rows // 16, columns // 16
        self.lanes = self.p * self.q
        self.devices = nx * ny

        def up(n):
            return -(-n // 128) * 128

        self.ext_rows = [(rows + 2 * HALO) >> l for l in range(3)]
        self.ext_columns = [up((columns + 2 * HALO) >> l) for l in range(3)]

    def column_at(self, level):
        own, halo, width = self.columns >> level, HALO >> level, self.ext_columns[level]
        lane = np.arange(width)
        inside = (lane < own + halo) | (lane >= width - halo)
        return np.where(lane < own + halo, lane, lane - width), inside

    def row_at(self, level):
        own, halo, height = self.rows >> level, HALO >> level, self.ext_rows[level]
        row = np.arange(height)
        return np.where(row < own + halo, row, row - height)

    def restrict_columns(self):
        fine, fine_in = self.column_at(0)
        coarse, coarse_in = self.column_at(1)
        hit = (fine[:, None] // 2 == coarse[None, :]) & fine_in[:, None] & coarse_in[None, :]
        return hit.astype(jnp.bfloat16)

    def pack_columns(self):
        x = np.arange(self.columns // 2)[:, None, None]
        r = np.arange(4)[None, :, None]
        lane = np.arange(self.lanes)[None, None, :]
        hit = x // 2 == 4 * (lane // self.p) + r
        return hit.reshape(self.columns // 2, 4 * self.lanes).astype(jnp.bfloat16)

    def pack_rows(self, fields):
        count = self.rows // 4
        f = np.arange(fields)
        s = np.arange(4)
        k = np.arange(count)
        hit = (f[:, None, None, None] == f[None, None, :, None]) & (k[None, None, None, :] % 4 == s[None, :, None, None])
        hit = hit.reshape(fields * 4, fields * count)
        pad = -hit.shape[0] % 8
        return np.pad(hit, ((0, pad), (0, 0))).astype(jnp.bfloat16)

    def spread_rows(self):
        k = self.row_at(1) // 2
        count = self.rows // 4
        block = k // count
        s = (k % count) % 4
        slot = (block + 1) * 4 + s
        return (slot[:, None] == np.arange(16)[None, :]).astype(jnp.bfloat16)

    def spread_columns(self):
        column, inside = self.column_at(1)
        m = column // 2
        count = self.columns // 4
        block = m // count
        r = (m % count) % 4
        q = (m % count) // 4
        beside = np.arange(2)[:, None, None, None]
        rr = np.arange(4)[None, :, None, None]
        lane = np.arange(self.lanes)[None, None, :, None]
        hit = ((block != 0) == beside) & (r == rr) & (q == lane // self.p) & inside
        return hit.reshape(8 * self.lanes, -1).astype(jnp.bfloat16)


def iota(shape, axis):
    return lax.broadcasted_iota(jnp.int32, shape, axis)


def inside_mask(sizes, level, gx, gy):
    shape = (sizes.ext_rows[level], sizes.ext_columns[level])
    own_r, own_c, halo = sizes.rows >> level, sizes.columns >> level, HALO >> level
    row, column = iota(shape, 0), iota(shape, 1)
    last_row = jnp.where(gx < sizes.nx - 1, own_r + halo, own_r)
    first_row = jnp.where(gx > 0, own_r + halo, shape[0])
    last_column = jnp.where(gy < sizes.ny - 1, own_c + halo, own_c)
    first_column = jnp.where(gy > 0, shape[1] - halo, shape[1])
    return ((row < last_row) | (row >= first_row)) & ((column < last_column) | (column >= first_column))


def pair_rows(scratch, values):
    rows, columns = values.shape
    outs = []
    for t in range(columns // 128):
        scratch[t, :rows, :] = values[:, t * 128 : (t + 1) * 128]
    for t in range(columns // 128):
        outs.append(scratch[t, pl.ds(0, rows // 2, stride=2), :] + scratch[t, pl.ds(1, rows // 2, stride=2), :])
    return jnp.concatenate(outs, axis=1)


def pack(sizes, scratch, fields, columns_ref, rows_ref, out_ref):
    own_r, own_c = sizes.rows // 2, sizes.columns // 2
    count = own_r // 2
    summed = jnp.concatenate([pair_rows(scratch, f[:own_r, :own_c]) for f in fields], axis=0)
    spread = f32dot_right(summed, columns_ref[...])
    shape = spread.shape
    keep = ((iota(shape, 0) % count) // 4) == (iota(shape, 1) % sizes.p)
    spread = jnp.where(keep, spread, 0.0)
    out = f32dot_left(rows_ref[...], spread)
    n = 4 * len(fields)
    for r in range(4):
        out_ref[r * n : (r + 1) * n, :] = out[:n, r * sizes.lanes : (r + 1) * sizes.lanes]


def down_kernel(sizes, at_ref, g_ref, s_ref, left_ref, right_ref, rc_ref, pc_ref, pr_ref,
                g0_ref, d0_ref, w0_ref, v0_ref, c1_ref, d1_ref, w1_ref, v1_ref, out_ref, scratch):
    gx, gy = at_ref[0], at_ref[1]
    rows, columns = sizes.ext_rows[0], sizes.ext_columns[0]
    lane = iota((rows, 128), 1)
    beside = []
    for k in range(2):
        beside.append(jnp.where(lane < HALO, right_ref[k], left_ref[k]))
    g = jnp.concatenate([g_ref[...], beside[0]], axis=1)
    sigma = jnp.concatenate([s_ref[...], beside[1]], axis=1)
    d = 4.0 + sigma
    w = jnp.where(inside_mask(sizes, 0, gx, gy), DAMPING / d, 0.0)
    v = w * g
    v = sweep(v, g, w)
    r = g - d * v + around(v)
    g0_ref[...] = g
    d0_ref[...] = d
    w0_ref[...] = w
    v0_ref[...] = v
    half = rows // 2
    both = jnp.concatenate([pair_rows(scratch, r), pair_rows(scratch, sigma)], axis=0)
    both = f32dot_right(both, rc_ref[...])
    g, sigma = both[:half], both[half:]
    d = 4.0 + sigma
    w = jnp.where(inside_mask(sizes, 1, gx, gy), DAMPING / d, 0.0)
    v = w * g
    v = sweep(v, g, w)
    r = g - d * v + around(v)
    c1_ref[...] = g
    d1_ref[...] = d
    w1_ref[...] = w
    v1_ref[...] = v
    pack(sizes, scratch, [r, sigma], pc_ref, pr_ref, out_ref)


class Coarse:
    def __init__(self, sizes, d_refs, w_refs, g_refs, v_refs, t_refs):
        self.z = sizes
        self.d, self.w, self.g, self.v, self.t = d_refs, w_refs, g_refs, v_refs, t_refs
        shape = (sizes.ny, sizes.lanes)
        lane, row = iota(shape, 1), iota(shape, 0)
        p, q = lane % sizes.p, lane // sizes.p
        self.first_p, self.last_p = p == 0, p == sizes.p - 1
        self.first_q, self.last_q = q == 0, q == sizes.q - 1
        self.first_row, self.last_row = row == 0, row == sizes.ny - 1

    def blocks(self, body):
        if self.z.nx <= 4:
            for gx in range(self.z.nx):
                body((gx + 1) * self.z.ny)
        else:
            def step(gx, carry):
                body(pl.multiple_of((gx + 1) * self.z.ny, 8))
                return carry

            lax.fori_loop(0, self.z.nx, step, 0)

    def at(self, ref, s, r, base):
        return ref[s, r, pl.ds(base, self.z.ny), :]

    def put(self, ref, s, r, base, value):
        ref[s, r, pl.ds(base, self.z.ny), :] = value

    def neighbours(self, ref, s, r, n, base):
        z = self.z
        if r < n - 1:
            right = self.at(ref, s, r + 1, base)
        else:
            x = self.at(ref, s, 0, base)
            moved = jnp.where(self.last_row, 0.0, pltpu.roll(x, z.ny - 1, 0))
            right = pltpu.roll(jnp.where(self.first_q, moved, x), z.lanes - z.p, 1)
        if r > 0:
            left = self.at(ref, s, r - 1, base)
        else:
            x = self.at(ref, s, n - 1, base)
            moved = jnp.where(self.first_row, 0.0, pltpu.roll(x, 1, 0))
            left = pltpu.roll(jnp.where(self.last_q, moved, x), z.p, 1)
        if s < n - 1:
            down = self.at(ref, s + 1, r, base)
        else:
            here = pltpu.roll(self.at(ref, 0, r, base), z.lanes - 1, 1)
            there = pltpu.roll(self.at(ref, 0, r, base + z.ny), z.p - 1, 1)
            down = jnp.where(self.last_p, there, here)
        if s > 0:
            up = self.at(ref, s - 1, r, base)
        else:
            here = pltpu.roll(self.at(ref, n - 1, r, base), 1, 1)
            there = pltpu.roll(self.at(ref, n - 1, r, base - z.ny), z.lanes - z.p + 1, 1)
            up = jnp.where(self.first_p, there, here)
        return (up + down) + (left + right)

    def each(self, level, body):
        n = 1 << (LEVELS - level)

        def block(base):
            for s in range(n):
                for r in range(n):
                    body(s, r, n, base)

        self.blocks(block)

    def first_sweep(self, level):
        l = level - 2

        def body(s, r, n, base):
            self.put(self.v[l], s, r, base, self.at(self.w[l], s, r, base) * self.at(self.g[l], s, r, base))

        self.each(level, body)

    def sweep(self, level, source, target):
        l = level - 2

        def body(s, r, n, base):
            v = self.at(source, s, r, base)
            total = self.at(self.g[l], s, r, base) + self.neighbours(source, s, r, n, base)
            self.put(target, s, r, base, (1.0 - DAMPING) * v + self.at(self.w[l], s, r, base) * total)

        self.each(level, body)

    def two_sweeps(self, level):
        l = level - 2
        self.sweep(level, self.v[l], self.t[l])
        self.sweep(level, self.t[l], self.v[l])

    def start(self, level):
        l = level - 2
        self.first_sweep(level)
        self.sweep(level, self.v[l], self.t[l])
        self.v[l], self.t[l] = self.t[l], self.v[l]

    def residual(self, level, s, r, n, base):
        l = level - 2
        v = self.at(self.v[l], s, r, base)
        g = self.at(self.g[l], s, r, base)
        return (g - self.at(self.d[l], s, r, base) * v) + self.neighbours(self.v[l], s, r, n, base)

    def restrict(self, level):
        l = level - 2
        n = 1 << (LEVELS - level)

        def block(base):
            for s in range(n // 2):
                for r in range(n // 2):
                    parts = [self.residual(level, 2 * s + a, 2 * r + b, n, base) for a in (0, 1) for b in (0, 1)]
                    self.put(self.g[l + 1], s, r, base, (parts[0] + parts[1]) + (parts[2] + parts[3]))

        self.blocks(block)

    def prolong(self, level):
        l = level - 2

        def body(s, r, n, base):
            e = self.at(self.v[l + 1], s // 2, r // 2, base)
            self.put(self.v[l], s, r, base, self.at(self.v[l], s, r, base) + e)

        self.each(level, body)

    def total(self, of):
        z = self.z
        if z.nx <= 4:
            parts = [of((gx + 1) * z.ny) for gx in range(z.nx)]
            value = parts[0]
            for part in parts[1:]:
                value = value + part
        else:
            value = lax.fori_loop(
                0, z.nx, lambda gx, acc: acc + of(pl.multiple_of((gx + 1) * z.ny, 8)),
                jnp.zeros((z.ny, z.lanes), jnp.float32))
        return jnp.sum(jnp.sum(value, axis=0, keepdims=True), axis=1, keepdims=True)

    def unit(self):
        z = self.z
        top = LEVELS - 2
        missing = 2.0 * (z.nx * z.p + z.ny * z.q) - 0.0
        cells = 4.0
        total = self.total(lambda base: self.at(self.d[top], 0, 0, base) - cells)
        return total + missing

    def coarse(self, fresh, unit):
        top = LEVELS - 2
        v, t, g = self.v[top], self.t[top], self.g[top]
        if fresh:
            left = self.total(lambda base: self.at(g, 0, 0, base)) / unit

            def body(base):
                self.put(v, 0, 0, base, jnp.broadcast_to(left, (self.z.ny, self.z.lanes)))
        else:
            left = self.total(lambda base: self.residual(LEVELS, 0, 0, 1, base)) / unit

            def body(base):
                self.put(v, 0, 0, base, self.at(v, 0, 0, base) + left)

        self.blocks(body)
        for turn in range(COARSE_SWEEPS // 2):
            self.sweep(LEVELS, v, t)
            self.sweep(LEVELS, t, v)

    def vcycle(self, level, fresh, unit):
        if level == LEVELS:
            self.coarse(fresh, unit)
            return
        if fresh:
            self.start(level)
        else:
            self.two_sweeps(level)
        self.restrict(level)
        self.vcycle(level + 1, True, unit)
        self.prolong(level)
        self.two_sweeps(level)

    def fcycle(self, level, unit):
        if level == LEVELS:
            self.coarse(True, unit)
            return
        self.start(level)
        self.restrict(level)
        self.fcycle(level + 1, unit)
        self.vcycle(level + 1, False, unit)
        self.prolong(level)
        self.two_sweeps(level)

    def clear_ends(self):
        z = self.z
        zero = jnp.zeros((z.ny, z.lanes), jnp.float32)
        for refs in (self.v, self.t):
            for ref in refs:
                n = ref.shape[0]
                for s in range(n):
                    for r in range(n):
                        ref[s, r, : z.ny, :] = zero
                        ref[s, r, (z.nx + 1) * z.ny :, :] = zero

    def take(self, y_ref, target, count, offset, add):
        z = self.z

        def block(base):
            for s in range(4):
                for r in range(4):
                    first = (base - z.ny) * 4 * count + r * count + offset + s
                    value = y_ref[pl.ds(first, z.ny, stride=4 * count), :]
                    self.put(target, s, r, base, value + add if add else value)

        self.blocks(block)

    def spread(self, gx, gy, rows_ref, columns_ref, e_ref):
        z = self.z
        row = (gx + 1) * z.ny + gy
        lane = iota((1, z.lanes), 1)
        low_half = lane // z.p < z.q // 2
        has_left, has_right = gy > 0, gy < z.ny - 1
        e_ref[12:, :] = jnp.zeros((4, 8 * z.lanes), jnp.float32)
        for dx in range(3):
            base = row + (dx - 1) * z.ny
            for s in range(4):
                for r in range(4):
                    ref = self.v[0]
                    own = ref[s, r, pl.ds(base, 1), :]
                    left = ref[s, r, pl.ds(jnp.where(has_left, base - 1, 0), 1), :]
                    right = ref[s, r, pl.ds(jnp.where(has_right, base + 1, 0), 1), :]
                    k = dx * 4 + s
                    e_ref[k : k + 1, r * z.lanes : (r + 1) * z.lanes] = own
                    e_ref[k : k + 1, (4 + r) * z.lanes : (5 + r) * z.lanes] = jnp.where(low_half, right, left)
        spread = f32dot_left(rows_ref[...], e_ref[...])
        shape = spread.shape
        index = iota(shape, 0)
        own_r, halo = z.rows // 2, HALO // 2
        cell = jnp.where(index < own_r + halo, index, index - shape[0]) + 2 * z.rows
        keep = ((cell // 8) % z.p) == (iota(shape, 1) % z.p)
        spread = jnp.where(keep, spread, 0.0)
        return f32dot_right(spread, columns_ref[...])


def level_shape(sizes, level):
    n = 1 << (LEVELS - level)
    return (n, n, (sizes.nx + 2) * sizes.ny, sizes.lanes)


def middle_kernel(sizes, at_ref, y_ref, c1_ref, d1_ref, w1_ref, v1_ref, sr_ref, sc_ref, pc_ref, pr_ref,
                  d2_ref, d3_ref, d4_ref, w2_ref, w3_ref, w4_ref, e1_ref, out_ref,
                  g2, g3, g4, v2, v3, v4, t2, t3, t4, e_ref, scratch):
    gx, gy = at_ref[0], at_ref[1]
    m = Coarse(sizes, [d2_ref, d3_ref, d4_ref], [w2_ref, w3_ref, w4_ref], [g2, g3, g4], [v2, v3, v4], [t2, t3, t4])
    m.clear_ends()
    m.take(y_ref, g2, 8, 0, 0.0)
    m.take(y_ref, d2_ref, 8, 4, 4.0)
    for l in range(2):
        n = 2 >> l

        def block(base):
            for s in range(n):
                for r in range(n):
                    parts = [m.at(m.d[l], 2 * s + a, 2 * r + b, base) for a in (0, 1) for b in (0, 1)]
                    m.put(m.d[l + 1], s, r, base, ((parts[0] + parts[1]) + (parts[2] + parts[3])) - 12.0)

        m.blocks(block)
    for l in range(3):
        def body(s, r, n, base):
            m.put(m.w[l], s, r, base, DAMPING / m.at(m.d[l], s, r, base))

        m.each(l + 2, body)
    unit = m.unit()
    m.fcycle(2, unit)
    m.vcycle(2, False, unit)
    g, d, w = c1_ref[...], d1_ref[...], w1_ref[...]
    v = v1_ref[...] + jnp.where(w > 0.0, m.spread(gx, gy, sr_ref, sc_ref, e_ref), 0.0)
    for turn in range(4):
        v = sweep(v, g, w)
    e1_ref[...] = v
    r = g - d * v + around(v)
    pack(sizes, scratch, [r], pc_ref, pr_ref, out_ref)


def up_kernel(sizes, at_ref, y_ref, d2_ref, d3_ref, d4_ref, w2_ref, w3_ref, w4_ref, c1_ref, w1_ref, e1_ref,
              g0_ref, d0_ref, w0_ref, v0_ref, sr_ref, sc_ref, rt_ref,
              solution_ref, residual_ref, g2, g3, g4, v2, v3, v4, t2, t3, t4, e_ref, scratch):
    gx, gy = at_ref[0], at_ref[1]
    m = Coarse(sizes, [d2_ref, d3_ref, d4_ref], [w2_ref, w3_ref, w4_ref], [g2, g3, g4], [v2, v3, v4], [t2, t3, t4])
    m.clear_ends()
    m.take(y_ref, g2, 4, 0, 0.0)
    unit = m.unit()
    m.vcycle(2, True, unit)
    g, w = c1_ref[...], w1_ref[...]
    v = e1_ref[...] + jnp.where(w > 0.0, m.spread(gx, gy, sr_ref, sc_ref, e_ref), 0.0)
    for turn in range(2):
        v = sweep(v, g, w)
    wide = f32dot_right(v, rt_ref[...])
    half = wide.shape[0]
    tiles = wide.shape[1] // 128
    for t in range(tiles):
        part = wide[:, t * 128 : (t + 1) * 128]
        scratch[t, pl.ds(0, half, stride=2), :] = part
        scratch[t, pl.ds(1, half, stride=2), :] = part
    g, d, w = g0_ref[...], d0_ref[...], w0_ref[...]
    v = v0_ref[...] + jnp.concatenate([scratch[t] for t in range(tiles)], axis=1)
    for turn in range(2):
        v = sweep(v, g, w)
    r = g - d * v + around(v)
    solution_ref[...] = v[: sizes.rows, : sizes.columns]
    residual_ref[...] = r[: sizes.rows, : sizes.columns]


def vmem(count):
    return [pl.BlockSpec(memory_space=pltpu.VMEM)] * count


def call(kernel, sizes, outs, scratch, *operands):
    shapes = [jax.ShapeDtypeStruct(shape, jnp.float32) for shape in outs]
    return pl.pallas_call(
        lambda *refs: kernel(sizes, *refs),
        name=kernel.__name__,
        out_shape=shapes,
        in_specs=[pl.BlockSpec(memory_space=pltpu.SMEM)] + vmem(len(operands) - 1),
        out_specs=vmem(len(outs)),
        scratch_shapes=[pltpu.VMEM(shape, jnp.float32) for shape in scratch],
    )(*operands)


def ring(values, axis, step):
    count = lax.axis_size(axis)
    return lax.ppermute(values, axis, [(i, (i + step) % count) for i in range(count)])


def gather(block, axes):
    count = lax.axis_size(axes)
    copies = jnp.broadcast_to(block[None], (count,) + block.shape)
    out = lax.all_to_all(copies, axes, 0, 0, tiled=True)
    return out.reshape(count * block.shape[0], block.shape[1])


def body(right_side, shift):
    nx, ny = lax.axis_size("gx"), lax.axis_size("gy")
    rows, columns = right_side.shape
    z = Sizes(rows, columns, nx, ny)
    at = jnp.stack([lax.axis_index("gx"), lax.axis_index("gy")]).astype(jnp.int32)
    both = jnp.stack([right_side, shift])
    below = ring(both[:, :HALO], "gx", -1)
    above = ring(both[:, rows - HALO :], "gx", 1)
    both = jnp.concatenate([both, below, above], axis=1)
    right = ring(both[:, :, :128], "gy", -1)
    left = ring(both[:, :, columns - 128 :], "gy", 1)
    restrict_columns = z.restrict_columns()
    pack_columns, spread_rows, spread_columns = z.pack_columns(), z.spread_rows(), z.spread_columns()
    fine, half = (z.ext_rows[0], z.ext_columns[0]), (z.ext_rows[1], z.ext_columns[1])
    tiles = (z.ext_columns[0] // 128, z.ext_rows[0], 128)
    g0, d0, w0, v0, c1, d1, w1, v1, packed = call(
        down_kernel, z, [fine] * 4 + [half] * 4 + [(32, z.lanes)], [tiles],
        at, both[0], both[1], left, right, restrict_columns, pack_columns, z.pack_rows(2))
    y = gather(packed, ("gx", "gy"))
    slabs = [level_shape(z, level) for level in (2, 3, 4)]
    work = slabs * 3 + [(16, 8 * z.lanes), tiles]
    d2, d3, d4, w2, w3, w4, e1, packed = call(
        middle_kernel, z, slabs * 2 + [half, (16, z.lanes)], work,
        at, y, c1, d1, w1, v1, spread_rows, spread_columns, pack_columns, z.pack_rows(1))
    y = gather(packed, ("gx", "gy"))
    return call(
        up_kernel, z, [(rows, columns)] * 2, work,
        at, y, d2, d3, d4, w2, w3, w4, c1, w1, e1, g0, d0, w0, v0,
        spread_rows, spread_columns, restrict_columns.T)


def solution(mesh):
    specs = (P("gx", "gy"), P("gx", "gy"))

    def run(right_side, shift):
        out = body(right_side, shift)
        return out[0], out[1]

    return jax.shard_map(run, mesh=mesh, in_specs=specs, out_specs=specs, check_vma=False)
```

time: 727 us -> 72.1 us (0.10)
  the two profiles are of different devices: /device:TPU:28 before, /device:TPU:0 now
where the time goes in v1:
time: 72.1 us; the launch traced here: 71.7 us
  blocking collectives  31.4 us (44%)
  Pallas kernels  17.7 us (25%)
  waiting for transfers between devices  11.9 us (17%)
  starting transfers between devices  5.69 us (8%)
  local copies, waits for them, and re-layouts  2.94 us (4%)
  other arithmetic  1.42 us (2%)
    all_to_all x2, blocking collectives, gather(): out = lax.all_to_all(copies, axes, 0, 0, tiled=True)  31.4 us
    pallas_call x3, Pallas kernels, call(): pl.pallas_call(lambda *refs: kernel(sizes, *refs), name=kernel.__name__,...  17.7 us
    ppermute x4, waiting for transfers between devices, ring(): lax.ppermute(values, axis, [(i, (i + step) % count) for i in range(count)])  11.9 us
    ppermute x4, starting transfers between devices, ring(): lax.ppermute(values, axis, [(i, (i + step) % count) for i in range(count)])  5.69 us
    broadcast_in_dim x2, local copies, waits for them, and re-layouts, gather(): copies = jnp.broadcast_to(block[None], (count,) + block.shape)  1.48 us
  transfers between devices with their start and end apart: 4, of which 4 were waited for; matrix products, arithmetic and copies ran while one was open for 2% of the time, Pallas kernels for 0%

profile of v1, /device:TPU:0, one launch (start us, length us, event | category | flops | bytes accessed | tf_op | source)
XLA Modules:
  0.0 71.7 jit_solution(11780038945847206631)
XLA Ops:
  0.6 0.0 copy-start
  0.6 0.0 copy-start.1
  0.6 0.8 %pad_maximum_fusion.2 = (f32[2,24,256]{2,1,0:T(8,128)S(1)}, f32[2,24,256]{2,1,0:T(8,128)S(1)}) fusion(f32[1,128,256]{2,1,0:T(8,128)} %bitcast.12, f32[1,128,256]{2,1,0:T(8,128)} %bitcast.14), kind=kLoop, calls=%fused_computation.4 | loop fusion | flops 24576 | bytes 360448 | tf_op jit(solution)/shard_map/slice | solution.py:532
  1.5 5.1 %collective-permute-start = (f32[2,24,256]{2,1,0:T(8,128)S(1)}, f32[2,24,256]{2,1,0:T(8,128)S(1)}, u32[]{:S(2)}, u32[]{:S(2)}) collective-permute-start(f32[2,24,256]{2,1,0:T(8,128)S(1)} %get-tuple-element.40), channel_id=1, source_target_pairs={{0,24},{8,0},{16,8},{24,16},{1,25},{9,1},{17,9},{25,17},{2,26},{10... | collective-permute-start | bytes 147464 | tf_op jit(solution)/shard_map/ppermute | solution.py:516
  6.6 0.0 collective-permute-start.1
  6.6 0.6 pad_add_fusion.refs_0_
  7.2 1.2 %collective-permute-done = f32[2,24,256]{2,1,0:T(8,128)S(1)} collective-permute-done((f32[2,24,256]{2,1,0:T(8,128)S(1)}, f32[2,24,256]{2,1,0:T(8,128)S(1)}, u32[]{:S(2)}, u32[]{:S(2)}) %collective-permute-start) | collective-permute-done | bytes 49184 | tf_op jit(solution)/shard_map/ppermute | solution.py:516
  8.4 4.1 %collective-permute-done.1 = f32[2,24,256]{2,1,0:T(8,128)S(1)} collective-permute-done((f32[2,24,256]{2,1,0:T(8,128)S(1)}, f32[2,24,256]{2,1,0:T(8,128)S(1)}, u32[]{:S(2)}, u32[]{:S(2)}) %collective-permute-start.1) | collective-permute-done | bytes 49184 | tf_op jit(solution)/shard_map/ppermute | solution.py:516
  12.5 0.0 copy-done
  12.5 0.0 copy-done.1
  12.6 0.5 collective-permute-start.3
  13.1 0.1 collective-permute-start.2
  13.1 0.8 %slice_bitcast_fusion = (f32[176,256]{1,0:T(8,128)}, f32[176,256]{1,0:T(8,128)}) fusion(f32[2,176,256]{2,1,0:T(8,128)S(1)} %pad_maximum_fusion), kind=kLoop, calls=%fused_computation.1 | loop fusion | bytes 720896 | tf_op jit(solution)/shard_map/squeeze | solution.py:543
  13.9 3.6 %collective-permute-done.3.refs_4_ = f32[2,176,128]{2,1,0:T(8,128)S(1)} collective-permute-done((f32[2,176,128]{2,1,0:T(8,128)S(1)}, f32[2,176,128]{2,1,0:T(8,128)S(1)}, u32[]{:S(2)}, u32[]{:S(2)}) %collective-permute-start.3) | collective-permute-done | bytes 180256 | tf_op jit(solution)/shard_map/ppermute | solution.py:516
  17.5 0.0 copy-start.2
  17.5 3.0 %collective-permute-done.2.refs_3_ = f32[2,176,128]{2,1,0:T(8,128)S(1)} collective-permute-done((f32[2,176,128]{2,1,0:T(8,128)S(1)}, f32[2,176,128]{2,1,0:T(8,128)S(1)}, u32[]{:S(2)}, u32[]{:S(2)}) %collective-permute-start.2) | collective-permute-done | bytes 180256 | tf_op jit(solution)/shard_map/ppermute | solution.py:516
  20.5 0.0 copy-start.3
  20.5 0.0 copy-done.2
  20.5 0.7 copy-done.3
  21.1 3.2 %down_kernel.1 = (f32[176,384]{1,0:T(8,128)}, f32[176,384]{1,0:T(8,128)}, f32[176,384]{1,0:T(8,128)}, f32[176,384]{1,0:T(8,128)}, f32[88,256]{1,0:T(8,128)}, /*i...) custom-call(s32[2]{0:T(128)} %pad_add_fusion.refs_0_, ...), custom_call_target="tpu_custom_call" | custom-call | tf_op jit(solution)/shard_map/down_kernel/pallas_call | solution.py:504
  24.3 0.8 %broadcast_in_dim.4 = f32[32,32,128]{2,1,0:T(8,128)S(1)} broadcast(f32[32,128]{1,0:T(8,128)} %get-tuple-element.19), dimensions={1,2} | broadcast | bytes 540672 | tf_op jit(solution)/shard_map/broadcast_in_dim | solution.py:521
  25.1 18.0 %all_to_all.10 = f32[32,32,128]{2,1,0:T(8,128)} all-to-all(f32[32,32,128]{2,1,0:T(8,128)S(1)} %broadcast_in_dim.4), channel_id=1, replica_groups=mesh['gx'=4,'gy'=8] {'gx','gy'}, dimensions={0} | all-to-all | bytes 1048576 | tf_op jit(solution)/shard_map/all_to_all | solution.py:522
  43.1 8.8 %middle_kernel.1 = (f32[4,4,48,128]{3,2,1,0:T(8,128)}, f32[2,2,48,128]{3,2,1,0:T(8,128)}, f32[1,1,48,128]{3,2,1,0:T(8,128)}, f32[4,4,48,128]{3,2,1,0:T(8,128)}, ...) custom-call(s32[2]{0:T(128)} %pad_add_fusion.refs_0_, ...), custom_call_target="tpu_custom_call" | custom-call | tf_op jit(solution)/shard_map/middle_kernel/pallas_call | solution.py:504
  52.0 0.7 broadcast_in_dim.5
  52.7 13.4 %all_to_all.11 = f32[32,16,128]{2,1,0:T(8,128)} all-to-all(f32[32,16,128]{2,1,0:T(8,128)S(1)} %broadcast_in_dim.5), channel_id=1, replica_groups=mesh['gx'=4,'gy'=8] {'gx','gy'}, dimensions={0} | all-to-all | bytes 524288 | tf_op jit(solution)/shard_map/all_to_all | solution.py:522
  66.1 5.7 %up_kernel.1 = (f32[128,256]{1,0:T(8,128)}, f32[128,256]{1,0:T(8,128)}) custom-call(s32[2]{0:T(128)} %pad_add_fusion.refs_0_, f32[512,128]{1,0:T(8,128)} %bitcast.11, f32[4,4,48,128]{3,2,1,0:T(8,128)} %get-tuple-element.25.refs_2_, f32[2,2,48,128]{3,2,1,0:T(8,128)} %get-tuple-element.26.refs_3_, f32[1,1,48,128]{3,2,1,0:T(8,128)} %get-tuple-element.27.refs_4_, ...), custom_call_target="tpu_custom_call" | custom-call | tf_op jit(solution)/shard_map/up_kernel/pallas_call | solution.py:504
  (2 shorter events, 0.0 us)
Async XLA Ops:
  0.6 11.9 %copy-start = (f32[128,256]{1,0:T(8,128)S(1)}, f32[128,256]{1,0:T(8,128)}, u32[]{:S(2)}) copy-start(f32[128,256]{1,0:T(8,128)} %param.10) | copy-start | bytes 393220
  0.6 11.9 %copy-start.1 = (f32[128,256]{1,0:T(8,128)S(1)}, f32[128,256]{1,0:T(8,128)}, u32[]{:S(2)}) copy-start(f32[128,256]{1,0:T(8,128)} %param.9) | copy-start | bytes 393220
  1.5 6.9 %collective-permute-start = (f32[2,24,256]{2,1,0:T(8,128)S(1)}, f32[2,24,256]{2,1,0:T(8,128)S(1)}, u32[]{:S(2)}, u32[]{:S(2)}) collective-permute-start(f32[2,24,256]{2,1,0:T(8,128)S(1)} %get-tuple-element.40), channel_id=1, source_target_pairs={{0,24},{8,0},{16,8},{24,16},{1,25},{9,1},{17,9},{25,17},{2,26},{10... | collective-permute-start | bytes 147464 | tf_op jit(solution)/shard_map/ppermute | solution.py:516
  6.6 5.9 %collective-permute-start.1 = (f32[2,24,256]{2,1,0:T(8,128)S(1)}, f32[2,24,256]{2,1,0:T(8,128)S(1)}, u32[]{:S(2)}, u32[]{:S(2)}) collective-permute-start(f32[2,24,256]{2,1,0:T(8,128)S(1)} %get-tuple-element.41), channel_id=1, source_target_pairs={{0,8},{8,16},{16,24},{24,0},{1,9},{9,17},{17,25},{25,1},{2,10},{10... | collective-permute-start | bytes 147464 | tf_op jit(solution)/shard_map/ppermute | solution.py:516
  12.6 4.9 %collective-permute-start.3 = (f32[2,176,128]{2,1,0:T(8,128)S(1)}, f32[2,176,128]{2,1,0:T(8,128)S(1)}, u32[]{:S(2)}, u32[]{:S(2)}) collective-permute-start(f32[2,176,128]{2,1,0:T(8,128)S(1)} %get-tuple-element.36), channel_id=1, source_target_pairs={{0,7},{1,0},{2,1},{3,2},{4,3},{5,4},{6,5},{7,6},{8,15},{9,8},{10,9... | collective-permute-start | bytes 540680 | tf_op jit(solution)/shard_map/ppermute | solution.py:516
  13.1 7.4 %collective-permute-start.2 = (f32[2,176,128]{2,1,0:T(8,128)S(1)}, f32[2,176,128]{2,1,0:T(8,128)S(1)}, u32[]{:S(2)}, u32[]{:S(2)}) collective-permute-start(f32[2,176,128]{2,1,0:T(8,128)S(1)} %get-tuple-element.37), channel_id=1, source_target_pairs={{0,1},{1,2},{2,3},{3,4},{4,5},{5,6},{6,7},{7,0},{8,9},{9,10},{10,1... | collective-permute-start | bytes 540680 | tf_op jit(solution)/shard_map/ppermute | solution.py:516
  17.5 3.0 %copy-start.2 = (f32[2,176,128]{2,1,0:T(8,128)}, f32[2,176,128]{2,1,0:T(8,128)S(1)}, u32[]{:S(2)}) copy-start(f32[2,176,128]{2,1,0:T(8,128)S(1)} %collective-permute-done.3.refs_4_) | copy-start | bytes 540676
  20.5 0.7 copy-start.3

commit v2 on v1

--- a/solution.py
+++ b/solution.py
@@ -9,7 +9,7 @@
 LEVELS = 4
 COARSE_SWEEPS = 6
 DAMPING = 0.8
-HALO = 24
+HALO = 48
 
 
 def f32dot_right(values, onehot):
@@ -70,49 +70,54 @@
         row = np.arange(height)
         return np.where(row < own + halo, row, row - height)
 
-    def restrict_columns(self):
-        fine, fine_in = self.column_at(0)
-        coarse, coarse_in = self.column_at(1)
+    def restrict_columns(self, level):
+        fine, fine_in = self.column_at(level)
+        coarse, coarse_in = self.column_at(level + 1)
         hit = (fine[:, None] // 2 == coarse[None, :]) & fine_in[:, None] & coarse_in[None, :]
         return hit.astype(jnp.bfloat16)
 
-    def pack_columns(self):
-        x = np.arange(self.columns // 2)[:, None, None]
-        r = np.arange(4)[None, :, None]
+    def pack_columns(self, level, pairs):
+        n = 1 << (LEVELS - level)
+        own = self.columns >> level
+        x = np.arange(self.ext_columns[2])[:, None, None]
+        cell = x // 2 if pairs else x
+        r = np.arange(n)[None, :, None]
         lane = np.arange(self.lanes)[None, None, :]
-        hit = x // 2 == 4 * (lane // self.p) + r
-        return hit.reshape(self.columns // 2, 4 * self.lanes).astype(jnp.bfloat16)
-
-    def pack_rows(self, fields):
-        count = self.rows // 4
+        hit = (cell == n * (lane // self.p) + r) & (cell < own)
+        return hit.reshape(len(x), n * self.lanes).astype(jnp.bfloat16)
+
+    def pack_rows(self, level, fields):
+        n = 1 << (LEVELS - level)
+        count = self.rows >> level
         f = np.arange(fields)
-        s = np.arange(4)
+        s = np.arange(n)
         k = np.arange(count)
-        hit = (f[:, None, None, None] == f[None, None, :, None]) & (k[None, None, None, :] % 4 == s[None, :, None, None])
-        hit = hit.reshape(fields * 4, fields * count)
+        hit = (f[:, None, None, None] == f[None, None, :, None]) & (k[None, None, None, :] % n == s[None, :, None, None])
+        hit = hit.reshape(fields * n, fields * count)
         pad = -hit.shape[0] % 8
         return np.pad(hit, ((0, pad), (0, 0))).astype(jnp.bfloat16)
 
-    def spread_rows(self):
-        k = self.row_at(1) // 2
-        count = self.rows // 4
-        block = k // count
-        s = (k % count) % 4
-        slot = (block + 1) * 4 + s
-        return (slot[:, None] == np.arange(16)[None, :]).astype(jnp.bfloat16)
-
-    def spread_columns(self):
-        column, inside = self.column_at(1)
+    def spread_rows(self, level):
+        n = 1 << (LEVELS - level)
+        k = self.row_at(level - 1) // 2
+        count = self.rows >> level
+        slot = (k // count + 1) * n + (k % count) % n
+        width = 3 * n + (-3 * n) % 8
+        return (slot[:, None] == np.arange(width)[None, :]).astype(jnp.bfloat16)
+
+    def spread_columns(self, level):
+        n = 1 << (LEVELS - level)
+        column, inside = self.column_at(level - 1)
         m = column // 2
-        count = self.columns // 4
+        count = self.columns >> level
         block = m // count
-        r = (m % count) % 4
-        q = (m % count) // 4
+        r = (m % count) % n
+        q = (m % count) // n
         beside = np.arange(2)[:, None, None, None]
-        rr = np.arange(4)[None, :, None, None]
+        rr = np.arange(n)[None, :, None, None]
         lane = np.arange(self.lanes)[None, None, :, None]
         hit = ((block != 0) == beside) & (r == rr) & (q == lane // self.p) & inside
-        return hit.reshape(8 * self.lanes, -1).astype(jnp.bfloat16)
+        return hit.reshape(2 * n * self.lanes, -1).astype(jnp.bfloat16)
 
 
 def iota(shape, axis):
@@ -140,32 +145,59 @@
     return jnp.concatenate(outs, axis=1)
 
 
-def pack(sizes, scratch, fields, columns_ref, rows_ref, out_ref):
-    own_r, own_c = sizes.rows // 2, sizes.columns // 2
-    count = own_r // 2
-    summed = jnp.concatenate([pair_rows(scratch, f[:own_r, :own_c]) for f in fields], axis=0)
-    spread = f32dot_right(summed, columns_ref[...])
+def double_rows(scratch, values):
+    rows, columns = values.shape
+    for t in range(columns // 128):
+        part = values[:, t * 128 : (t + 1) * 128]
+        scratch[t, pl.ds(0, rows, stride=2), :] = part
+        scratch[t, pl.ds(1, rows, stride=2), :] = part
+    return jnp.concatenate([scratch[t, : 2 * rows, :] for t in range(columns // 128)], axis=1)
+
+
+def pack(sizes, level, fields, columns_ref, rows_ref, out_ref):
+    n = 1 << (LEVELS - level)
+    count = sizes.rows >> level
+    spread = f32dot_right(jnp.concatenate(fields, axis=0), columns_ref[...])
     shape = spread.shape
-    keep = ((iota(shape, 0) % count) // 4) == (iota(shape, 1) % sizes.p)
-    spread = jnp.where(keep, spread, 0.0)
-    out = f32dot_left(rows_ref[...], spread)
-    n = 4 * len(fields)
-    for r in range(4):
-        out_ref[r * n : (r + 1) * n, :] = out[:n, r * sizes.lanes : (r + 1) * sizes.lanes]
-
-
-def down_kernel(sizes, at_ref, g_ref, s_ref, left_ref, right_ref, rc_ref, pc_ref, pr_ref,
-                g0_ref, d0_ref, w0_ref, v0_ref, c1_ref, d1_ref, w1_ref, v1_ref, out_ref, scratch):
+    keep = ((iota(shape, 0) % count) // n) == (iota(shape, 1) % sizes.p)
+    out = f32dot_left(rows_ref[...], jnp.where(keep, spread, 0.0))
+    height = n * len(fields)
+    block = jnp.concatenate([out[:height, r * sizes.lanes : (r + 1) * sizes.lanes] for r in range(n)], axis=0)
+    copies = max(1, 8 // block.shape[0])
+    block = jnp.concatenate([block] * copies, axis=0)
+    for k in range(out_ref.shape[0] // block.shape[0]):
+        out_ref[k * block.shape[0] : (k + 1) * block.shape[0], :] = block
+
+
+def strip_kernel(sizes, at_ref, g_ref, s_ref, below_ref, above_ref, left_ref, right_ref):
+    last = sizes.columns - 128
+    for rows, sources in ((slice(0, sizes.rows), (g_ref, s_ref)),
+                          (slice(sizes.rows, sizes.rows + HALO), (below_ref.at[0], below_ref.at[1])),
+                          (slice(sizes.rows + HALO, sizes.rows + 2 * HALO), (above_ref.at[0], above_ref.at[1]))):
+        g, s = sources
+        first_g, first_s = g[:, :128], s[:, :128]
+        last_g, last_s = g[:, last:], s[:, last:]
+        lane = iota(first_g.shape, 1)
+        left_ref[rows, :] = jnp.where(lane < HALO, first_g, pltpu.roll(first_s, HALO, 1))
+        right_ref[rows, :] = jnp.where(lane >= 128 - HALO, last_g, pltpu.roll(last_s, 128 - HALO, 1))
+
+
+def coefficients(sizes, level, gx, gy, sigma):
+    d = 4.0 + sigma
+    return d, jnp.where(inside_mask(sizes, level, gx, gy), DAMPING / d, 0.0)
+
+
+def down_kernel(sizes, at_ref, g_ref, s_ref, below_ref, above_ref, left_ref, right_ref, rc0_ref, rc1_ref, pc_ref, pr_ref,
+                g0_ref, d0_ref, w0_ref, v0_ref, c1_ref, d1_ref, w1_ref, v1_ref, d2_ref, w2_ref, out_ref, scratch):
     gx, gy = at_ref[0], at_ref[1]
-    rows, columns = sizes.ext_rows[0], sizes.ext_columns[0]
+    rows = sizes.ext_rows[0]
     lane = iota((rows, 128), 1)
-    beside = []
-    for k in range(2):
-        beside.append(jnp.where(lane < HALO, right_ref[k], left_ref[k]))
-    g = jnp.concatenate([g_ref[...], beside[0]], axis=1)
-    sigma = jnp.concatenate([s_ref[...], beside[1]], axis=1)
-    d = 4.0 + sigma
-    w = jnp.where(inside_mask(sizes, 0, gx, gy), DAMPING / d, 0.0)
+    from_left, from_right = left_ref[...], right_ref[...]
+    g = jnp.where(lane < HALO, from_right, from_left)
+    sigma = jnp.where(lane < HALO, pltpu.roll(from_right, 128 - HALO, 1), pltpu.roll(from_left, HALO, 1))
+    g = jnp.concatenate([jnp.concatenate([g_ref[...], below_ref[0], above_ref[0]], axis=0), g], axis=1)
+    sigma = jnp.concatenate([jnp.concatenate([s_ref[...], below_ref[1], above_ref[1]], axis=0), sigma], axis=1)
+    d, w = coefficients(sizes, 0, gx, gy, sigma)
     v = w * g
     v = sweep(v, g, w)
     r = g - d * v + around(v)
@@ -175,10 +207,9 @@
     v0_ref[...] = v
     half = rows // 2
     both = jnp.concatenate([pair_rows(scratch, r), pair_rows(scratch, sigma)], axis=0)
-    both = f32dot_right(both, rc_ref[...])
+    both = f32dot_right(both, rc0_ref[...])
     g, sigma = both[:half], both[half:]
-    d = 4.0 + sigma
-    w = jnp.where(inside_mask(sizes, 1, gx, gy), DAMPING / d, 0.0)
+    d, w = coefficients(sizes, 1, gx, gy, sigma)
     v = w * g
     v = sweep(v, g, w)
     r = g - d * v + around(v)
@@ -186,12 +217,21 @@
     d1_ref[...] = d
     w1_ref[...] = w
     v1_ref[...] = v
-    pack(sizes, scratch, [r, sigma], pc_ref, pr_ref, out_ref)
+    half = half // 2
+    both = jnp.concatenate([pair_rows(scratch, r), pair_rows(scratch, sigma)], axis=0)
+    both = f32dot_right(both, rc1_ref[...])
+    g, sigma = both[:half], both[half:]
+    d, w = coefficients(sizes, 2, gx, gy, sigma)
+    d2_ref[...] = d
+    w2_ref[...] = w
+    own = sizes.rows // 4
+    pack(sizes, 2, [g[:own], sigma[:own]], pc_ref, pr_ref, out_ref)
 
 
 class Coarse:
-    def __init__(self, sizes, d_refs, w_refs, g_refs, v_refs, t_refs):
+    def __init__(self, sizes, first, d_refs, w_refs, g_refs, v_refs, t_refs):
         self.z = sizes
+        self.first = first
         self.d, self.w, self.g, self.v, self.t = d_refs, w_refs, g_refs, v_refs, t_refs
         shape = (sizes.ny, sizes.lanes)
         lane, row = iota(shape, 1), iota(shape, 0)
@@ -256,7 +296,7 @@
         self.blocks(block)
 
     def first_sweep(self, level):
-        l = level - 2
+        l = level - self.first
 
         def body(s, r, n, base):
             self.put(self.v[l], s, r, base, self.at(self.w[l], s, r, base) * self.at(self.g[l], s, r, base))
@@ -264,7 +304,7 @@
         self.each(level, body)
 
     def sweep(self, level, source, target):
-        l = level - 2
+        l = level - self.first
 
         def body(s, r, n, base):
             v = self.at(source, s, r, base)
@@ -274,24 +314,24 @@
         self.each(level, body)
 
     def two_sweeps(self, level):
-        l = level - 2
+        l = level - self.first
         self.sweep(level, self.v[l], self.t[l])
         self.sweep(level, self.t[l], self.v[l])
 
     def start(self, level):
-        l = level - 2
+        l = level - self.first
         self.first_sweep(level)
         self.sweep(level, self.v[l], self.t[l])
         self.v[l], self.t[l] = self.t[l], self.v[l]
 
     def residual(self, level, s, r, n, base):
-        l = level - 2
+        l = level - self.first
         v = self.at(self.v[l], s, r, base)
         g = self.at(self.g[l], s, r, base)
         return (g - self.at(self.d[l], s, r, base) * v) + self.neighbours(self.v[l], s, r, n, base)
 
     def restrict(self, level):
-        l = level - 2
+        l = level - self.first
         n = 1 << (LEVELS - level)
 
         def block(base):
@@ -303,7 +343,7 @@
         self.blocks(block)
 
     def prolong(self, level):
-        l = level - 2
+        l = level - self.first
 
         def body(s, r, n, base):
             e = self.at(self.v[l + 1], s // 2, r // 2, base)
@@ -326,14 +366,14 @@
 
     def unit(self):
         z = self.z
-        top = LEVELS - 2
+        top = LEVELS - self.first
         missing = 2.0 * (z.nx * z.p + z.ny * z.q) - 0.0
         cells = 4.0
         total = self.total(lambda base: self.at(self.d[top], 0, 0, base) - cells)
         return total + missing
 
     def coarse(self, fresh, unit):
-        top = LEVELS - 2
+        top = LEVELS - self.first
         v, t, g = self.v[top], self.t[top], self.g[top]
         if fresh:
             left = self.total(lambda base: self.at(g, 0, 0, base)) / unit
@@ -386,44 +426,60 @@
                         ref[s, r, : z.ny, :] = zero
                         ref[s, r, (z.nx + 1) * z.ny :, :] = zero
 
-    def take(self, y_ref, target, count, offset, add):
+    def take(self, y_ref, target, offset, height):
         z = self.z
+        n = target.shape[0]
 
         def block(base):
-            for s in range(4):
-                for r in range(4):
-                    first = (base - z.ny) * 4 * count + r * count + offset + s
-                    value = y_ref[pl.ds(first, z.ny, stride=4 * count), :]
-                    self.put(target, s, r, base, value + add if add else value)
+            for s in range(n):
+                for r in range(n):
+                    first = (base - z.ny) * n * height + r * height + offset + s
+                    self.put(target, s, r, base, y_ref[pl.ds(first, z.ny, stride=n * height), :])
+
+        self.blocks(block)
+
+    def take_cores(self, even_ref, odd_ref, target, offset, height, add):
+        z = self.z
+        n = target.shape[0]
+        half = z.ny // 2
+
+        def block(base):
+            for s in range(n):
+                for r in range(n):
+                    first = (base - z.ny) // 2 * n * height + r * height + offset + s
+                    for core, ref in ((0, even_ref), (1, odd_ref)):
+                        value = ref[pl.ds(first, half, stride=n * height), :]
+                        target[s, r, pl.ds(base + core, half, stride=2), :] = value + add if add else value
 
         self.blocks(block)
 
     def spread(self, gx, gy, rows_ref, columns_ref, e_ref):
         z = self.z
+        n = 1 << (LEVELS - self.first)
         row = (gx + 1) * z.ny + gy
         lane = iota((1, z.lanes), 1)
         low_half = lane // z.p < z.q // 2
         has_left, has_right = gy > 0, gy < z.ny - 1
-        e_ref[12:, :] = jnp.zeros((4, 8 * z.lanes), jnp.float32)
+        e_ref[...] = jnp.zeros(e_ref.shape, jnp.float32)
+        ref = self.v[0]
         for dx in range(3):
             base = row + (dx - 1) * z.ny
-            for s in range(4):
-                for r in range(4):
-                    ref = self.v[0]
+            for s in range(n):
+                for r in range(n):
                     own = ref[s, r, pl.ds(base, 1), :]
                     left = ref[s, r, pl.ds(jnp.where(has_left, base - 1, 0), 1), :]
                     right = ref[s, r, pl.ds(jnp.where(has_right, base + 1, 0), 1), :]
-                    k = dx * 4 + s
+                    k = dx * n + s
                     e_ref[k : k + 1, r * z.lanes : (r + 1) * z.lanes] = own
-                    e_ref[k : k + 1, (4 + r) * z.lanes : (5 + r) * z.lanes] = jnp.where(low_half, right, left)
+                    e_ref[k : k + 1, (n + r) * z.lanes : (n + r + 1) * z.lanes] = jnp.where(low_half, right, left)
         spread = f32dot_left(rows_ref[...], e_ref[...])
         shape = spread.shape
         index = iota(shape, 0)
-        own_r, halo = z.rows // 2, HALO // 2
+        above = self.first - 1
+        own_r, halo = z.rows >> above, HALO >> above
         cell = jnp.where(index < own_r + halo, index, index - shape[0]) + 2 * z.rows
-        keep = ((cell // 8) % z.p) == (iota(shape, 1) % z.p)
-        spread = jnp.where(keep, spread, 0.0)
-        return f32dot_right(spread, columns_ref[...])
+        keep = ((cell // (2 * n)) % z.p) == (iota(shape, 1) % z.p)
+        return f32dot_right(jnp.where(keep, spread, 0.0), columns_ref[...])
 
 
 def level_shape(sizes, level):
@@ -431,14 +487,25 @@
     return (n, n, (sizes.nx + 2) * sizes.ny, sizes.lanes)
 
 
-def middle_kernel(sizes, at_ref, y_ref, c1_ref, d1_ref, w1_ref, v1_ref, sr_ref, sc_ref, pc_ref, pr_ref,
-                  d2_ref, d3_ref, d4_ref, w2_ref, w3_ref, w4_ref, e1_ref, out_ref,
-                  g2, g3, g4, v2, v3, v4, t2, t3, t4, e_ref, scratch):
+def middle_kernel(sizes, at_ref, y_ref, other_ref, c1_ref, d1_ref, w1_ref, v1_ref, w2l_ref, d2l_ref, sr_ref, sc_ref,
+                  rc1_ref, pc_ref, pr_ref,
+                  d3_ref, d4_ref, w3_ref, w4_ref, e1_ref, c2_ref, e2_ref, out_ref,
+                  d2, w2, g2, g3, g4, v2, v3, v4, t2, t3, t4, e_ref, scratch):
     gx, gy = at_ref[0], at_ref[1]
-    m = Coarse(sizes, [d2_ref, d3_ref, d4_ref], [w2_ref, w3_ref, w4_ref], [g2, g3, g4], [v2, v3, v4], [t2, t3, t4])
+    m = Coarse(sizes, 2, [d2, d3_ref, d4_ref], [w2, w3_ref, w4_ref], [g2, g3, g4], [v2, v3, v4], [t2, t3, t4])
     m.clear_ends()
-    m.take(y_ref, g2, 8, 0, 0.0)
-    m.take(y_ref, d2_ref, 8, 4, 4.0)
+    core = lax.rem(gy, 2)
+
+    @pl.when(core == 0)
+    def _():
+        m.take_cores(y_ref, other_ref, g2, 0, 8, 0.0)
+        m.take_cores(y_ref, other_ref, d2, 4, 8, 4.0)
+
+    @pl.when(core == 1)
+    def _():
+        m.take_cores(other_ref, y_ref, g2, 0, 8, 0.0)
+        m.take_cores(other_ref, y_ref, d2, 4, 8, 4.0)
+
     for l in range(2):
         n = 2 >> l
 
@@ -463,31 +530,34 @@
         v = sweep(v, g, w)
     e1_ref[...] = v
     r = g - d * v + around(v)
-    pack(sizes, scratch, [r], pc_ref, pr_ref, out_ref)
-
-
-def up_kernel(sizes, at_ref, y_ref, d2_ref, d3_ref, d4_ref, w2_ref, w3_ref, w4_ref, c1_ref, w1_ref, e1_ref,
-              g0_ref, d0_ref, w0_ref, v0_ref, sr_ref, sc_ref, rt_ref,
-              solution_ref, residual_ref, g2, g3, g4, v2, v3, v4, t2, t3, t4, e_ref, scratch):
+    g = f32dot_right(pair_rows(scratch, r), rc1_ref[...])
+    d, w = d2l_ref[...], w2l_ref[...]
+    v = w * g
+    v = sweep(v, g, w)
+    r = g - d * v + around(v)
+    c2_ref[...] = g
+    e2_ref[...] = v
+    pack(sizes, 3, [pair_rows(scratch, r[: sizes.rows // 4])], pc_ref, pr_ref, out_ref)
+
+
+def up_kernel(sizes, at_ref, y_ref, d3_ref, d4_ref, w3_ref, w4_ref, c2_ref, w2_ref, e2_ref, c1_ref, w1_ref, e1_ref,
+              g0_ref, d0_ref, w0_ref, v0_ref, sr_ref, sc_ref, pc1_ref, pc0_ref,
+              solution_ref, residual_ref, g3, g4, v3, v4, t3, t4, e_ref, scratch):
     gx, gy = at_ref[0], at_ref[1]
-    m = Coarse(sizes, [d2_ref, d3_ref, d4_ref], [w2_ref, w3_ref, w4_ref], [g2, g3, g4], [v2, v3, v4], [t2, t3, t4])
+    m = Coarse(sizes, 3, [d3_ref, d4_ref], [w3_ref, w4_ref], [g3, g4], [v3, v4], [t3, t4])
     m.clear_ends()
-    m.take(y_ref, g2, 4, 0, 0.0)
-    unit = m.unit()
-    m.vcycle(2, True, unit)
-    g, w = c1_ref[...], w1_ref[...]
-    v = e1_ref[...] + jnp.where(w > 0.0, m.spread(gx, gy, sr_ref, sc_ref, e_ref), 0.0)
+    m.take(y_ref, g3, 0, 2)
+    m.vcycle(3, True, m.unit())
+    g, w = c2_ref[...], w2_ref[...]
+    v = e2_ref[...] + jnp.where(w > 0.0, m.spread(gx, gy, sr_ref, sc_ref, e_ref), 0.0)
     for turn in range(2):
         v = sweep(v, g, w)
-    wide = f32dot_right(v, rt_ref[...])
-    half = wide.shape[0]
-    tiles = wide.shape[1] // 128
-    for t in range(tiles):
-        part = wide[:, t * 128 : (t + 1) * 128]
-        scratch[t, pl.ds(0, half, stride=2), :] = part
-        scratch[t, pl.ds(1, half, stride=2), :] = part
+    g, w = c1_ref[...], w1_ref[...]
+    v = e1_ref[...] + double_rows(scratch, f32dot_right(v, pc1_ref[...]))
+    for turn in range(2):
+        v = sweep(v, g, w)
     g, d, w = g0_ref[...], d0_ref[...], w0_ref[...]
-    v = v0_ref[...] + jnp.concatenate([scratch[t] for t in range(tiles)], axis=1)
+    v = v0_ref[...] + double_rows(scratch, f32dot_right(v, pc0_ref[...]))
     for turn in range(2):
         v = sweep(v, g, w)
     r = g - d * v + around(v)
@@ -516,11 +586,15 @@
     return lax.ppermute(values, axis, [(i, (i + step) % count) for i in range(count)])
 
 
-def gather(block, axes):
-    count = lax.axis_size(axes)
-    copies = jnp.broadcast_to(block[None], (count,) + block.shape)
-    out = lax.all_to_all(copies, axes, 0, 0, tiled=True)
-    return out.reshape(count * block.shape[0], block.shape[1])
+def gather(copies):
+    return lax.all_to_all(copies, ("gx", "gy"), 0, 0, tiled=True)
+
+
+def gather_by_core(copies, nx, ny):
+    index = np.arange(nx * ny)
+    groups = [index[core::2].tolist() for core in range(2)]
+    own = lax.all_to_all(copies, ("gx", "gy"), 0, 0, tiled=True, axis_index_groups=groups)
+    return own, lax.ppermute(own, "gy", [(j, j ^ 1) for j in range(ny)])
 
 
 def body(right_side, shift):
@@ -528,30 +602,30 @@
     rows, columns = right_side.shape
     z = Sizes(rows, columns, nx, ny)
     at = jnp.stack([lax.axis_index("gx"), lax.axis_index("gy")]).astype(jnp.int32)
-    both = jnp.stack([right_side, shift])
-    below = ring(both[:, :HALO], "gx", -1)
-    above = ring(both[:, rows - HALO :], "gx", 1)
-    both = jnp.concatenate([both, below, above], axis=1)
-    right = ring(both[:, :, :128], "gy", -1)
-    left = ring(both[:, :, columns - 128 :], "gy", 1)
-    restrict_columns = z.restrict_columns()
-    pack_columns, spread_rows, spread_columns = z.pack_columns(), z.spread_rows(), z.spread_columns()
-    fine, half = (z.ext_rows[0], z.ext_columns[0]), (z.ext_rows[1], z.ext_columns[1])
-    tiles = (z.ext_columns[0] // 128, z.ext_rows[0], 128)
-    g0, d0, w0, v0, c1, d1, w1, v1, packed = call(
-        down_kernel, z, [fine] * 4 + [half] * 4 + [(32, z.lanes)], [tiles],
-        at, both[0], both[1], left, right, restrict_columns, pack_columns, z.pack_rows(2))
-    y = gather(packed, ("gx", "gy"))
+    below = ring(jnp.stack([right_side[:HALO], shift[:HALO]]), "gx", -1)
+    above = ring(jnp.stack([right_side[rows - HALO :], shift[rows - HALO :]]), "gx", 1)
+    ext = [(z.ext_rows[l], z.ext_columns[l]) for l in range(3)]
+    strip = (z.ext_rows[0], 128)
+    to_left, to_right = call(strip_kernel, z, [strip] * 2, [], at, right_side, shift, below, above)
+    right = ring(to_left, "gy", -1)
+    left = ring(to_right, "gy", 1)
+    rc0, rc1 = z.restrict_columns(0), z.restrict_columns(1)
+    tiles = (ext[0][1] // 128, ext[0][0], 128)
+    g0, d0, w0, v0, c1, d1, w1, v1, d2, w2, packed = call(
+        down_kernel, z, [ext[0]] * 4 + [ext[1]] * 4 + [ext[2]] * 2 + [(nx * ny // 2 * 32, z.lanes)], [tiles],
+        at, right_side, shift, below, above, left, right, rc0, rc1, z.pack_columns(2, False), z.pack_rows(2, 2))
+    y, other = gather_by_core(packed, nx, ny)
     slabs = [level_shape(z, level) for level in (2, 3, 4)]
-    work = slabs * 3 + [(16, 8 * z.lanes), tiles]
-    d2, d3, d4, w2, w3, w4, e1, packed = call(
-        middle_kernel, z, slabs * 2 + [half, (16, z.lanes)], work,
-        at, y, c1, d1, w1, v1, spread_rows, spread_columns, pack_columns, z.pack_rows(1))
-    y = gather(packed, ("gx", "gy"))
+    d3, d4, w3, w4, e1, c2, e2, packed = call(
+        middle_kernel, z, slabs[1:] * 2 + [ext[1], ext[2], ext[2], (nx * ny * 4, z.lanes)],
+        [slabs[0]] * 2 + slabs * 3 + [(16, 8 * z.lanes), tiles],
+        at, y, other, c1, d1, w1, v1, w2, d2, z.spread_rows(2), z.spread_columns(2),
+        rc1, z.pack_columns(3, True), z.pack_rows(3, 1))
+    y = gather(packed)
     return call(
-        up_kernel, z, [(rows, columns)] * 2, work,
-        at, y, d2, d3, d4, w2, w3, w4, c1, w1, e1, g0, d0, w0, v0,
-        spread_rows, spread_columns, restrict_columns.T)
+        up_kernel, z, [(rows, columns)] * 2, slabs[1:] * 3 + [(8, 4 * z.lanes), tiles],
+        at, y, d3, d4, w3, w4, c2, w2, e2, c1, w1, e1, g0, d0, w0, v0,
+        z.spread_rows(3), z.spread_columns(3), rc1.T, rc0.T)
 
 
 def solution(mesh):

time: 72.1 us -> 68.7 us (0.953)
  blocking collectives: 31.4 us -> 25.6 us
  Pallas kernels: 17.7 us -> 20 us
  starting transfers between devices: 5.69 us -> 7.83 us
  waiting for transfers between devices: 11.9 us -> 9.95 us
  other arithmetic: 1.42 us -> 0.68 us
    all_to_all x2, blocking collectives: 31.4 us -> 25.6 us  [the longest x1 14.9 us: gather_by_core(): lax.all_to_all(copies, ('gx', 'gy'), 0, 0, tiled=True, axis_index_groups=...]
    ppermute x4, waiting for transfers between devices: 11.9 us -> 8.41 us  [ring(): lax.ppermute(values, axis, [(i, (i + step) % count) for i in range(count)])]
    pallas_call x3 -> x4, Pallas kernels: 17.7 us -> 20 us  [call(): pl.pallas_call(lambda *refs: kernel(sizes, *refs), name=kernel.__name__,...]
    ppermute x4, starting transfers between devices: 5.69 us -> 7.83 us  [ring(): lax.ppermute(values, axis, [(i, (i + step) % count) for i in range(count)])]
    unnamed x8 -> x12, local copies, waits for them, and re-layouts: 0.67 us -> 2.64 us
    ppermute x0 -> x1, waiting for transfers between devices: none -> 1.53 us  [gather_by_core(): return (own, lax.ppermute(own, 'gy', [(j, j ^ 1) for j in range(ny)]))]
    broadcast_in_dim x2 -> x0, local copies, waits for them, and re-layouts: 1.48 us -> none  [gather(): copies = jnp.broadcast_to(block[None], (count,) + block.shape)]
    another operation x0 -> x1, local copies, waits for them, and re-layouts: none -> 0.89 us  [body(): jnp.stack([right_side[rows - HALO:], shift[rows - HALO:]])]
  transfers between devices with their start and end apart: 4 -> 5, of which waited for: 4 -> 4; matrix products, arithmetic and copies ran while one was open for 2% -> 1% of each run, Pallas kernels for 0% -> 0%
where the time goes in v2:
time: 68.7 us; the launch traced here: 68.2 us
  blocking collectives  25.6 us (37%)
  Pallas kernels  20 us (29%)
  waiting for transfers between devices  9.95 us (14%)
  starting transfers between devices  7.83 us (11%)
  local copies, waits for them, and re-layouts  3.53 us (5%)
    pallas_call x4, Pallas kernels, call(): pl.pallas_call(lambda *refs: kernel(sizes, *refs), name=kernel.__name__,...  20 us
    all_to_all x1, blocking collectives, gather_by_core(): lax.all_to_all(copies, ('gx', 'gy'), 0, 0, tiled=True, axis_index_groups=...  14.9 us
    all_to_all x1, blocking collectives, gather(): return lax.all_to_all(copies, ('gx', 'gy'), 0, 0, tiled=True)  10.7 us
    ppermute x4, waiting for transfers between devices, ring(): lax.ppermute(values, axis, [(i, (i + step) % count) for i in range(count)])  8.41 us
    ppermute x4, starting transfers between devices, ring(): lax.ppermute(values, axis, [(i, (i + step) % count) for i in range(count)])  7.83 us
    unnamed x12, local copies, waits for them, and re-layouts  2.64 us
    ppermute x1, waiting for transfers between devices, gather_by_core(): return (own, lax.ppermute(own, 'gy', [(j, j ^ 1) for j in range(ny)]))  1.53 us
  transfers between devices with their start and end apart: 5, of which 4 were waited for; matrix products, arithmetic and copies ran while one was open for 1% of the time, Pallas kernels for 0%

profile of v2, /device:TPU:0, one launch (start us, length us, event | category | flops | bytes accessed | tf_op | source)
XLA Modules:
  0.0 68.2 jit_solution(4029830483855406412)
XLA Ops:
  0.6 0.9 %slice_bitcast_fusion = (f32[1,48,256]{2,1,0:T(8,128)S(1)}, f32[1,48,256]{2,1,0:T(8,128)S(1)}, f32[1,48,256]{2,1,0:T(8,128)S(1)}, f32[1,48,256]{2,1,0:T(8,128)S(1)}) fusion(f32[128,256]{1,0:T(8,128)} %refs_2_.3, f32[128,256]{1,0:T(8,128)} %refs_1_.3), kind=kLoop, calls=%fused_computation.2 | loop fusion | bytes 393216 | tf_op jit(solution)/shard_map/stack | solution.py:606
  1.5 5.1 %collective-permute-start = (f32[2,48,256]{2,1,0:T(8,128)S(1)}, f32[2,48,256]{2,1,0:T(8,128)S(1)}, u32[]{:S(2)}, u32[]{:S(2)}) collective-permute-start(f32[2,48,256]{2,1,0:T(8,128)S(1)} %pad_maximum_fusion), channel_id=1, source_target_pairs={{0,24},{8,0},{16,8},{24,16},{1,25},{9,1},{17,9},{25,17},{2,26},{10... | collective-permute-start | bytes 294920 | tf_op jit(solution)/shard_map/ppermute | solution.py:586
  6.7 0.1 collective-permute-start.1
  6.7 0.7 pad_add_fusion.refs_0_
  7.4 2.4 %collective-permute-done.refs_3_ = f32[2,48,256]{2,1,0:T(8,128)S(1)} collective-permute-done((f32[2,48,256]{2,1,0:T(8,128)S(1)}, f32[2,48,256]{2,1,0:T(8,128)S(1)}, u32[]{:S(2)}, u32[]{:S(2)}) %collective-permute-start) | collective-permute-done | bytes 98336 | tf_op jit(solution)/shard_map/ppermute | solution.py:586
  9.9 0.0 copy-start.1
  9.9 3.3 %collective-permute-done.1.refs_4_ = f32[2,48,256]{2,1,0:T(8,128)S(1)} collective-permute-done((f32[2,48,256]{2,1,0:T(8,128)S(1)}, f32[2,48,256]{2,1,0:T(8,128)S(1)}, u32[]{:S(2)}, u32[]{:S(2)}) %collective-permute-start.1) | collective-permute-done | bytes 98336 | tf_op jit(solution)/shard_map/ppermute | solution.py:586
  13.1 0.0 copy-done.1
  13.1 0.0 copy-start.2
  13.1 0.7 copy-done.2
  13.8 1.9 %strip_kernel.1 = (f32[224,128]{1,0:T(8,128)}, f32[224,128]{1,0:T(8,128)}) custom-call(s32[2]{0:T(128)} %pad_add_fusion.refs_0_, f32[128,256]{1,0:T(8,128)} %refs_1_.3, f32[128,256]{1,0:T(8,128)} %refs_2_.3, f32[2,48,256]{2,1,0:T(8,128)} %copy-done.1, f32[2,48,256]{2,1,0:T(8,128)} %copy-done.2), custom_call_target="tpu_custom_call" | custom-call | tf_op jit(solution)/shard_map/strip_kernel/pallas_call | solution.py:574
  15.7 0.0 collective-permute-start.2
  15.7 2.6 %collective-permute-start.3 = (f32[224,128]{1,0:T(8,128)}, f32[224,128]{1,0:T(8,128)S(1)}, u32[]{:S(2)}, u32[]{:S(2)}) collective-permute-start(f32[224,128]{1,0:T(8,128)} %get-tuple-element.24), channel_id=1, source_target_pairs={{0,7},{1,0},{2,1},{3,2},{4,3},{5,4},{6,5},{7,6},{8,15},{9,8},{10,9... | collective-permute-start | bytes 344072 | tf_op jit(solution)/shard_map/ppermute | solution.py:586
  18.3 2.7 %collective-permute-done.2.refs_5_ = f32[224,128]{1,0:T(8,128)S(1)} collective-permute-done((f32[224,128]{1,0:T(8,128)}, f32[224,128]{1,0:T(8,128)S(1)}, u32[]{:S(2)}, u32[]{:S(2)}) %collective-permute-start.2) | collective-permute-done | bytes 114720 | tf_op jit(solution)/shard_map/ppermute | solution.py:586
  21.0 0.0 copy-start.4
  21.0 0.0 collective-permute-done.3.refs_6_
  21.0 0.6 copy-done.4
  21.6 0.0 copy-start.5
  21.7 0.6 copy-done.5
  22.3 3.7 %down_kernel.1 = (f32[224,384]{1,0:T(8,128)}, f32[224,384]{1,0:T(8,128)}, f32[224,384]{1,0:T(8,128)}, f32[224,384]{1,0:T(8,128)}, f32[112,256]{1,0:T(8,128)}, /*...) custom-call(s32[2]{0:T(128)} %pad_add_fusion.refs_0_, ...), custom_call_target="tpu_custom_call" | custom-call | tf_op jit(solution)/shard_map/down_kernel/pallas_call | solution.py:574
  26.0 14.9 %all_to_all.22 = f32[16,32,128]{2,1,0:T(8,128)S(1)} all-to-all(f32[16,32,128]{2,1,0:T(8,128)} %bitcast.17), channel_id=1, replica_groups={{0,2,4,6,8,10,12,14,16,18,20,22,24,26,28,30},{1,3,5,7,9,11,13,15,17,19,..., dimensions={0} | all-to-all | bytes 524288 | tf_op jit(solution)/shard_map/all_to_all | solution.py:596
  40.9 0.0 copy-start
  40.9 0.0 collective-permute-start.4
  41.0 1.5 %collective-permute-done.4.refs_2_ = f32[512,128]{1,0:T(8,128)S(1)} collective-permute-done((f32[512,128]{1,0:T(8,128)S(1)}, f32[512,128]{1,0:T(8,128)S(1)}, u32[]{:S(2)}, u32[]{:S(2)}) %collective-permute-start.4) | collective-permute-done | bytes 262176 | tf_op jit(solution)/shard_map/ppermute | solution.py:597
  42.5 0.0 copy-start.3
  42.5 0.0 copy-done
  42.5 0.7 %copy-done.3 = f32[512,128]{1,0:T(8,128)} copy-done((f32[512,128]{1,0:T(8,128)}, f32[512,128]{1,0:T(8,128)S(1)}, u32[]{:S(2)}) %copy-start.3) | copy-done | bytes 262168
  43.2 9.5 %middle_kernel.1 = (f32[2,2,48,128]{3,2,1,0:T(8,128)}, f32[1,1,48,128]{3,2,1,0:T(8,128)}, f32[2,2,48,128]{3,2,1,0:T(8,128)}, f32[1,1,48,128]{3,2,1,0:T(8,128)}, ...) custom-call(s32[2]{0:T(128)} %pad_add_fusion.refs_0_, f32[512,128]{1,0:T(8,128)} %bitcast.15, ...), custom_call_target="tpu_custom_call" | custom-call | tf_op jit(solution)/shard_map/middle_kernel/pallas_call | solution.py:574
  52.6 10.7 %all_to_all.23 = f32[32,4,128]{2,1,0:T(4,128)} all-to-all(f32[32,4,128]{2,1,0:T(4,128)} %bitcast.18), channel_id=1, replica_groups=mesh['gx'=4,'gy'=8] {'gx','gy'}, dimensions={0} | all-to-all | bytes 131072 | tf_op jit(solution)/shard_map/all_to_all | solution.py:590
  63.3 4.9 %up_kernel.1 = (f32[128,256]{1,0:T(8,128)}, f32[128,256]{1,0:T(8,128)}) custom-call(s32[2]{0:T(128)} %pad_add_fusion.refs_0_, f32[128,128]{1,0:T(8,128)} %bitcast.16, f32[2,2,48,128]{3,2,1,0:T(8,128)} %get-tuple-element.33.refs_2_, f32[1,1,48,128]{3,2,1,0:T(8,128)} %get-tuple-element.34.refs_3_, f32[2,2,48,128]{3,2,1,0:T(8,128)} %get-tuple-element.35.refs_4_, ...), custom_call_target="tpu_custom_call" | custom-call | tf_op jit(solution)/shard_map/up_kernel/pallas_call | solution.py:574
  (2 shorter events, 0.0 us)
Async XLA Ops:
  1.5 8.3 %collective-permute-start = (f32[2,48,256]{2,1,0:T(8,128)S(1)}, f32[2,48,256]{2,1,0:T(8,128)S(1)}, u32[]{:S(2)}, u32[]{:S(2)}) collective-permute-start(f32[2,48,256]{2,1,0:T(8,128)S(1)} %pad_maximum_fusion), channel_id=1, source_target_pairs={{0,24},{8,0},{16,8},{24,16},{1,25},{9,1},{17,9},{25,17},{2,26},{10... | collective-permute-start | bytes 294920 | tf_op jit(solution)/shard_map/ppermute | solution.py:586
  6.7 6.5 %collective-permute-start.1 = (f32[2,48,256]{2,1,0:T(8,128)S(1)}, f32[2,48,256]{2,1,0:T(8,128)S(1)}, u32[]{:S(2)}, u32[]{:S(2)}) collective-permute-start(f32[2,48,256]{2,1,0:T(8,128)S(1)} %pad_maximum_fusion.1), channel_id=1, source_target_pairs={{0,8},{8,16},{16,24},{24,0},{1,9},{9,17},{17,25},{25,1},{2,10},{10... | collective-permute-start | bytes 294920 | tf_op jit(solution)/shard_map/ppermute | solution.py:586
  9.9 3.3 %copy-start.1 = (f32[2,48,256]{2,1,0:T(8,128)}, f32[2,48,256]{2,1,0:T(8,128)S(1)}, u32[]{:S(2)}) copy-start(f32[2,48,256]{2,1,0:T(8,128)S(1)} %collective-permute-done.refs_3_) | copy-start | bytes 294916
  13.1 0.7 copy-start.2
  15.7 5.3 %collective-permute-start.2 = (f32[224,128]{1,0:T(8,128)}, f32[224,128]{1,0:T(8,128)S(1)}, u32[]{:S(2)}, u32[]{:S(2)}) collective-permute-start(f32[224,128]{1,0:T(8,128)} %get-tuple-element.23), channel_id=1, source_target_pairs={{0,1},{1,2},{2,3},{3,4},{4,5},{5,6},{6,7},{7,0},{8,9},{9,10},{10,1... | collective-permute-start | bytes 344072 | tf_op jit(solution)/shard_map/ppermute | solution.py:586
  15.7 5.3 %collective-permute-start.3 = (f32[224,128]{1,0:T(8,128)}, f32[224,128]{1,0:T(8,128)S(1)}, u32[]{:S(2)}, u32[]{:S(2)}) collective-permute-start(f32[224,128]{1,0:T(8,128)} %get-tuple-element.24), channel_id=1, source_target_pairs={{0,7},{1,0},{2,1},{3,2},{4,3},{5,4},{6,5},{7,6},{8,15},{9,8},{10,9... | collective-permute-start | bytes 344072 | tf_op jit(solution)/shard_map/ppermute | solution.py:586
  21.0 0.6 copy-start.4
  21.6 0.6 copy-start.5
  40.9 1.5 %copy-start = (f32[16,32,128]{2,1,0:T(8,128)}, f32[16,32,128]{2,1,0:T(8,128)S(1)}, u32[]{:S(2)}) copy-start(f32[16,32,128]{2,1,0:T(8,128)S(1)} %all_to_all.22) | copy-start | bytes 786436
  40.9 1.5 %collective-permute-start.4 = (f32[512,128]{1,0:T(8,128)S(1)}, f32[512,128]{1,0:T(8,128)S(1)}, u32[]{:S(2)}, u32[]{:S(2)}) collective-permute-start(f32[512,128]{1,0:T(8,128)S(1)} %bitcast.14), channel_id=1, source_target_pairs={{0,1},{1,0},{2,3},{3,2},{4,5},{5,4},{6,7},{7,6},{8,9},{9,8},{10,11... | collective-permute-start | bytes 786440 | tf_op jit(solution)/shard_map/ppermute | solution.py:597
  42.5 0.7 %copy-start.3 = (f32[512,128]{1,0:T(8,128)}, f32[512,128]{1,0:T(8,128)S(1)}, u32[]{:S(2)}) copy-start(f32[512,128]{1,0:T(8,128)S(1)} %collective-permute-done.4.refs_2_) | copy-start | bytes 786436

commit v3 on v2

--- a/solution.py
+++ b/solution.py
@@ -571,6 +571,8 @@
 
 def call(kernel, sizes, outs, scratch, *operands):
     shapes = [jax.ShapeDtypeStruct(shape, jnp.float32) for shape in outs]
+    used = sum(4 * int(np.prod(shape)) for shape in list(outs) + list(scratch))
+    used += sum(x.size * x.dtype.itemsize for x in operands)
     return pl.pallas_call(
         lambda *refs: kernel(sizes, *refs),
         name=kernel.__name__,
@@ -578,6 +580,7 @@
         in_specs=[pl.BlockSpec(memory_space=pltpu.SMEM)] + vmem(len(operands) - 1),
         out_specs=vmem(len(outs)),
         scratch_shapes=[pltpu.VMEM(shape, jnp.float32) for shape in scratch],
+        compiler_params=pltpu.CompilerParams(vmem_limit_bytes=used + used // 4 + (4 << 20)),
     )(*operands)
 
 

time: 68.7 us -> 61.1 us (0.89)
  Pallas kernels: 20 us -> 14.8 us
  local copies, waits for them, and re-layouts: 3.53 us -> 2.33 us
  blocking collectives: 25.6 us -> 24.6 us
    pallas_call x4, Pallas kernels: 20 us -> 14.8 us  [call(): pl.pallas_call(lambda *refs: kernel(sizes, *refs), name=kernel.__name__,...]
    unnamed x12 -> x28, local copies, waits for them, and re-layouts: 2.64 us -> 1.44 us
  transfers between devices with their start and end apart: 5 -> 5, of which waited for: 4 -> 4; matrix products, arithmetic and copies ran while one was open for 1% -> 0% of each run, Pallas kernels for 0% -> 0%
where the time goes in v3:
time: 61.1 us; the launch traced here: 60.8 us
  blocking collectives  24.6 us (40%)
  Pallas kernels  14.8 us (24%)
  waiting for transfers between devices  10.3 us (17%)
  starting transfers between devices  7.88 us (13%)
  local copies, waits for them, and re-layouts  2.33 us (4%)
  between operations  0.77 us (1%)
    pallas_call x4, Pallas kernels, call(): pl.pallas_call(lambda *refs: kernel(sizes, *refs), name=kernel.__name__,...  14.8 us
    all_to_all x1, blocking collectives, gather_by_core(): lax.all_to_all(copies, ('gx', 'gy'), 0, 0, tiled=True, axis_index_groups=...  14.4 us
    all_to_all x1, blocking collectives, gather(): return lax.all_to_all(copies, ('gx', 'gy'), 0, 0, tiled=True)  10.2 us
    ppermute x4, waiting for transfers between devices, ring(): lax.ppermute(values, axis, [(i, (i + step) % count) for i in range(count)])  8.79 us
    ppermute x4, starting transfers between devices, ring(): lax.ppermute(values, axis, [(i, (i + step) % count) for i in range(count)])  7.87 us
    ppermute x1, waiting for transfers between devices, gather_by_core(): return (own, lax.ppermute(own, 'gy', [(j, j ^ 1) for j in range(ny)]))  1.53 us
    unnamed x28, local copies, waits for them, and re-layouts  1.44 us
  transfers between devices with their start and end apart: 5, of which 4 were waited for; matrix products, arithmetic and copies ran while one was open for 0% of the time, Pallas kernels for 0%

profile of v3, /device:TPU:0, one launch (start us, length us, event | category | flops | bytes accessed | tf_op | source)
XLA Modules:
  0.0 60.8 jit_solution(11048352802377849)
XLA Ops:
  0.6 0.9 %slice_bitcast_fusion = (f32[1,48,256]{2,1,0:T(8,128)S(1)}, f32[1,48,256]{2,1,0:T(8,128)S(1)}, f32[1,48,256]{2,1,0:T(8,128)S(1)}, f32[1,48,256]{2,1,0:T(8,128)S(1)}) fusion(f32[128,256]{1,0:T(8,128)} %refs_2_.3, f32[128,256]{1,0:T(8,128)} %refs_1_.3), kind=kLoop, calls=%fused_computation.2 | loop fusion | bytes 393216 | tf_op jit(solution)/shard_map/stack | solution.py:609
  1.5 0.0 copy-start.1
  1.5 0.0 copy-start
  1.6 5.1 %collective-permute-start = (f32[2,48,256]{2,1,0:T(8,128)S(1)}, f32[2,48,256]{2,1,0:T(8,128)S(1)}, u32[]{:S(2)}, u32[]{:S(2)}) collective-permute-start(f32[2,48,256]{2,1,0:T(8,128)S(1)} %pad_maximum_fusion), channel_id=1, source_target_pairs={{0,24},{8,0},{16,8},{24,16},{1,25},{9,1},{17,9},{25,17},{2,26},{10... | collective-permute-start | bytes 294920 | tf_op jit(solution)/shard_map/ppermute | solution.py:589
  6.7 0.1 collective-permute-start.1
  6.8 0.1 pad_add_fusion.refs_0_
  6.8 3.0 %collective-permute-done.refs_3_ = f32[2,48,256]{2,1,0:T(8,128)S(1)} collective-permute-done((f32[2,48,256]{2,1,0:T(8,128)S(1)}, f32[2,48,256]{2,1,0:T(8,128)S(1)}, u32[]{:S(2)}, u32[]{:S(2)}) %collective-permute-start) | collective-permute-done | bytes 98336 | tf_op jit(solution)/shard_map/ppermute | solution.py:589
  9.9 3.3 %collective-permute-done.1.refs_4_ = f32[2,48,256]{2,1,0:T(8,128)S(1)} collective-permute-done((f32[2,48,256]{2,1,0:T(8,128)S(1)}, f32[2,48,256]{2,1,0:T(8,128)S(1)}, u32[]{:S(2)}, u32[]{:S(2)}) %collective-permute-start.1) | collective-permute-done | bytes 98336 | tf_op jit(solution)/shard_map/ppermute | solution.py:589
  13.2 0.0 copy-done.1
  13.2 0.0 copy-done
  13.2 0.7 %strip_kernel.1 = (f32[224,128]{1,0:T(8,128)S(1)}, f32[224,128]{1,0:T(8,128)S(1)}) custom-call(s32[2]{0:T(128)S(1)} %pad_add_fusion.refs_0_, f32[128,256]{1,0:T(8,128)S(1)} %copy-done, f32[128,256]{1,0:T(8,128)S(1)} %copy-done.1, f32[2,48,256]{2,1,0:T(8,128)S(1)} %collective-permute-done.refs_3_, f32[2,48,256]{2,1,0:T(8,128)S(1)} %collective-permute-done.1.refs_4_), custom_call_target="tpu_custom_call" | custom-call | tf_op jit(solution)/shard_map/strip_kernel/pallas_call | solution.py:576
  13.8 0.0 copy-start.13
  13.9 0.1 collective-permute-start.2
  13.9 2.6 %collective-permute-start.3 = (f32[224,128]{1,0:T(8,128)S(1)}, f32[224,128]{1,0:T(8,128)S(1)}, u32[]{:S(2)}, u32[]{:S(2)}) collective-permute-start(f32[224,128]{1,0:T(8,128)S(1)} %get-tuple-element.24), channel_id=1, source_target_pairs={{0,7},{1,0},{2,1},{3,2},{4,3},{5,4},{6,5},{7,6},{8,15},{9,8},{10,9... | collective-permute-start | bytes 344072 | tf_op jit(solution)/shard_map/ppermute | solution.py:589
  16.6 2.5 %collective-permute-done.2.refs_5_ = f32[224,128]{1,0:T(8,128)S(1)} collective-permute-done((f32[224,128]{1,0:T(8,128)S(1)}, f32[224,128]{1,0:T(8,128)S(1)}, u32[]{:S(2)}, u32[]{:S(2)}) %collective-permute-start.2) | collective-permute-done | bytes 114720 | tf_op jit(solution)/shard_map/ppermute | solution.py:589
  19.0 0.0 collective-permute-done.3.refs_6_
  19.0 0.0 copy-done.3
  19.0 0.0 copy-done.5
  19.0 0.0 copy-done.7
  19.1 0.0 copy-start.9
  19.1 0.0 copy-start.10
  19.1 2.3 %down_kernel.1 = (f32[224,384]{1,0:T(8,128)S(1)}, f32[224,384]{1,0:T(8,128)S(1)}, f32[224,384]{1,0:T(8,128)S(1)}, f32[224,384]{1,0:T(8,128)S(1)}, f32[112,256]{1...) custom-call(s32[2]{0:T(128)S(1)} %pad_add_fusion.refs_0_, ...), custom_call_target="tpu_custom_call" | custom-call | tf_op jit(solution)/shard_map/down_kernel/pallas_call | solution.py:576
  21.4 0.0 copy-start.2
  21.4 14.4 %all_to_all.22 = f32[16,32,128]{2,1,0:T(8,128)S(1)} all-to-all(f32[16,32,128]{2,1,0:T(8,128)S(1)} %bitcast.17), channel_id=1, replica_groups={{0,2,4,6,8,10,12,14,16,18,20,22,24,26,28,30},{1,3,5,7,9,11,13,15,17,19,..., dimensions={0} | all-to-all | bytes 524288 | tf_op jit(solution)/shard_map/all_to_all | solution.py:599
  35.8 0.0 collective-permute-start.4
  35.8 1.5 %collective-permute-done.4.refs_2_ = f32[512,128]{1,0:T(8,128)S(1)} collective-permute-done((f32[512,128]{1,0:T(8,128)S(1)}, f32[512,128]{1,0:T(8,128)S(1)}, u32[]{:S(2)}, u32[]{:S(2)}) %collective-permute-start.4) | collective-permute-done | bytes 262176 | tf_op jit(solution)/shard_map/ppermute | solution.py:600
  37.3 0.7 %copy-done.12 = bf16[8,16]{1,0:T(8,128)(2,1)S(1)} copy-done((bf16[8,16]{1,0:T(8,128)(2,1)S(1)}, bf16[8,16]{1,0:T(8,128)(2,1)}, u32[]{:S(2)}) %copy-start.12) | copy-done | bytes 280
  38.0 8.0 %middle_kernel.1 = (f32[2,2,48,128]{3,2,1,0:T(8,128)S(1)}, f32[1,1,48,128]{3,2,1,0:T(8,128)S(1)}, f32[2,2,48,128]{3,2,1,0:T(8,128)S(1)}, f32[1,1,48,128]{3,2,1,0...) custom-call(s32[2]{0:T(128)S(1)} %pad_add_fusion.refs_0_, ...), custom_call_target="tpu_custom_call" | custom-call | tf_op jit(solution)/shard_map/middle_kernel/pallas_call | solution.py:576
  46.0 0.0 copy-start.6
  46.0 10.2 %all_to_all.23 = f32[32,4,128]{2,1,0:T(4,128)S(1)} all-to-all(f32[32,4,128]{2,1,0:T(4,128)S(1)} %bitcast.18), channel_id=1, replica_groups=mesh['gx'=4,'gy'=8] {'gx','gy'}, dimensions={0} | all-to-all | bytes 131072 | tf_op jit(solution)/shard_map/all_to_all | solution.py:593
  56.3 0.7 %copy-done.11 = bf16[56,8]{1,0:T(8,128)(2,1)S(1)} copy-done((bf16[56,8]{1,0:T(8,128)(2,1)S(1)}, bf16[56,8]{1,0:T(8,128)(2,1)}, u32[]{:S(2)}) %copy-start.11) | copy-done | bytes 920
  57.0 3.8 %up_kernel.1 = (f32[128,256]{1,0:T(8,128)}, f32[128,256]{1,0:T(8,128)}) custom-call(s32[2]{0:T(128)S(1)} %pad_add_fusion.refs_0_, f32[128,128]{1,0:T(8,128)S(1)} %bitcast.16, f32[2,2,48,128]{3,2,1,0:T(8,128)S(1)} %get-tuple-element.33.refs_2_, f32[1,1,48,128]{3,2,1,0:T(8,128)S(1)} %get-tuple-element.34.refs_3_, ...), custom_call_target="tpu_custom_call" | custom-call | tf_op jit(solution)/shard_map/up_kernel/pallas_call | solution.py:576
  (16 shorter events, 0.0 us)
Async XLA Ops:
  1.5 11.6 %copy-start.1 = (f32[128,256]{1,0:T(8,128)S(1)}, f32[128,256]{1,0:T(8,128)}, u32[]{:S(2)}) copy-start(f32[128,256]{1,0:T(8,128)} %refs_2_.3) | copy-start | bytes 393220
  1.5 11.6 %copy-start = (f32[128,256]{1,0:T(8,128)S(1)}, f32[128,256]{1,0:T(8,128)}, u32[]{:S(2)}) copy-start(f32[128,256]{1,0:T(8,128)} %refs_1_.3) | copy-start | bytes 393220
  1.6 8.3 %collective-permute-start = (f32[2,48,256]{2,1,0:T(8,128)S(1)}, f32[2,48,256]{2,1,0:T(8,128)S(1)}, u32[]{:S(2)}, u32[]{:S(2)}) collective-permute-start(f32[2,48,256]{2,1,0:T(8,128)S(1)} %pad_maximum_fusion), channel_id=1, source_target_pairs={{0,24},{8,0},{16,8},{24,16},{1,25},{9,1},{17,9},{25,17},{2,26},{10... | collective-permute-start | bytes 294920 | tf_op jit(solution)/shard_map/ppermute | solution.py:589
  6.7 6.5 %collective-permute-start.1 = (f32[2,48,256]{2,1,0:T(8,128)S(1)}, f32[2,48,256]{2,1,0:T(8,128)S(1)}, u32[]{:S(2)}, u32[]{:S(2)}) collective-permute-start(f32[2,48,256]{2,1,0:T(8,128)S(1)} %pad_maximum_fusion.1), channel_id=1, source_target_pairs={{0,8},{8,16},{16,24},{24,0},{1,9},{9,17},{17,25},{25,1},{2,10},{10... | collective-permute-start | bytes 294920 | tf_op jit(solution)/shard_map/ppermute | solution.py:589
  6.8 12.2 %copy-start.3 = (bf16[256,128]{1,0:T(8,128)(2,1)S(1)}, bf16[256,128]{1,0:T(8,128)(2,1)}, u32[]{:S(2)}) copy-start(bf16[256,128]{1,0:T(8,128)(2,1)} %constant.33.clone.refs_8_.refs_11_) | copy-start | bytes 196612
  6.8 12.2 %copy-start.5 = (bf16[384,256]{1,0:T(8,128)(2,1)S(1)}, bf16[384,256]{1,0:T(8,128)(2,1)}, u32[]{:S(2)}) copy-start(bf16[384,256]{1,0:T(8,128)(2,1)} %constant.32.clone.refs_7_) | copy-start | bytes 589828
  6.8 12.2 %copy-start.7 = (bf16[128,512]{1,0:T(8,128)(2,1)S(1)}, bf16[128,512]{1,0:T(8,128)(2,1)}, u32[]{:S(2)}) copy-start(bf16[128,512]{1,0:T(8,128)(2,1)} %constant.34.clone.refs_9_) | copy-start | bytes 393220
  13.8 5.2 %copy-start.13 = (bf16[8,64]{1,0:T(8,128)(2,1)S(1)}, bf16[8,64]{1,0:T(8,128)(2,1)}, u32[]{:S(2)}) copy-start(bf16[8,64]{1,0:T(8,128)(2,1)} %constant.35.clone.refs_10_) | copy-start | bytes 3076
  13.9 5.2 %collective-permute-start.2 = (f32[224,128]{1,0:T(8,128)S(1)}, f32[224,128]{1,0:T(8,128)S(1)}, u32[]{:S(2)}, u32[]{:S(2)}) collective-permute-start(f32[224,128]{1,0:T(8,128)S(1)} %get-tuple-element.23), channel_id=1, source_target_pairs={{0,1},{1,2},{2,3},{3,4},{4,5},{5,6},{6,7},{7,0},{8,9},{9,10},{10,1... | collective-permute-start | bytes 344072 | tf_op jit(solution)/shard_map/ppermute | solution.py:589
  13.9 5.1 %collective-permute-start.3 = (f32[224,128]{1,0:T(8,128)S(1)}, f32[224,128]{1,0:T(8,128)S(1)}, u32[]{:S(2)}, u32[]{:S(2)}) collective-permute-start(f32[224,128]{1,0:T(8,128)S(1)} %get-tuple-element.24), channel_id=1, source_target_pairs={{0,7},{1,0},{2,1},{3,2},{4,3},{5,4},{6,5},{7,6},{8,15},{9,8},{10,9... | collective-permute-start | bytes 344072 | tf_op jit(solution)/shard_map/ppermute | solution.py:589
  19.1 18.3 %copy-start.9 = (bf16[128,256]{1,0:T(8,128)(2,1)S(1)}, bf16[128,256]{1,0:T(8,128)(2,1)}, u32[]{:S(2)}) copy-start(bf16[128,256]{1,0:T(8,128)(2,1)} %constant.38.clone.refs_12_) | copy-start | bytes 196612
  19.1 18.3 %copy-start.10 = (bf16[112,16]{1,0:T(8,128)(2,1)S(1)}, bf16[112,16]{1,0:T(8,128)(2,1)}, u32[]{:S(2)}) copy-start(bf16[112,16]{1,0:T(8,128)(2,1)} %constant.36.clone.refs_9_) | copy-start | bytes 10756
  21.4 15.9 %copy-start.2 = (bf16[1024,256]{1,0:T(8,128)(2,1)S(1)}, bf16[1024,256]{1,0:T(8,128)(2,1)}, u32[]{:S(2)}) copy-start(bf16[1024,256]{1,0:T(8,128)(2,1)} %constant.37.clone.refs_10_) | copy-start | bytes 1572868
  35.8 1.5 %collective-permute-start.4 = (f32[512,128]{1,0:T(8,128)S(1)}, f32[512,128]{1,0:T(8,128)S(1)}, u32[]{:S(2)}, u32[]{:S(2)}) collective-permute-start(f32[512,128]{1,0:T(8,128)S(1)} %bitcast.14), channel_id=1, source_target_pairs={{0,1},{1,0},{2,3},{3,2},{4,5},{5,4},{6,7},{7,6},{8,9},{9,8},{10,11... | collective-permute-start | bytes 786440 | tf_op jit(solution)/shard_map/ppermute | solution.py:600
  37.3 0.7 %copy-start.12 = (bf16[8,16]{1,0:T(8,128)(2,1)S(1)}, bf16[8,16]{1,0:T(8,128)(2,1)}, u32[]{:S(2)}) copy-start(bf16[8,16]{1,0:T(8,128)(2,1)} %constant.39.clone.refs_13_) | copy-start | bytes 772
  38.0 18.2 %copy-start.4 = (bf16[256,384]{1,0:T(8,128)(2,1)S(1)}, bf16[256,384]{1,0:T(8,128)(2,1)}, u32[]{:S(2)}) copy-start(bf16[256,384]{1,0:T(8,128)(2,1)} %constant.43.clone.refs_19_) | copy-start | bytes 589828
  38.0 18.2 %copy-start.8 = (bf16[128,256]{1,0:T(8,128)(2,1)S(1)}, bf16[128,256]{1,0:T(8,128)(2,1)}, u32[]{:S(2)}) copy-start(bf16[128,256]{1,0:T(8,128)(2,1)} %constant.42.clone.refs_18_) | copy-start | bytes 196612
  46.0 10.2 %copy-start.6 = (bf16[512,128]{1,0:T(8,128)(2,1)S(1)}, bf16[512,128]{1,0:T(8,128)(2,1)}, u32[]{:S(2)}) copy-start(bf16[512,128]{1,0:T(8,128)(2,1)} %constant.41.clone.refs_17_) | copy-start | bytes 393220
  56.3 0.7 %copy-start.11 = (bf16[56,8]{1,0:T(8,128)(2,1)S(1)}, bf16[56,8]{1,0:T(8,128)(2,1)}, u32[]{:S(2)}) copy-start(bf16[56,8]{1,0:T(8,128)(2,1)} %constant.40.clone.refs_16_) | copy-start | bytes 2692

commit v4 on v3

--- a/solution.py
+++ b/solution.py
@@ -50,8 +50,8 @@
     def __init__(self, rows, columns, nx, ny):
         self.rows, self.columns, self.nx, self.ny = rows, columns, nx, ny
         self.p, self.q = rows // 16, columns // 16
-        self.lanes = self.p * self.q
-        self.devices = nx * ny
+        self.coarse_rows, self.coarse_columns = nx * self.p, ny * self.q
+        assert self.p == 8 and 8 * self.q == 128, "block shape"
 
         def up(n):
             return -(-n // 128) * 128
@@ -76,48 +76,26 @@
         hit = (fine[:, None] // 2 == coarse[None, :]) & fine_in[:, None] & coarse_in[None, :]
         return hit.astype(jnp.bfloat16)
 
-    def pack_columns(self, level, pairs):
-        n = 1 << (LEVELS - level)
-        own = self.columns >> level
-        x = np.arange(self.ext_columns[2])[:, None, None]
-        cell = x // 2 if pairs else x
-        r = np.arange(n)[None, :, None]
-        lane = np.arange(self.lanes)[None, None, :]
-        hit = (cell == n * (lane // self.p) + r) & (cell < own)
-        return hit.reshape(len(x), n * self.lanes).astype(jnp.bfloat16)
-
-    def pack_rows(self, level, fields):
-        n = 1 << (LEVELS - level)
-        count = self.rows >> level
-        f = np.arange(fields)
-        s = np.arange(n)
-        k = np.arange(count)
-        hit = (f[:, None, None, None] == f[None, None, :, None]) & (k[None, None, None, :] % n == s[None, :, None, None])
-        hit = hit.reshape(fields * n, fields * count)
-        pad = -hit.shape[0] % 8
-        return np.pad(hit, ((0, pad), (0, 0))).astype(jnp.bfloat16)
-
-    def spread_rows(self, level):
-        n = 1 << (LEVELS - level)
-        k = self.row_at(level - 1) // 2
-        count = self.rows >> level
-        slot = (k // count + 1) * n + (k % count) % n
-        width = 3 * n + (-3 * n) % 8
-        return (slot[:, None] == np.arange(width)[None, :]).astype(jnp.bfloat16)
+    def pack_pair(self):
+        own = self.columns >> 2
+        x = np.arange(2 * own)
+        target = (x // own) * own + (x % own % 4) * self.q + x % own // 4
+        return (target[:, None] == np.arange(2 * own)[None, :]).astype(jnp.bfloat16)
+
+    def pack_single(self):
+        x = np.arange(self.ext_columns[2])[:, None]
+        lane = np.arange(128)[None, :]
+        hit = (x // 2 == 2 * (lane % self.q) + (lane // self.q) % 2) & (x < self.columns >> 2)
+        return hit.astype(jnp.bfloat16)
 
     def spread_columns(self, level):
         n = 1 << (LEVELS - level)
         column, inside = self.column_at(level - 1)
         m = column // 2
-        count = self.columns >> level
-        block = m // count
-        r = (m % count) % n
-        q = (m % count) // n
-        beside = np.arange(2)[:, None, None, None]
-        rr = np.arange(n)[None, :, None, None]
-        lane = np.arange(self.lanes)[None, None, :, None]
-        hit = ((block != 0) == beside) & (r == rr) & (q == lane // self.p) & inside
-        return hit.reshape(2 * n * self.lanes, -1).astype(jnp.bfloat16)
+        r = np.arange(n)[:, None, None]
+        lane = np.arange(128)[None, :, None]
+        hit = (m % n == r) & (m // n + self.q == lane) & inside
+        return hit.reshape(n * 128, -1).astype(jnp.bfloat16)
 
 
 def iota(shape, axis):
@@ -154,19 +132,30 @@
     return jnp.concatenate([scratch[t, : 2 * rows, :] for t in range(columns // 128)], axis=1)
 
 
-def pack(sizes, level, fields, columns_ref, rows_ref, out_ref):
-    n = 1 << (LEVELS - level)
-    count = sizes.rows >> level
-    spread = f32dot_right(jnp.concatenate(fields, axis=0), columns_ref[...])
-    shape = spread.shape
-    keep = ((iota(shape, 0) % count) // n) == (iota(shape, 1) % sizes.p)
-    out = f32dot_left(rows_ref[...], jnp.where(keep, spread, 0.0))
-    height = n * len(fields)
-    block = jnp.concatenate([out[:height, r * sizes.lanes : (r + 1) * sizes.lanes] for r in range(n)], axis=0)
-    copies = max(1, 8 // block.shape[0])
-    block = jnp.concatenate([block] * copies, axis=0)
-    for k in range(out_ref.shape[0] // block.shape[0]):
-        out_ref[k * block.shape[0] : (k + 1) * block.shape[0], :] = block
+def repeat(block, out_ref):
+    height = block.shape[0]
+    for k in range(out_ref.shape[0] // height):
+        out_ref[k * height : (k + 1) * height, :] = block
+
+
+def pack_two(sizes, gy, first, second, scratch, columns_ref, out_ref):
+    own = sizes.columns >> 2
+    both = jnp.where(iota(first.shape, 1) < own, first, pltpu.roll(second, own, 1))
+    rows = both.shape[0]
+    scratch[0, :rows, :] = f32dot_right(both, columns_ref[...])
+    block = jnp.concatenate([scratch[0, pl.ds(s, sizes.p, stride=4), :] for s in range(4)], axis=0)
+    repeat(pltpu.roll(block, lax.rem(gy, 8) * sizes.q, 1), out_ref)
+
+
+def pack_one(sizes, gy, values, scratch, columns_ref, out_ref):
+    rows = values.shape[0]
+    scratch[0, :rows, :] = f32dot_right(values, columns_ref[...])
+    part = iota((4, 128), 1) // (2 * sizes.q)
+    block = scratch[0, pl.ds(0, 4, stride=2), :]
+    for k in range(1, 4):
+        block = jnp.where(part == k, scratch[0, pl.ds(8 * (k // 2) + k % 2, 4, stride=2), :], block)
+    block = jnp.concatenate([block, block], axis=0)
+    repeat(pltpu.roll(block, lax.rem(gy, 8) * sizes.q, 1), out_ref)
 
 
 def strip_kernel(sizes, at_ref, g_ref, s_ref, below_ref, above_ref, left_ref, right_ref):
@@ -187,7 +176,7 @@
     return d, jnp.where(inside_mask(sizes, level, gx, gy), DAMPING / d, 0.0)
 
 
-def down_kernel(sizes, at_ref, g_ref, s_ref, below_ref, above_ref, left_ref, right_ref, rc0_ref, rc1_ref, pc_ref, pr_ref,
+def down_kernel(sizes, at_ref, g_ref, s_ref, below_ref, above_ref, left_ref, right_ref, rc0_ref, rc1_ref, pc_ref,
                 g0_ref, d0_ref, w0_ref, v0_ref, c1_ref, d1_ref, w1_ref, v1_ref, d2_ref, w2_ref, out_ref, scratch):
     gx, gy = at_ref[0], at_ref[1]
     rows = sizes.ext_rows[0]
@@ -225,7 +214,7 @@
     d2_ref[...] = d
     w2_ref[...] = w
     own = sizes.rows // 4
-    pack(sizes, 2, [g[:own], sigma[:own]], pc_ref, pr_ref, out_ref)
+    pack_two(sizes, gy, g[:own], sigma[:own], scratch, pc_ref, out_ref)
 
 
 class Coarse:
@@ -233,56 +222,45 @@
         self.z = sizes
         self.first = first
         self.d, self.w, self.g, self.v, self.t = d_refs, w_refs, g_refs, v_refs, t_refs
-        shape = (sizes.ny, sizes.lanes)
-        lane, row = iota(shape, 1), iota(shape, 0)
-        p, q = lane % sizes.p, lane // sizes.p
-        self.first_p, self.last_p = p == 0, p == sizes.p - 1
-        self.first_q, self.last_q = q == 0, q == sizes.q - 1
-        self.first_row, self.last_row = row == 0, row == sizes.ny - 1
+        lane = iota((sizes.p, sizes.coarse_columns), 1)
+        self.first_lane, self.last_lane = lane == 0, lane == sizes.coarse_columns - 1
 
     def blocks(self, body):
+        p = self.z.p
         if self.z.nx <= 4:
             for gx in range(self.z.nx):
-                body((gx + 1) * self.z.ny)
+                body((gx + 1) * p)
         else:
             def step(gx, carry):
-                body(pl.multiple_of((gx + 1) * self.z.ny, 8))
+                body(pl.multiple_of((gx + 1) * p, 8))
                 return carry
 
             lax.fori_loop(0, self.z.nx, step, 0)
 
     def at(self, ref, s, r, base):
-        return ref[s, r, pl.ds(base, self.z.ny), :]
+        return ref[s, r, pl.ds(base, self.z.p), :]
 
     def put(self, ref, s, r, base, value):
-        ref[s, r, pl.ds(base, self.z.ny), :] = value
+        ref[s, r, pl.ds(base, self.z.p), :] = value
+
+    def beside(self, ref, s, r, base, step):
+        p = self.z.p
+        if isinstance(base, int):
+            return ref[s, r, pl.ds(base + step, p), :]
+        return ref[s, r, pl.ds(base - p, 3 * p), :][p + step : 2 * p + step]
 
     def neighbours(self, ref, s, r, n, base):
-        z = self.z
+        columns = self.z.coarse_columns
         if r < n - 1:
             right = self.at(ref, s, r + 1, base)
         else:
-            x = self.at(ref, s, 0, base)
-            moved = jnp.where(self.last_row, 0.0, pltpu.roll(x, z.ny - 1, 0))
-            right = pltpu.roll(jnp.where(self.first_q, moved, x), z.lanes - z.p, 1)
+            right = jnp.where(self.last_lane, 0.0, pltpu.roll(self.at(ref, s, 0, base), columns - 1, 1))
         if r > 0:
             left = self.at(ref, s, r - 1, base)
         else:
-            x = self.at(ref, s, n - 1, base)
-            moved = jnp.where(self.first_row, 0.0, pltpu.roll(x, 1, 0))
-            left = pltpu.roll(jnp.where(self.last_q, moved, x), z.p, 1)
-        if s < n - 1:
-            down = self.at(ref, s + 1, r, base)
-        else:
-            here = pltpu.roll(self.at(ref, 0, r, base), z.lanes - 1, 1)
-            there = pltpu.roll(self.at(ref, 0, r, base + z.ny), z.p - 1, 1)
-            down = jnp.where(self.last_p, there, here)
-        if s > 0:
-            up = self.at(ref, s - 1, r, base)
-        else:
-            here = pltpu.roll(self.at(ref, n - 1, r, base), 1, 1)
-            there = pltpu.roll(self.at(ref, n - 1, r, base - z.ny), z.lanes - z.p + 1, 1)
-            up = jnp.where(self.first_p, there, here)
+            left = jnp.where(self.first_lane, 0.0, pltpu.roll(self.at(ref, s, n - 1, base), 1, 1))
+        down = self.at(ref, s + 1, r, base) if s < n - 1 else self.beside(ref, 0, r, base, 1)
+        up = self.at(ref, s - 1, r, base) if s > 0 else self.beside(ref, n - 1, r, base, -1)
         return (up + down) + (left + right)
 
     def each(self, level, body):
@@ -351,45 +329,62 @@
 
         self.each(level, body)
 
-    def total(self, of):
-        z = self.z
-        if z.nx <= 4:
-            parts = [of((gx + 1) * z.ny) for gx in range(z.nx)]
-            value = parts[0]
-            for part in parts[1:]:
-                value = value + part
-        else:
-            value = lax.fori_loop(
-                0, z.nx, lambda gx, acc: acc + of(pl.multiple_of((gx + 1) * z.ny, 8)),
-                jnp.zeros((z.ny, z.lanes), jnp.float32))
-        return jnp.sum(jnp.sum(value, axis=0, keepdims=True), axis=1, keepdims=True)
+    def inner(self, ref):
+        p = self.z.p
+        return ref[0, 0, p : p + self.z.coarse_rows, :]
+
+    def shifted(self, x, k):
+        if k == 0:
+            return x
+        columns = self.z.coarse_columns
+        lane = iota(x.shape, 1)
+        keep = lane < columns - k if k > 0 else lane >= -k
+        return jnp.where(keep, pltpu.roll(x, -k % columns, 1), 0.0)
 
     def unit(self):
         z = self.z
         top = LEVELS - self.first
-        missing = 2.0 * (z.nx * z.p + z.ny * z.q) - 0.0
-        cells = 4.0
-        total = self.total(lambda base: self.at(self.d[top], 0, 0, base) - cells)
-        return total + missing
+        d, w = self.inner(self.d[top]), self.inner(self.w[top])
+        missing = 2.0 * (z.coarse_rows + z.coarse_columns)
+        return 1.0 / (jnp.sum(d - 4.0, keepdims=True) + missing), {k: self.shifted(w, k) for k in range(-2, 3)}
 
     def coarse(self, fresh, unit):
         top = LEVELS - self.first
-        v, t, g = self.v[top], self.t[top], self.g[top]
+        one, w = unit
+        g = self.inner(self.g[top])
+        shape = g.shape
+        row, lane = iota(shape, 0), iota(shape, 1)
+        first_row, last_row = row == 0, row == shape[0] - 1
+        sources = {k: self.shifted(g, k) for k in range(-2, 3)}
+
+        def vertical(x):
+            return jnp.where(first_row, 0.0, pltpu.roll(x, 1, 0)) + jnp.where(last_row, 0.0, pltpu.roll(x, shape[0] - 1, 0))
+
+        def three(v):
+            for reach in (2, 1, 0):
+                v = {
+                    k: (1.0 - DAMPING) * v[k] + w[k] * ((sources[k] + vertical(v[k])) + (v[k - 1] + v[k + 1]))
+                    for k in range(-reach, reach + 1)
+                }
+            return v[0]
+
         if fresh:
-            left = self.total(lambda base: self.at(g, 0, 0, base)) / unit
-
-            def body(base):
-                self.put(v, 0, 0, base, jnp.broadcast_to(left, (self.z.ny, self.z.lanes)))
+            left = jnp.sum(g, keepdims=True) * one
+            v = {k: 0.0 for k in range(-3, 4)}
         else:
-            left = self.total(lambda base: self.residual(LEVELS, 0, 0, 1, base)) / unit
-
-            def body(base):
-                self.put(v, 0, 0, base, self.at(v, 0, 0, base) + left)
-
-        self.blocks(body)
-        for turn in range(COARSE_SWEEPS // 2):
-            self.sweep(LEVELS, v, t)
-            self.sweep(LEVELS, t, v)
+            v = self.inner(self.v[top])
+            v = {k: self.shifted(v, k) for k in range(-3, 4)}
+            around_v = vertical(v[0]) + (v[-1] + v[1])
+            left = jnp.sum((g - self.inner(self.d[top]) * v[0]) + around_v, keepdims=True) * one
+        left = jnp.broadcast_to(left, shape)
+        for k in range(-3, 4):
+            v[k] = v[k] + jnp.where((lane < shape[1] - k) & (lane >= -k), left, 0.0)
+        for turn in range(COARSE_SWEEPS // 3):
+            if turn:
+                v = {k: self.shifted(v, k) for k in range(-3, 4)}
+            v = three(v)
+        p = self.z.p
+        self.v[top][0, 0, p : p + shape[0], :] = v
 
     def vcycle(self, level, fresh, unit):
         if level == LEVELS:
@@ -417,80 +412,87 @@
 
     def clear_ends(self):
         z = self.z
-        zero = jnp.zeros((z.ny, z.lanes), jnp.float32)
+        zero = jnp.zeros((z.p, z.coarse_columns), jnp.float32)
         for refs in (self.v, self.t):
             for ref in refs:
                 n = ref.shape[0]
                 for s in range(n):
                     for r in range(n):
-                        ref[s, r, : z.ny, :] = zero
-                        ref[s, r, (z.nx + 1) * z.ny :, :] = zero
-
-    def take(self, y_ref, target, offset, height):
+                        ref[s, r, : z.p, :] = zero
+                        ref[s, r, z.p + z.coarse_rows :, :] = zero
+
+    def turned(self, blocks, k):
+        q = self.z.q
+        part = iota(blocks[0].shape, 1) // q
+        out = blocks[-k % 8]
+        for x in range(1, 8):
+            out = jnp.where(part == x, blocks[(x - k) % 8], out)
+        return pltpu.roll(out, -k * q % 128, 1) if k else out
+
+    def take_two(self, even_ref, odd_ref, targets):
         z = self.z
-        n = target.shape[0]
-
-        def block(base):
-            for s in range(n):
-                for r in range(n):
-                    first = (base - z.ny) * n * height + r * height + offset + s
-                    self.put(target, s, r, base, y_ref[pl.ds(first, z.ny, stride=n * height), :])
-
-        self.blocks(block)
-
-    def take_cores(self, even_ref, odd_ref, target, offset, height, add):
+        for gx in range(z.nx):
+            for group in range(z.ny // 8):
+                lanes = slice(group * 128, (group + 1) * 128)
+                for s in range(4):
+                    blocks = []
+                    for g in range(8):
+                        first = (gx * (z.ny // 2) + group * 4 + g // 2) * 4 * z.p + s * z.p
+                        blocks.append((even_ref, odd_ref)[g % 2][first : first + z.p, :])
+                    for k in range(8):
+                        target, add = targets[k // 4]
+                        value = self.turned(blocks, k)
+                        target[s, k % 4, (gx + 1) * z.p : (gx + 2) * z.p, lanes] = value + add if add else value
+
+    def take_one(self, y_ref, target):
         z = self.z
-        n = target.shape[0]
-        half = z.ny // 2
-
-        def block(base):
-            for s in range(n):
-                for r in range(n):
-                    first = (base - z.ny) // 2 * n * height + r * height + offset + s
-                    for core, ref in ((0, even_ref), (1, odd_ref)):
-                        value = ref[pl.ds(first, half, stride=n * height), :]
-                        target[s, r, pl.ds(base + core, half, stride=2), :] = value + add if add else value
-
-        self.blocks(block)
-
-    def spread(self, gx, gy, rows_ref, columns_ref, e_ref):
+        low = iota((8, 128), 0) < 4
+        for gx in range(z.nx):
+            for group in range(z.ny // 8):
+                upper, lower = [], []
+                for g in range(0, 8, 2):
+                    first = (gx * z.ny + group * 8 + g) * 4
+                    pair = y_ref[first : first + 8, :]
+                    swapped = pltpu.roll(pair, 4, 0)
+                    upper += [pair, swapped]
+                    lower += [swapped, pair]
+                for k in range(4):
+                    value = jnp.where(low, self.turned(upper, k), self.turned(lower, k + 4))
+                    target[k // 2, k % 2, (gx + 1) * z.p : (gx + 2) * z.p, group * 128 : (group + 1) * 128] = value
+
+    def spread(self, gx, gy, columns_ref, scratch):
         z = self.z
         n = 1 << (LEVELS - self.first)
-        row = (gx + 1) * z.ny + gy
-        lane = iota((1, z.lanes), 1)
-        low_half = lane // z.p < z.q // 2
-        has_left, has_right = gy > 0, gy < z.ny - 1
-        e_ref[...] = jnp.zeros(e_ref.shape, jnp.float32)
-        ref = self.v[0]
-        for dx in range(3):
-            base = row + (dx - 1) * z.ny
+        above = self.first - 1
+        columns = z.coarse_columns
+        turn = lax.rem(columns + z.q - gy * z.q, columns)
+        start = pl.multiple_of(gx * z.p, 8)
+        parts = []
+        for s in range(n):
+            line = [pltpu.roll(self.v[0][s, r, pl.ds(start, 3 * z.p), :], turn, 1)[:, :128] for r in range(n)]
+            parts.append(jnp.concatenate(line, axis=1))
+        wide = f32dot_right(jnp.concatenate(parts, axis=0), columns_ref[...])
+        own, halo = z.rows >> above, HALO >> above
+        inner, outer = (own + halo) // (2 * n), halo // (2 * n)
+        tiles = wide.shape[1] // 128
+        for t in range(tiles):
             for s in range(n):
-                for r in range(n):
-                    own = ref[s, r, pl.ds(base, 1), :]
-                    left = ref[s, r, pl.ds(jnp.where(has_left, base - 1, 0), 1), :]
-                    right = ref[s, r, pl.ds(jnp.where(has_right, base + 1, 0), 1), :]
-                    k = dx * n + s
-                    e_ref[k : k + 1, r * z.lanes : (r + 1) * z.lanes] = own
-                    e_ref[k : k + 1, (n + r) * z.lanes : (n + r + 1) * z.lanes] = jnp.where(low_half, right, left)
-        spread = f32dot_left(rows_ref[...], e_ref[...])
-        shape = spread.shape
-        index = iota(shape, 0)
-        above = self.first - 1
-        own_r, halo = z.rows >> above, HALO >> above
-        cell = jnp.where(index < own_r + halo, index, index - shape[0]) + 2 * z.rows
-        keep = ((cell // (2 * n)) % z.p) == (iota(shape, 1) % z.p)
-        return f32dot_right(jnp.where(keep, spread, 0.0), columns_ref[...])
+                part = wide[s * 3 * z.p : (s + 1) * 3 * z.p, t * 128 : (t + 1) * 128]
+                for a in range(2):
+                    scratch[t, pl.ds(2 * s + a, inner, stride=2 * n), :] = part[z.p : z.p + inner]
+                    scratch[t, pl.ds(own + halo + 2 * s + a, outer, stride=2 * n), :] = part[z.p - outer : z.p]
+        return jnp.concatenate([scratch[t, : own + 2 * halo, :] for t in range(tiles)], axis=1)
 
 
 def level_shape(sizes, level):
     n = 1 << (LEVELS - level)
-    return (n, n, (sizes.nx + 2) * sizes.ny, sizes.lanes)
-
-
-def middle_kernel(sizes, at_ref, y_ref, other_ref, c1_ref, d1_ref, w1_ref, v1_ref, w2l_ref, d2l_ref, sr_ref, sc_ref,
-                  rc1_ref, pc_ref, pr_ref,
+    return (n, n, sizes.coarse_rows + 2 * sizes.p, sizes.coarse_columns)
+
+
+def middle_kernel(sizes, at_ref, y_ref, other_ref, c1_ref, d1_ref, w1_ref, v1_ref, w2l_ref, d2l_ref, sc_ref,
+                  rc1_ref, pc_ref,
                   d3_ref, d4_ref, w3_ref, w4_ref, e1_ref, c2_ref, e2_ref, out_ref,
-                  d2, w2, g2, g3, g4, v2, v3, v4, t2, t3, t4, e_ref, scratch):
+                  d2, w2, g2, g3, g4, v2, v3, v4, t2, t3, t4, scratch):
     gx, gy = at_ref[0], at_ref[1]
     m = Coarse(sizes, 2, [d2, d3_ref, d4_ref], [w2, w3_ref, w4_ref], [g2, g3, g4], [v2, v3, v4], [t2, t3, t4])
     m.clear_ends()
@@ -498,13 +500,11 @@
 
     @pl.when(core == 0)
     def _():
-        m.take_cores(y_ref, other_ref, g2, 0, 8, 0.0)
-        m.take_cores(y_ref, other_ref, d2, 4, 8, 4.0)
+        m.take_two(y_ref, other_ref, ((g2, 0.0), (d2, 4.0)))
 
     @pl.when(core == 1)
     def _():
-        m.take_cores(other_ref, y_ref, g2, 0, 8, 0.0)
-        m.take_cores(other_ref, y_ref, d2, 4, 8, 4.0)
+        m.take_two(other_ref, y_ref, ((g2, 0.0), (d2, 4.0)))
 
     for l in range(2):
         n = 2 >> l
@@ -525,7 +525,7 @@
     m.fcycle(2, unit)
     m.vcycle(2, False, unit)
     g, d, w = c1_ref[...], d1_ref[...], w1_ref[...]
-    v = v1_ref[...] + jnp.where(w > 0.0, m.spread(gx, gy, sr_ref, sc_ref, e_ref), 0.0)
+    v = v1_ref[...] + jnp.where(w > 0.0, m.spread(gx, gy, sc_ref, scratch), 0.0)
     for turn in range(4):
         v = sweep(v, g, w)
     e1_ref[...] = v
@@ -537,19 +537,19 @@
     r = g - d * v + around(v)
     c2_ref[...] = g
     e2_ref[...] = v
-    pack(sizes, 3, [pair_rows(scratch, r[: sizes.rows // 4])], pc_ref, pr_ref, out_ref)
+    pack_one(sizes, gy, pair_rows(scratch, r[: sizes.rows // 4]), scratch, pc_ref, out_ref)
 
 
 def up_kernel(sizes, at_ref, y_ref, d3_ref, d4_ref, w3_ref, w4_ref, c2_ref, w2_ref, e2_ref, c1_ref, w1_ref, e1_ref,
-              g0_ref, d0_ref, w0_ref, v0_ref, sr_ref, sc_ref, pc1_ref, pc0_ref,
-              solution_ref, residual_ref, g3, g4, v3, v4, t3, t4, e_ref, scratch):
+              g0_ref, d0_ref, w0_ref, v0_ref, sc_ref, pc1_ref, pc0_ref,
+              solution_ref, residual_ref, g3, g4, v3, v4, t3, t4, scratch):
     gx, gy = at_ref[0], at_ref[1]
     m = Coarse(sizes, 3, [d3_ref, d4_ref], [w3_ref, w4_ref], [g3, g4], [v3, v4], [t3, t4])
     m.clear_ends()
-    m.take(y_ref, g3, 0, 2)
+    m.take_one(y_ref, g3)
     m.vcycle(3, True, m.unit())
     g, w = c2_ref[...], w2_ref[...]
-    v = e2_ref[...] + jnp.where(w > 0.0, m.spread(gx, gy, sr_ref, sc_ref, e_ref), 0.0)
+    v = e2_ref[...] + jnp.where(w > 0.0, m.spread(gx, gy, sc_ref, scratch), 0.0)
     for turn in range(2):
         v = sweep(v, g, w)
     g, w = c1_ref[...], w1_ref[...]
@@ -615,20 +615,20 @@
     rc0, rc1 = z.restrict_columns(0), z.restrict_columns(1)
     tiles = (ext[0][1] // 128, ext[0][0], 128)
     g0, d0, w0, v0, c1, d1, w1, v1, d2, w2, packed = call(
-        down_kernel, z, [ext[0]] * 4 + [ext[1]] * 4 + [ext[2]] * 2 + [(nx * ny // 2 * 32, z.lanes)], [tiles],
-        at, right_side, shift, below, above, left, right, rc0, rc1, z.pack_columns(2, False), z.pack_rows(2, 2))
+        down_kernel, z, [ext[0]] * 4 + [ext[1]] * 4 + [ext[2]] * 2 + [(nx * ny // 2 * 4 * z.p, 128)], [tiles],
+        at, right_side, shift, below, above, left, right, rc0, rc1, z.pack_pair())
     y, other = gather_by_core(packed, nx, ny)
     slabs = [level_shape(z, level) for level in (2, 3, 4)]
     d3, d4, w3, w4, e1, c2, e2, packed = call(
-        middle_kernel, z, slabs[1:] * 2 + [ext[1], ext[2], ext[2], (nx * ny * 4, z.lanes)],
-        [slabs[0]] * 2 + slabs * 3 + [(16, 8 * z.lanes), tiles],
-        at, y, other, c1, d1, w1, v1, w2, d2, z.spread_rows(2), z.spread_columns(2),
-        rc1, z.pack_columns(3, True), z.pack_rows(3, 1))
+        middle_kernel, z, slabs[1:] * 2 + [ext[1], ext[2], ext[2], (nx * ny * 4, 128)],
+        [slabs[0]] * 2 + slabs * 3 + [tiles],
+        at, y, other, c1, d1, w1, v1, w2, d2, z.spread_columns(2),
+        rc1, z.pack_single())
     y = gather(packed)
     return call(
-        up_kernel, z, [(rows, columns)] * 2, slabs[1:] * 3 + [(8, 4 * z.lanes), tiles],
+        up_kernel, z, [(rows, columns)] * 2, slabs[1:] * 3 + [tiles],
         at, y, d3, d4, w3, w4, c2, w2, e2, c1, w1, e1, g0, d0, w0, v0,
-        z.spread_rows(3), z.spread_columns(3), rc1.T, rc0.T)
+        z.spread_columns(3), rc1.T, rc0.T)
 
 
 def solution(mesh):

time: 61.1 us -> 56.2 us (0.920)
  Pallas kernels: 14.8 us -> 11.4 us
  local copies, waits for them, and re-layouts: 2.33 us -> 0.94 us
    pallas_call x4, Pallas kernels: 14.8 us -> 11.4 us  [call(): pl.pallas_call(lambda *refs: kernel(sizes, *refs), name=kernel.__name__,...]
    unnamed x28 -> x20, local copies, waits for them, and re-layouts: 1.44 us -> 0.05 us
where the time goes in v4:
time: 56.2 us; the launch traced here: 55.9 us
  blocking collectives  24.6 us (44%)
  Pallas kernels  11.4 us (20%)
  waiting for transfers between devices  10.3 us (18%)
  starting transfers between devices  7.88 us (14%)
  local copies, waits for them, and re-layouts  0.94 us (2%)
  between operations  0.75 us (1%)
    all_to_all x1, blocking collectives, gather_by_core(): lax.all_to_all(copies, ('gx', 'gy'), 0, 0, tiled=True, axis_index_groups=...  14.4 us
    pallas_call x4, Pallas kernels, call(): pl.pallas_call(lambda *refs: kernel(sizes, *refs), name=kernel.__name__,...  11.4 us
    all_to_all x1, blocking collectives, gather(): return lax.all_to_all(copies, ('gx', 'gy'), 0, 0, tiled=True)  10.2 us
    ppermute x4, waiting for transfers between devices, ring(): lax.ppermute(values, axis, [(i, (i + step) % count) for i in range(count)])  8.79 us
    ppermute x4, starting transfers between devices, ring(): lax.ppermute(values, axis, [(i, (i + step) % count) for i in range(count)])  7.87 us
    ppermute x1, waiting for transfers between devices, gather_by_core(): return (own, lax.ppermute(own, 'gy', [(j, j ^ 1) for j in range(ny)]))  1.53 us
  transfers between devices with their start and end apart: 5, of which 4 were waited for; matrix products, arithmetic and copies ran while one was open for 0% of the time, Pallas kernels for 0%

profile of v4, /device:TPU:0, one launch (start us, length us, event | category | flops | bytes accessed | tf_op | source)
XLA Modules:
  0.0 55.9 jit_solution(12247169988574249385)
XLA Ops:
  0.6 0.9 %slice_bitcast_fusion = (f32[1,48,256]{2,1,0:T(8,128)S(1)}, f32[1,48,256]{2,1,0:T(8,128)S(1)}, f32[1,48,256]{2,1,0:T(8,128)S(1)}, f32[1,48,256]{2,1,0:T(8,128)S(1)}) fusion(f32[128,256]{1,0:T(8,128)} %refs_2_.3, f32[128,256]{1,0:T(8,128)} %refs_1_.3), kind=kLoop, calls=%fused_computation.2 | loop fusion | bytes 393216 | tf_op jit(solution)/shard_map/stack | solution.py:609
  1.5 0.0 copy-start.1
  1.5 0.0 copy-start
  1.6 5.1 %collective-permute-start = (f32[2,48,256]{2,1,0:T(8,128)S(1)}, f32[2,48,256]{2,1,0:T(8,128)S(1)}, u32[]{:S(2)}, u32[]{:S(2)}) collective-permute-start(f32[2,48,256]{2,1,0:T(8,128)S(1)} %pad_maximum_fusion), channel_id=1, source_target_pairs={{0,24},{8,0},{16,8},{24,16},{1,25},{9,1},{17,9},{25,17},{2,26},{10... | collective-permute-start | bytes 294920 | tf_op jit(solution)/shard_map/ppermute | solution.py:589
  6.7 0.1 collective-permute-start.1
  6.8 0.1 pad_add_fusion.refs_0_
  6.8 3.0 %collective-permute-done.refs_3_ = f32[2,48,256]{2,1,0:T(8,128)S(1)} collective-permute-done((f32[2,48,256]{2,1,0:T(8,128)S(1)}, f32[2,48,256]{2,1,0:T(8,128)S(1)}, u32[]{:S(2)}, u32[]{:S(2)}) %collective-permute-start) | collective-permute-done | bytes 98336 | tf_op jit(solution)/shard_map/ppermute | solution.py:589
  9.9 3.3 %collective-permute-done.1.refs_4_ = f32[2,48,256]{2,1,0:T(8,128)S(1)} collective-permute-done((f32[2,48,256]{2,1,0:T(8,128)S(1)}, f32[2,48,256]{2,1,0:T(8,128)S(1)}, u32[]{:S(2)}, u32[]{:S(2)}) %collective-permute-start.1) | collective-permute-done | bytes 98336 | tf_op jit(solution)/shard_map/ppermute | solution.py:589
  13.2 0.0 copy-done.1
  13.2 0.0 copy-done
  13.2 0.7 %strip_kernel.1 = (f32[224,128]{1,0:T(8,128)S(1)}, f32[224,128]{1,0:T(8,128)S(1)}) custom-call(s32[2]{0:T(128)S(1)} %pad_add_fusion.refs_0_, f32[128,256]{1,0:T(8,128)S(1)} %copy-done, f32[128,256]{1,0:T(8,128)S(1)} %copy-done.1, f32[2,48,256]{2,1,0:T(8,128)S(1)} %collective-permute-done.refs_3_, f32[2,48,256]{2,1,0:T(8,128)S(1)} %collective-permute-done.1.refs_4_), custom_call_target="tpu_custom_call" | custom-call | tf_op jit(solution)/shard_map/strip_kernel/pallas_call | solution.py:576
  13.8 0.1 collective-permute-start.2
  13.9 2.6 %collective-permute-start.3 = (f32[224,128]{1,0:T(8,128)S(1)}, f32[224,128]{1,0:T(8,128)S(1)}, u32[]{:S(2)}, u32[]{:S(2)}) collective-permute-start(f32[224,128]{1,0:T(8,128)S(1)} %get-tuple-element.24), channel_id=1, source_target_pairs={{0,7},{1,0},{2,1},{3,2},{4,3},{5,4},{6,5},{7,6},{8,15},{9,8},{10,9... | collective-permute-start | bytes 344072 | tf_op jit(solution)/shard_map/ppermute | solution.py:589
  16.5 2.5 %collective-permute-done.2.refs_5_ = f32[224,128]{1,0:T(8,128)S(1)} collective-permute-done((f32[224,128]{1,0:T(8,128)S(1)}, f32[224,128]{1,0:T(8,128)S(1)}, u32[]{:S(2)}, u32[]{:S(2)}) %collective-permute-start.2) | collective-permute-done | bytes 114720 | tf_op jit(solution)/shard_map/ppermute | solution.py:589
  19.0 0.0 collective-permute-done.3.refs_6_
  19.0 0.0 copy-done.3
  19.0 0.0 copy-done.4
  19.0 0.0 copy-done.9
  19.0 2.2 %down_kernel.1 = (f32[224,384]{1,0:T(8,128)S(1)}, f32[224,384]{1,0:T(8,128)S(1)}, f32[224,384]{1,0:T(8,128)S(1)}, f32[224,384]{1,0:T(8,128)S(1)}, f32[112,256]{1...) custom-call(s32[2]{0:T(128)S(1)} %pad_add_fusion.refs_0_, ...), custom_call_target="tpu_custom_call" | custom-call | tf_op jit(solution)/shard_map/down_kernel/pallas_call | solution.py:576
  21.2 0.0 copy-start.2
  21.2 0.0 copy-start.8
  21.3 14.4 %all_to_all.22 = f32[16,32,128]{2,1,0:T(8,128)S(1)} all-to-all(f32[16,32,128]{2,1,0:T(8,128)S(1)} %bitcast.17), channel_id=1, replica_groups={{0,2,4,6,8,10,12,14,16,18,20,22,24,26,28,30},{1,3,5,7,9,11,13,15,17,19,..., dimensions={0} | all-to-all | bytes 524288 | tf_op jit(solution)/shard_map/all_to_all | solution.py:599
  35.6 0.0 collective-permute-start.4
  35.6 1.5 %collective-permute-done.4.refs_2_ = f32[512,128]{1,0:T(8,128)S(1)} collective-permute-done((f32[512,128]{1,0:T(8,128)S(1)}, f32[512,128]{1,0:T(8,128)S(1)}, u32[]{:S(2)}, u32[]{:S(2)}) %collective-permute-start.4) | collective-permute-done | bytes 262176 | tf_op jit(solution)/shard_map/ppermute | solution.py:600
  37.2 0.0 copy-done.2
  37.2 0.0 copy-done.8
  37.2 5.2 %middle_kernel.1 = (f32[2,2,48,128]{3,2,1,0:T(8,128)S(1)}, f32[1,1,48,128]{3,2,1,0:T(8,128)S(1)}, f32[2,2,48,128]{3,2,1,0:T(8,128)S(1)}, f32[1,1,48,128]{3,2,1,0...) custom-call(s32[2]{0:T(128)S(1)} %pad_add_fusion.refs_0_, ...), custom_call_target="tpu_custom_call" | custom-call | tf_op jit(solution)/shard_map/middle_kernel/pallas_call | solution.py:576
  42.4 10.2 %all_to_all.23 = f32[32,4,128]{2,1,0:T(4,128)S(1)} all-to-all(f32[32,4,128]{2,1,0:T(4,128)S(1)} %bitcast.18), channel_id=1, replica_groups=mesh['gx'=4,'gy'=8] {'gx','gy'}, dimensions={0} | all-to-all | bytes 131072 | tf_op jit(solution)/shard_map/all_to_all | solution.py:593
  52.6 0.0 copy-done.5
  52.6 0.0 copy-done.6
  52.6 0.0 copy-done.7
  52.6 3.3 %up_kernel.1 = (f32[128,256]{1,0:T(8,128)}, f32[128,256]{1,0:T(8,128)}) custom-call(s32[2]{0:T(128)S(1)} %pad_add_fusion.refs_0_, f32[128,128]{1,0:T(8,128)S(1)} %bitcast.16, f32[2,2,48,128]{3,2,1,0:T(8,128)S(1)} %get-tuple-element.33.refs_2_, f32[1,1,48,128]{3,2,1,0:T(8,128)S(1)} %get-tuple-element.34.refs_3_, ...), custom_call_target="tpu_custom_call" | custom-call | tf_op jit(solution)/shard_map/up_kernel/pallas_call | solution.py:576
  (8 shorter events, 0.0 us)
Async XLA Ops:
  1.5 11.6 %copy-start.1 = (f32[128,256]{1,0:T(8,128)S(1)}, f32[128,256]{1,0:T(8,128)}, u32[]{:S(2)}) copy-start(f32[128,256]{1,0:T(8,128)} %refs_2_.3) | copy-start | bytes 393220
  1.5 11.6 %copy-start = (f32[128,256]{1,0:T(8,128)S(1)}, f32[128,256]{1,0:T(8,128)}, u32[]{:S(2)}) copy-start(f32[128,256]{1,0:T(8,128)} %refs_1_.3) | copy-start | bytes 393220
  1.6 8.3 %collective-permute-start = (f32[2,48,256]{2,1,0:T(8,128)S(1)}, f32[2,48,256]{2,1,0:T(8,128)S(1)}, u32[]{:S(2)}, u32[]{:S(2)}) collective-permute-start(f32[2,48,256]{2,1,0:T(8,128)S(1)} %pad_maximum_fusion), channel_id=1, source_target_pairs={{0,24},{8,0},{16,8},{24,16},{1,25},{9,1},{17,9},{25,17},{2,26},{10... | collective-permute-start | bytes 294920 | tf_op jit(solution)/shard_map/ppermute | solution.py:589
  6.7 6.5 %collective-permute-start.1 = (f32[2,48,256]{2,1,0:T(8,128)S(1)}, f32[2,48,256]{2,1,0:T(8,128)S(1)}, u32[]{:S(2)}, u32[]{:S(2)}) collective-permute-start(f32[2,48,256]{2,1,0:T(8,128)S(1)} %pad_maximum_fusion.1), channel_id=1, source_target_pairs={{0,8},{8,16},{16,24},{24,0},{1,9},{9,17},{17,25},{25,1},{2,10},{10... | collective-permute-start | bytes 294920 | tf_op jit(solution)/shard_map/ppermute | solution.py:589
  6.8 12.2 %copy-start.3 = (bf16[256,128]{1,0:T(8,128)(2,1)S(1)}, bf16[256,128]{1,0:T(8,128)(2,1)}, u32[]{:S(2)}) copy-start(bf16[256,128]{1,0:T(8,128)(2,1)} %constant.25.clone.refs_8_.refs_10_) | copy-start | bytes 196612
  6.8 12.2 %copy-start.4 = (bf16[384,256]{1,0:T(8,128)(2,1)S(1)}, bf16[384,256]{1,0:T(8,128)(2,1)}, u32[]{:S(2)}) copy-start(bf16[384,256]{1,0:T(8,128)(2,1)} %constant.24.clone.refs_7_) | copy-start | bytes 589828
  6.8 12.2 %copy-start.9 = (bf16[128,128]{1,0:T(8,128)(2,1)S(1)}, bf16[128,128]{1,0:T(8,128)(2,1)}, u32[]{:S(2)}) copy-start(bf16[128,128]{1,0:T(8,128)(2,1)} %constant.26.clone.refs_9_) | copy-start | bytes 98308
  13.8 5.2 %collective-permute-start.2 = (f32[224,128]{1,0:T(8,128)S(1)}, f32[224,128]{1,0:T(8,128)S(1)}, u32[]{:S(2)}, u32[]{:S(2)}) collective-permute-start(f32[224,128]{1,0:T(8,128)S(1)} %get-tuple-element.23), channel_id=1, source_target_pairs={{0,1},{1,2},{2,3},{3,4},{4,5},{5,6},{6,7},{7,0},{8,9},{9,10},{10,1... | collective-permute-start | bytes 344072 | tf_op jit(solution)/shard_map/ppermute | solution.py:589
  13.9 5.1 %collective-permute-start.3 = (f32[224,128]{1,0:T(8,128)S(1)}, f32[224,128]{1,0:T(8,128)S(1)}, u32[]{:S(2)}, u32[]{:S(2)}) collective-permute-start(f32[224,128]{1,0:T(8,128)S(1)} %get-tuple-element.24), channel_id=1, source_target_pairs={{0,7},{1,0},{2,1},{3,2},{4,3},{5,4},{6,5},{7,6},{8,15},{9,8},{10,9... | collective-permute-start | bytes 344072 | tf_op jit(solution)/shard_map/ppermute | solution.py:589
  21.2 15.9 %copy-start.2 = (bf16[512,256]{1,0:T(8,128)(2,1)S(1)}, bf16[512,256]{1,0:T(8,128)(2,1)}, u32[]{:S(2)}) copy-start(bf16[512,256]{1,0:T(8,128)(2,1)} %constant.27.clone.refs_9_) | copy-start | bytes 786436
  21.2 15.9 %copy-start.8 = (bf16[128,128]{1,0:T(8,128)(2,1)S(1)}, bf16[128,128]{1,0:T(8,128)(2,1)}, u32[]{:S(2)}) copy-start(bf16[128,128]{1,0:T(8,128)(2,1)} %constant.28.clone.refs_11_) | copy-start | bytes 98308
  35.6 1.5 %collective-permute-start.4 = (f32[512,128]{1,0:T(8,128)S(1)}, f32[512,128]{1,0:T(8,128)S(1)}, u32[]{:S(2)}, u32[]{:S(2)}) collective-permute-start(f32[512,128]{1,0:T(8,128)S(1)} %bitcast.14), channel_id=1, source_target_pairs={{0,1},{1,0},{2,3},{3,2},{4,5},{5,4},{6,7},{7,6},{8,9},{9,8},{10,11... | collective-permute-start | bytes 786440 | tf_op jit(solution)/shard_map/ppermute | solution.py:600
  37.2 15.5 %copy-start.5 = (bf16[256,384]{1,0:T(8,128)(2,1)S(1)}, bf16[256,384]{1,0:T(8,128)(2,1)}, u32[]{:S(2)}) copy-start(bf16[256,384]{1,0:T(8,128)(2,1)} %constant.31.clone.refs_18_) | copy-start | bytes 589828
  42.4 10.2 %copy-start.6 = (bf16[128,256]{1,0:T(8,128)(2,1)S(1)}, bf16[128,256]{1,0:T(8,128)(2,1)}, u32[]{:S(2)}) copy-start(bf16[128,256]{1,0:T(8,128)(2,1)} %constant.30.clone.refs_17_) | copy-start | bytes 196612
  42.4 10.2 %copy-start.7 = (bf16[256,128]{1,0:T(8,128)(2,1)S(1)}, bf16[256,128]{1,0:T(8,128)(2,1)}, u32[]{:S(2)}) copy-start(bf16[256,128]{1,0:T(8,128)(2,1)} %constant.29.clone.refs_16_) | copy-start | bytes 196612

commit v5 on v4

--- a/solution.py
+++ b/solution.py
@@ -9,7 +9,9 @@
 LEVELS = 4
 COARSE_SWEEPS = 6
 DAMPING = 0.8
-HALO = 48
+HALOS = (40, 16, 8)
+HALO = HALOS[0]
+NEAR = 8
 
 
 def f32dot_right(values, onehot):
@@ -23,16 +25,6 @@
     return (out[2 * rows :] + out[rows : 2 * rows]) + out[:rows]
 
 
-def f32dot_left(onehot, values):
-    high = values.astype(jnp.bfloat16)
-    rest = values - high.astype(jnp.float32)
-    middle = rest.astype(jnp.bfloat16)
-    low = (rest - middle.astype(jnp.float32)).astype(jnp.bfloat16)
-    total = jnp.dot(onehot, low, preferred_element_type=jnp.float32)
-    total = total + jnp.dot(onehot, middle, preferred_element_type=jnp.float32)
-    return total + jnp.dot(onehot, high, preferred_element_type=jnp.float32)
-
-
 def around(v):
     rows, columns = v.shape
     up = pltpu.roll(v, 1, 0)
@@ -56,19 +48,14 @@
         def up(n):
             return -(-n // 128) * 128
 
-        self.ext_rows = [(rows + 2 * HALO) >> l for l in range(3)]
-        self.ext_columns = [up((columns + 2 * HALO) >> l) for l in range(3)]
+        self.ext_rows = [(rows >> l) + 2 * HALOS[l] for l in range(3)]
+        self.ext_columns = [up((columns >> l) + 2 * HALOS[l]) for l in range(3)]
 
     def column_at(self, level):
-        own, halo, width = self.columns >> level, HALO >> level, self.ext_columns[level]
+        own, halo, width = self.columns >> level, HALOS[level], self.ext_columns[level]
         lane = np.arange(width)
         inside = (lane < own + halo) | (lane >= width - halo)
         return np.where(lane < own + halo, lane, lane - width), inside
-
-    def row_at(self, level):
-        own, halo, height = self.rows >> level, HALO >> level, self.ext_rows[level]
-        row = np.arange(height)
-        return np.where(row < own + halo, row, row - height)
 
     def restrict_columns(self, level):
         fine, fine_in = self.column_at(level)
@@ -104,7 +91,7 @@
 
 def inside_mask(sizes, level, gx, gy):
     shape = (sizes.ext_rows[level], sizes.ext_columns[level])
-    own_r, own_c, halo = sizes.rows >> level, sizes.columns >> level, HALO >> level
+    own_r, own_c, halo = sizes.rows >> level, sizes.columns >> level, HALOS[level]
     row, column = iota(shape, 0), iota(shape, 1)
     last_row = jnp.where(gx < sizes.nx - 1, own_r + halo, own_r)
     first_row = jnp.where(gx > 0, own_r + halo, shape[0])
@@ -158,17 +145,29 @@
     repeat(pltpu.roll(block, lax.rem(gy, 8) * sizes.q, 1), out_ref)
 
 
-def strip_kernel(sizes, at_ref, g_ref, s_ref, below_ref, above_ref, left_ref, right_ref):
+def near(values, own):
+    return jnp.concatenate([values[: own + NEAR], values[values.shape[0] - NEAR :]], axis=0)
+
+
+def sides(at, first_ref, second_ref):
+    even = lax.rem(at, 2) == 0
+    first, second = first_ref[...], second_ref[...]
+    return jnp.where(even, first, second), jnp.where(even, second, first)
+
+
+def strip_kernel(sizes, at_ref, g_ref, s_ref, rows_a_ref, rows_b_ref, first_ref, second_ref):
     last = sizes.columns - 128
-    for rows, sources in ((slice(0, sizes.rows), (g_ref, s_ref)),
-                          (slice(sizes.rows, sizes.rows + HALO), (below_ref.at[0], below_ref.at[1])),
-                          (slice(sizes.rows + HALO, sizes.rows + 2 * HALO), (above_ref.at[0], above_ref.at[1]))):
-        g, s = sources
-        first_g, first_s = g[:, :128], s[:, :128]
-        last_g, last_s = g[:, last:], s[:, last:]
-        lane = iota(first_g.shape, 1)
-        left_ref[rows, :] = jnp.where(lane < HALO, first_g, pltpu.roll(first_s, HALO, 1))
-        right_ref[rows, :] = jnp.where(lane >= 128 - HALO, last_g, pltpu.roll(last_s, 128 - HALO, 1))
+    even = lax.rem(at_ref[1], 2) == 0
+    below, above = sides(at_ref[0], rows_a_ref, rows_b_ref)
+    start = 0
+    for g, s in ((g_ref[...], s_ref[...]), (below[0], below[1]), (above[0], above[1])):
+        rows = slice(start, start + g.shape[0])
+        start += g.shape[0]
+        lane = iota((g.shape[0], 128), 1)
+        left = jnp.where(lane < HALO, g[:, :128], pltpu.roll(s[:, :128], HALO, 1))
+        right = jnp.where(lane >= 128 - HALO, g[:, last:], pltpu.roll(s[:, last:], 128 - HALO, 1))
+        first_ref[rows, :] = jnp.where(even, right, left)
+        second_ref[rows, :] = jnp.where(even, left, right)
 
 
 def coefficients(sizes, level, gx, gy, sigma):
@@ -176,27 +175,31 @@
     return d, jnp.where(inside_mask(sizes, level, gx, gy), DAMPING / d, 0.0)
 
 
-def down_kernel(sizes, at_ref, g_ref, s_ref, below_ref, above_ref, left_ref, right_ref, rc0_ref, rc1_ref, pc_ref,
+def down_kernel(sizes, at_ref, g_ref, s_ref, rows_a_ref, rows_b_ref, columns_a_ref, columns_b_ref,
+                rc0_ref, rc1_ref, pc_ref,
                 g0_ref, d0_ref, w0_ref, v0_ref, c1_ref, d1_ref, w1_ref, v1_ref, d2_ref, w2_ref, out_ref, scratch):
     gx, gy = at_ref[0], at_ref[1]
     rows = sizes.ext_rows[0]
     lane = iota((rows, 128), 1)
-    from_left, from_right = left_ref[...], right_ref[...]
+    below, above = sides(gx, rows_a_ref, rows_b_ref)
+    from_right, from_left = sides(gy, columns_a_ref, columns_b_ref)
     g = jnp.where(lane < HALO, from_right, from_left)
     sigma = jnp.where(lane < HALO, pltpu.roll(from_right, 128 - HALO, 1), pltpu.roll(from_left, HALO, 1))
-    g = jnp.concatenate([jnp.concatenate([g_ref[...], below_ref[0], above_ref[0]], axis=0), g], axis=1)
-    sigma = jnp.concatenate([jnp.concatenate([s_ref[...], below_ref[1], above_ref[1]], axis=0), sigma], axis=1)
+    g = jnp.concatenate([jnp.concatenate([g_ref[...], below[0], above[0]], axis=0), g], axis=1)
+    sigma = jnp.concatenate([jnp.concatenate([s_ref[...], below[1], above[1]], axis=0), sigma], axis=1)
     d, w = coefficients(sizes, 0, gx, gy, sigma)
     v = w * g
     v = sweep(v, g, w)
     r = g - d * v + around(v)
-    g0_ref[...] = g
-    d0_ref[...] = d
-    w0_ref[...] = w
-    v0_ref[...] = v
-    half = rows // 2
-    both = jnp.concatenate([pair_rows(scratch, r), pair_rows(scratch, sigma)], axis=0)
-    both = f32dot_right(both, rc0_ref[...])
+    for ref, values in ((g0_ref, g), (d0_ref, d), (w0_ref, w), (v0_ref, v)):
+        ref[...] = near(values, sizes.rows)
+    both = []
+    own, halo = sizes.rows // 2, HALOS[1]
+    for values in (r, sigma):
+        pairs = pair_rows(scratch, values)
+        both += [pairs[: own + halo], pairs[pairs.shape[0] - halo :]]
+    both = f32dot_right(jnp.concatenate(both, axis=0), rc0_ref[...])
+    half = own + 2 * halo
     g, sigma = both[:half], both[half:]
     d, w = coefficients(sizes, 1, gx, gy, sigma)
     v = w * g
@@ -472,7 +475,7 @@
             line = [pltpu.roll(self.v[0][s, r, pl.ds(start, 3 * z.p), :], turn, 1)[:, :128] for r in range(n)]
             parts.append(jnp.concatenate(line, axis=1))
         wide = f32dot_right(jnp.concatenate(parts, axis=0), columns_ref[...])
-        own, halo = z.rows >> above, HALO >> above
+        own, halo = z.rows >> above, HALOS[above]
         inner, outer = (own + halo) // (2 * n), halo // (2 * n)
         tiles = wide.shape[1] // 128
         for t in range(tiles):
@@ -552,12 +555,13 @@
     v = e2_ref[...] + jnp.where(w > 0.0, m.spread(gx, gy, sc_ref, scratch), 0.0)
     for turn in range(2):
         v = sweep(v, g, w)
-    g, w = c1_ref[...], w1_ref[...]
-    v = e1_ref[...] + double_rows(scratch, f32dot_right(v, pc1_ref[...]))
+    own = sizes.rows // 2
+    g, w = near(c1_ref, own), near(w1_ref, own)
+    v = near(e1_ref, own) + near(double_rows(scratch, f32dot_right(v, pc1_ref[...])), own)
     for turn in range(2):
         v = sweep(v, g, w)
     g, d, w = g0_ref[...], d0_ref[...], w0_ref[...]
-    v = v0_ref[...] + double_rows(scratch, f32dot_right(v, pc0_ref[...]))
+    v = v0_ref[...] + near(double_rows(scratch, f32dot_right(v, pc0_ref[...])), sizes.rows)
     for turn in range(2):
         v = sweep(v, g, w)
     r = g - d * v + around(v)
@@ -584,9 +588,19 @@
     )(*operands)
 
 
-def ring(values, axis, step):
+def swaps(first, second, axis, spare):
+    nx, ny = lax.axis_size("gx"), lax.axis_size("gy")
     count = lax.axis_size(axis)
-    return lax.ppermute(values, axis, [(i, (i + step) % count) for i in range(count)])
+
+    def target(gx, gy):
+        place = gx if axis == "gx" else gy
+        if place in (0, count - 1):
+            return (gx ^ 1) * ny + gy if spare == "gx" else gx * ny + (gy ^ 1)
+        place = place + 1 if place % 2 else place - 1
+        return place * ny + gy if axis == "gx" else gx * ny + place
+
+    pairs = [(gx * ny + gy, target(gx, gy)) for gx in range(nx) for gy in range(ny)]
+    return lax.ppermute(first, axis, [(i, i ^ 1) for i in range(count)]), lax.ppermute(second, ("gx", "gy"), pairs)
 
 
 def gather(copies):
@@ -605,18 +619,22 @@
     rows, columns = right_side.shape
     z = Sizes(rows, columns, nx, ny)
     at = jnp.stack([lax.axis_index("gx"), lax.axis_index("gy")]).astype(jnp.int32)
-    below = ring(jnp.stack([right_side[:HALO], shift[:HALO]]), "gx", -1)
-    above = ring(jnp.stack([right_side[rows - HALO :], shift[rows - HALO :]]), "gx", 1)
+    even = lax.axis_index("gx") % 2 == 0
+
+    def strips(start):
+        return jnp.stack([lax.dynamic_slice(x, (start, 0), (HALO, columns)) for x in (right_side, shift)])
+
+    last = rows - HALO
+    rows_a, rows_b = swaps(strips(jnp.where(even, last, 0)), strips(jnp.where(even, 0, last)), "gx", "gy")
     ext = [(z.ext_rows[l], z.ext_columns[l]) for l in range(3)]
     strip = (z.ext_rows[0], 128)
-    to_left, to_right = call(strip_kernel, z, [strip] * 2, [], at, right_side, shift, below, above)
-    right = ring(to_left, "gy", -1)
-    left = ring(to_right, "gy", 1)
+    first, second = call(strip_kernel, z, [strip] * 2, [], at, right_side, shift, rows_a, rows_b)
+    columns_a, columns_b = swaps(first, second, "gy", "gx")
     rc0, rc1 = z.restrict_columns(0), z.restrict_columns(1)
     tiles = (ext[0][1] // 128, ext[0][0], 128)
     g0, d0, w0, v0, c1, d1, w1, v1, d2, w2, packed = call(
-        down_kernel, z, [ext[0]] * 4 + [ext[1]] * 4 + [ext[2]] * 2 + [(nx * ny // 2 * 4 * z.p, 128)], [tiles],
-        at, right_side, shift, below, above, left, right, rc0, rc1, z.pack_pair())
+        down_kernel, z, [(rows + 2 * NEAR, ext[0][1])] * 4 + [ext[1]] * 4 + [ext[2]] * 2 + [(nx * ny // 2 * 4 * z.p, 128)], [tiles],
+        at, right_side, shift, rows_a, rows_b, columns_a, columns_b, rc0, rc1, z.pack_pair())
     y, other = gather_by_core(packed, nx, ny)
     slabs = [level_shape(z, level) for level in (2, 3, 4)]
     d3, d4, w3, w4, e1, c2, e2, packed = call(

time: 56.2 us -> 53 us (0.943)
  waiting for transfers between devices: 10.3 us -> 6.56 us
  blocking collectives: 24.6 us -> 26.8 us
  starting transfers between devices: 7.88 us -> 6.39 us
    ppermute x4, waiting for transfers between devices: 8.79 us -> 5.03 us  [the longest x2 2.68 us: swaps(): lax.ppermute(second, ('gx', 'gy'), pairs)]
    all_to_all x1, blocking collectives: 14.4 us -> 17.1 us  [gather_by_core(): lax.all_to_all(copies, ('gx', 'gy'), 0, 0, tiled=True, axis_index_groups=...]
    ppermute x4, starting transfers between devices: 7.87 us -> 6.38 us  [the longest x2 3.2 us: swaps(): lax.ppermute(second, ('gx', 'gy'), pairs)]
  transfers between devices with their start and end apart: 5 -> 5, of which waited for: 4 -> 3; matrix products, arithmetic and copies ran while one was open for 0% -> 0% of each run, Pallas kernels for 0% -> 0%
where the time goes in v5:
time: 53 us; the launch traced here: 52.8 us
  blocking collectives  26.8 us (51%)
  Pallas kernels  11.2 us (21%)
  waiting for transfers between devices  6.56 us (12%)
  starting transfers between devices  6.39 us (12%)
  local copies, waits for them, and re-layouts  0.91 us (2%)
  between operations  0.75 us (1%)
    all_to_all x1, blocking collectives, gather_by_core(): lax.all_to_all(copies, ('gx', 'gy'), 0, 0, tiled=True, axis_index_groups=...  17.1 us
    pallas_call x4, Pallas kernels, call(): pl.pallas_call(lambda *refs: kernel(sizes, *refs), name=kernel.__name__,...  11.2 us
    all_to_all x1, blocking collectives, gather(): return lax.all_to_all(copies, ('gx', 'gy'), 0, 0, tiled=True)  9.74 us
    ppermute x2, starting transfers between devices, swaps(): lax.ppermute(second, ('gx', 'gy'), pairs)  3.2 us
    ppermute x2, starting transfers between devices, swaps(): lax.ppermute(first, axis, [(i, i ^ 1) for i in range(count)])  3.19 us
    ppermute x2, waiting for transfers between devices, swaps(): lax.ppermute(second, ('gx', 'gy'), pairs)  2.68 us
    ppermute x2, waiting for transfers between devices, swaps(): lax.ppermute(first, axis, [(i, i ^ 1) for i in range(count)])  2.34 us
    ppermute x1, waiting for transfers between devices, gather_by_core(): return (own, lax.ppermute(own, 'gy', [(j, j ^ 1) for j in range(ny)]))  1.53 us
  transfers between devices with their start and end apart: 5, of which 3 were waited for; matrix products, arithmetic and copies ran while one was open for 0% of the time, Pallas kernels for 0%

profile of v5, /device:TPU:0, one launch (start us, length us, event | category | flops | bytes accessed | tf_op | source)
XLA Modules:
  0.0 52.8 jit_solution(1259839773243433384)
XLA Ops:
  0.6 0.9 %dynamic-slice_bitcast_fusion = (f32[1,40,256]{2,1,0:T(8,128)S(1)}, f32[1,40,256]{2,1,0:T(8,128)S(1)}, f32[1,40,256]{2,1,0:T(8,128)S(1)}, f32[1,40,256]{2,1,0:T(8,128)S(1)}) fusion(f32[128,256]{1,0:T(8,128)} %refs_2_.3, s32[]{:T(128)S(6)} %select_n.20, s32[]{:T(128)S(6)} %select_n.19, f32[128,256]{1,0:T(8,128)} %refs_1_.3), kind=kLoop, calls=%fused_computation.2 | loop fusion | bytes 327688 | tf_op jit(solution)/shard_map/stack | solution.py:625
  1.5 0.0 copy-start
  1.5 0.0 copy-start.1
  1.5 3.1 %collective-permute-start = (f32[2,40,256]{2,1,0:T(8,128)S(1)}, f32[2,40,256]{2,1,0:T(8,128)S(1)}, u32[]{:S(2)}, u32[]{:S(2)}) collective-permute-start(f32[2,40,256]{2,1,0:T(8,128)S(1)} %pad_maximum_fusion), channel_id=1, source_target_pairs={{0,8},{8,0},{16,24},{24,16},{1,9},{9,1},{17,25},{25,17},{2,10},{10... | collective-permute-start | bytes 245768 | tf_op jit(solution)/shard_map/ppermute | solution.py:603
  4.7 0.0 collective-permute-start.1
  4.7 0.1 pad_add_fusion.refs_0_
  4.8 2.3 %collective-permute-done.refs_3_ = f32[2,40,256]{2,1,0:T(8,128)S(1)} collective-permute-done((f32[2,40,256]{2,1,0:T(8,128)S(1)}, f32[2,40,256]{2,1,0:T(8,128)S(1)}, u32[]{:S(2)}, u32[]{:S(2)}) %collective-permute-start) | collective-permute-done | bytes 81952 | tf_op jit(solution)/shard_map/ppermute | solution.py:603
  7.1 0.0 collective-permute-done.1.refs_4_
  7.1 0.0 copy-done
  7.1 0.0 copy-done.1
  7.1 0.7 %strip_kernel.1 = (f32[208,128]{1,0:T(8,128)S(1)}, f32[208,128]{1,0:T(8,128)S(1)}) custom-call(s32[2]{0:T(128)S(1)} %pad_add_fusion.refs_0_, f32[128,256]{1,0:T(8,128)S(1)} %copy-done, f32[128,256]{1,0:T(8,128)S(1)} %copy-done.1, f32[2,40,256]{2,1,0:T(8,128)S(1)} %collective-permute-done.refs_3_, f32[2,40,256]{2,1,0:T(8,128)S(1)} %collective-permute-done.1.refs_4_), custom_call_target="tpu_custom_call" | custom-call | tf_op jit(solution)/shard_map/strip_kernel/pallas_call | solution.py:580
  7.8 0.1 collective-permute-start.2
  7.9 3.2 %collective-permute-start.3 = (f32[208,128]{1,0:T(8,128)S(1)}, f32[208,128]{1,0:T(8,128)S(1)}, u32[]{:S(2)}, u32[]{:S(2)}) collective-permute-start(f32[208,128]{1,0:T(8,128)S(1)} %get-tuple-element.24), channel_id=1, source_target_pairs={{0,8},{1,2},{2,1},{3,4},{4,3},{5,6},{6,5},{7,15},{8,0},{9,10},{10,... | collective-permute-start | bytes 319496 | tf_op jit(solution)/shard_map/ppermute | solution.py:603
  11.1 0.0 collective-permute-done.2.refs_5_
  11.1 2.7 %collective-permute-done.3.refs_6_ = f32[208,128]{1,0:T(8,128)S(1)} collective-permute-done((f32[208,128]{1,0:T(8,128)S(1)}, f32[208,128]{1,0:T(8,128)S(1)}, u32[]{:S(2)}, u32[]{:S(2)}) %collective-permute-start.3) | collective-permute-done | bytes 106528 | tf_op jit(solution)/shard_map/ppermute | solution.py:603
  13.7 0.0 copy-done.3
  13.7 0.0 copy-done.5
  13.8 0.0 copy-done.9
  13.8 2.1 %down_kernel.1 = (f32[144,384]{1,0:T(8,128)S(1)}, f32[144,384]{1,0:T(8,128)S(1)}, f32[144,384]{1,0:T(8,128)S(1)}, f32[144,384]{1,0:T(8,128)S(1)}, f32[96,256]{1,...) custom-call(s32[2]{0:T(128)S(1)} %pad_add_fusion.refs_0_, ...), custom_call_target="tpu_custom_call" | custom-call | tf_op jit(solution)/shard_map/down_kernel/pallas_call | solution.py:580
  15.9 0.0 copy-start.2
  15.9 0.0 copy-start.8
  15.9 17.1 %all_to_all.22 = f32[16,32,128]{2,1,0:T(8,128)S(1)} all-to-all(f32[16,32,128]{2,1,0:T(8,128)S(1)} %bitcast.17), channel_id=1, replica_groups={{0,2,4,6,8,10,12,14,16,18,20,22,24,26,28,30},{1,3,5,7,9,11,13,15,17,19,..., dimensions={0} | all-to-all | bytes 524288 | tf_op jit(solution)/shard_map/all_to_all | solution.py:613
  33.0 0.0 collective-permute-start.4
  33.0 1.5 %collective-permute-done.4.refs_2_ = f32[512,128]{1,0:T(8,128)S(1)} collective-permute-done((f32[512,128]{1,0:T(8,128)S(1)}, f32[512,128]{1,0:T(8,128)S(1)}, u32[]{:S(2)}, u32[]{:S(2)}) %collective-permute-start.4) | collective-permute-done | bytes 262176 | tf_op jit(solution)/shard_map/ppermute | solution.py:614
  34.5 0.0 copy-done.2
  34.5 0.0 copy-done.8
  34.5 5.2 %middle_kernel.1 = (f32[2,2,48,128]{3,2,1,0:T(8,128)S(1)}, f32[1,1,48,128]{3,2,1,0:T(8,128)S(1)}, f32[2,2,48,128]{3,2,1,0:T(8,128)S(1)}, f32[1,1,48,128]{3,2,1,0...) custom-call(s32[2]{0:T(128)S(1)} %pad_add_fusion.refs_0_, ...), custom_call_target="tpu_custom_call" | custom-call | tf_op jit(solution)/shard_map/middle_kernel/pallas_call | solution.py:580
  39.8 9.7 %all_to_all.23 = f32[32,4,128]{2,1,0:T(4,128)S(1)} all-to-all(f32[32,4,128]{2,1,0:T(4,128)S(1)} %bitcast.18), channel_id=1, replica_groups=mesh['gx'=4,'gy'=8] {'gx','gy'}, dimensions={0} | all-to-all | bytes 131072 | tf_op jit(solution)/shard_map/all_to_all | solution.py:607
  49.5 0.0 copy-done.4
  49.5 0.0 copy-done.6
  49.5 0.0 copy-done.7
  49.5 3.3 %up_kernel.1 = (f32[128,256]{1,0:T(8,128)}, f32[128,256]{1,0:T(8,128)}) custom-call(s32[2]{0:T(128)S(1)} %pad_add_fusion.refs_0_, f32[128,128]{1,0:T(8,128)S(1)} %bitcast.16, f32[2,2,48,128]{3,2,1,0:T(8,128)S(1)} %get-tuple-element.33.refs_2_, f32[1,1,48,128]{3,2,1,0:T(8,128)S(1)} %get-tuple-element.34.refs_3_, ...), custom_call_target="tpu_custom_call" | custom-call | tf_op jit(solution)/shard_map/up_kernel/pallas_call | solution.py:580
  (8 shorter events, 0.0 us)
Async XLA Ops:
  1.5 5.6 %copy-start = (f32[128,256]{1,0:T(8,128)S(1)}, f32[128,256]{1,0:T(8,128)}, u32[]{:S(2)}) copy-start(f32[128,256]{1,0:T(8,128)} %refs_1_.3) | copy-start | bytes 393220
  1.5 5.6 %copy-start.1 = (f32[128,256]{1,0:T(8,128)S(1)}, f32[128,256]{1,0:T(8,128)}, u32[]{:S(2)}) copy-start(f32[128,256]{1,0:T(8,128)} %refs_2_.3) | copy-start | bytes 393220
  1.5 5.6 %collective-permute-start = (f32[2,40,256]{2,1,0:T(8,128)S(1)}, f32[2,40,256]{2,1,0:T(8,128)S(1)}, u32[]{:S(2)}, u32[]{:S(2)}) collective-permute-start(f32[2,40,256]{2,1,0:T(8,128)S(1)} %pad_maximum_fusion), channel_id=1, source_target_pairs={{0,8},{8,0},{16,24},{24,16},{1,9},{9,1},{17,25},{25,17},{2,10},{10... | collective-permute-start | bytes 245768 | tf_op jit(solution)/shard_map/ppermute | solution.py:603
  4.7 2.4 %collective-permute-start.1 = (f32[2,40,256]{2,1,0:T(8,128)S(1)}, f32[2,40,256]{2,1,0:T(8,128)S(1)}, u32[]{:S(2)}, u32[]{:S(2)}) collective-permute-start(f32[2,40,256]{2,1,0:T(8,128)S(1)} %pad_maximum_fusion.1), channel_id=1, source_target_pairs={{0,1},{1,0},{2,3},{3,2},{4,5},{5,4},{6,7},{7,6},{8,16},{9,17},{10,... | collective-permute-start | bytes 245768 | tf_op jit(solution)/shard_map/ppermute | solution.py:603
  4.8 9.0 %copy-start.3 = (bf16[256,128]{1,0:T(8,128)(2,1)S(1)}, bf16[256,128]{1,0:T(8,128)(2,1)}, u32[]{:S(2)}) copy-start(bf16[256,128]{1,0:T(8,128)(2,1)} %constant.44.clone.refs_8_.refs_10_) | copy-start | bytes 196612
  4.8 9.0 %copy-start.5 = (bf16[384,256]{1,0:T(8,128)(2,1)S(1)}, bf16[384,256]{1,0:T(8,128)(2,1)}, u32[]{:S(2)}) copy-start(bf16[384,256]{1,0:T(8,128)(2,1)} %constant.43.clone.refs_7_) | copy-start | bytes 589828
  4.8 9.0 %copy-start.9 = (bf16[128,128]{1,0:T(8,128)(2,1)S(1)}, bf16[128,128]{1,0:T(8,128)(2,1)}, u32[]{:S(2)}) copy-start(bf16[128,128]{1,0:T(8,128)(2,1)} %constant.45.clone.refs_9_) | copy-start | bytes 98308
  7.8 3.3 %collective-permute-start.2 = (f32[208,128]{1,0:T(8,128)S(1)}, f32[208,128]{1,0:T(8,128)S(1)}, u32[]{:S(2)}, u32[]{:S(2)}) collective-permute-start(f32[208,128]{1,0:T(8,128)S(1)} %get-tuple-element.23), channel_id=1, source_target_pairs={{0,1},{1,0},{2,3},{3,2},{4,5},{5,4},{6,7},{7,6},{8,9},{9,8},{10,11... | collective-permute-start | bytes 319496 | tf_op jit(solution)/shard_map/ppermute | solution.py:603
  7.9 5.9 %collective-permute-start.3 = (f32[208,128]{1,0:T(8,128)S(1)}, f32[208,128]{1,0:T(8,128)S(1)}, u32[]{:S(2)}, u32[]{:S(2)}) collective-permute-start(f32[208,128]{1,0:T(8,128)S(1)} %get-tuple-element.24), channel_id=1, source_target_pairs={{0,8},{1,2},{2,1},{3,4},{4,3},{5,6},{6,5},{7,15},{8,0},{9,10},{10,... | collective-permute-start | bytes 319496 | tf_op jit(solution)/shard_map/ppermute | solution.py:603
  15.9 18.7 %copy-start.2 = (bf16[512,256]{1,0:T(8,128)(2,1)S(1)}, bf16[512,256]{1,0:T(8,128)(2,1)}, u32[]{:S(2)}) copy-start(bf16[512,256]{1,0:T(8,128)(2,1)} %constant.46.clone.refs_9_) | copy-start | bytes 786436
  15.9 18.7 %copy-start.8 = (bf16[128,128]{1,0:T(8,128)(2,1)S(1)}, bf16[128,128]{1,0:T(8,128)(2,1)}, u32[]{:S(2)}) copy-start(bf16[128,128]{1,0:T(8,128)(2,1)} %constant.47.clone.refs_11_) | copy-start | bytes 98308
  33.0 1.5 %collective-permute-start.4 = (f32[512,128]{1,0:T(8,128)S(1)}, f32[512,128]{1,0:T(8,128)S(1)}, u32[]{:S(2)}, u32[]{:S(2)}) collective-permute-start(f32[512,128]{1,0:T(8,128)S(1)} %bitcast.14), channel_id=1, source_target_pairs={{0,1},{1,0},{2,3},{3,2},{4,5},{5,4},{6,7},{7,6},{8,9},{9,8},{10,11... | collective-permute-start | bytes 786440 | tf_op jit(solution)/shard_map/ppermute | solution.py:614
  34.5 15.0 %copy-start.4 = (bf16[256,384]{1,0:T(8,128)(2,1)S(1)}, bf16[256,384]{1,0:T(8,128)(2,1)}, u32[]{:S(2)}) copy-start(bf16[256,384]{1,0:T(8,128)(2,1)} %constant.50.clone.refs_18_) | copy-start | bytes 589828
  39.7 9.8 %copy-start.6 = (bf16[128,256]{1,0:T(8,128)(2,1)S(1)}, bf16[128,256]{1,0:T(8,128)(2,1)}, u32[]{:S(2)}) copy-start(bf16[128,256]{1,0:T(8,128)(2,1)} %constant.49.clone.refs_17_) | copy-start | bytes 196612
  39.8 9.8 %copy-start.7 = (bf16[256,128]{1,0:T(8,128)(2,1)S(1)}, bf16[256,128]{1,0:T(8,128)(2,1)}, u32[]{:S(2)}) copy-start(bf16[256,128]{1,0:T(8,128)(2,1)} %constant.48.clone.refs_16_) | copy-start | bytes 196612

commit v6 on v5

--- a/solution.py
+++ b/solution.py
@@ -155,10 +155,24 @@
     return jnp.where(even, first, second), jnp.where(even, second, first)
 
 
-def strip_kernel(sizes, at_ref, g_ref, s_ref, rows_a_ref, rows_b_ref, first_ref, second_ref):
+def rows_kernel(sizes, g_ref, s_ref, first_ref, second_ref, semaphores):
+    even = lax.rem(lax.axis_index("gx"), 2) == 0
+    last = sizes.rows - HALO
+    copies = []
+    for k, (out, start) in enumerate(((first_ref, jnp.where(even, last, 0)), (second_ref, jnp.where(even, 0, last)))):
+        for f, ref in enumerate((g_ref, s_ref)):
+            rows = pl.ds(pl.multiple_of(start, 8), HALO)
+            copies.append(pltpu.make_async_copy(ref.at[rows, :], out.at[f], semaphores.at[2 * k + f]))
+    for copy in copies:
+        copy.start()
+    for copy in copies:
+        copy.wait()
+
+
+def strip_kernel(sizes, g_ref, s_ref, rows_a_ref, rows_b_ref, first_ref, second_ref):
     last = sizes.columns - 128
-    even = lax.rem(at_ref[1], 2) == 0
-    below, above = sides(at_ref[0], rows_a_ref, rows_b_ref)
+    even = lax.rem(lax.axis_index("gy"), 2) == 0
+    below, above = sides(lax.axis_index("gx"), rows_a_ref, rows_b_ref)
     start = 0
     for g, s in ((g_ref[...], s_ref[...]), (below[0], below[1]), (above[0], above[1])):
         rows = slice(start, start + g.shape[0])
@@ -175,10 +189,10 @@
     return d, jnp.where(inside_mask(sizes, level, gx, gy), DAMPING / d, 0.0)
 
 
-def down_kernel(sizes, at_ref, g_ref, s_ref, rows_a_ref, rows_b_ref, columns_a_ref, columns_b_ref,
+def down_kernel(sizes, g_ref, s_ref, rows_a_ref, rows_b_ref, columns_a_ref, columns_b_ref,
                 rc0_ref, rc1_ref, pc_ref,
                 g0_ref, d0_ref, w0_ref, v0_ref, c1_ref, d1_ref, w1_ref, v1_ref, d2_ref, w2_ref, out_ref, scratch):
-    gx, gy = at_ref[0], at_ref[1]
+    gx, gy = lax.axis_index("gx"), lax.axis_index("gy")
     rows = sizes.ext_rows[0]
     lane = iota((rows, 128), 1)
     below, above = sides(gx, rows_a_ref, rows_b_ref)
@@ -221,10 +235,11 @@
 
 
 class Coarse:
-    def __init__(self, sizes, first, d_refs, w_refs, g_refs, v_refs, t_refs):
+    def __init__(self, sizes, first, d_refs, w_refs, g_refs, v_refs, t_refs, coarsest):
         self.z = sizes
         self.first = first
         self.d, self.w, self.g, self.v, self.t = d_refs, w_refs, g_refs, v_refs, t_refs
+        self.va, self.vb, self.wk, self.gk = coarsest
         lane = iota((sizes.p, sizes.coarse_columns), 1)
         self.first_lane, self.last_lane = lane == 0, lane == sizes.coarse_columns - 1
 
@@ -349,45 +364,53 @@
         top = LEVELS - self.first
         d, w = self.inner(self.d[top]), self.inner(self.w[top])
         missing = 2.0 * (z.coarse_rows + z.coarse_columns)
-        return 1.0 / (jnp.sum(d - 4.0, keepdims=True) + missing), {k: self.shifted(w, k) for k in range(-2, 3)}
+        for k in range(-2, 3):
+            self.wk[k + 2] = self.shifted(w, k)
+        return 1.0 / (jnp.sum(d - 4.0, keepdims=True) + missing)
 
     def coarse(self, fresh, unit):
         top = LEVELS - self.first
-        one, w = unit
+        p, height = self.z.p, self.z.coarse_rows
         g = self.inner(self.g[top])
-        shape = g.shape
-        row, lane = iota(shape, 0), iota(shape, 1)
-        first_row, last_row = row == 0, row == shape[0] - 1
-        sources = {k: self.shifted(g, k) for k in range(-2, 3)}
-
-        def vertical(x):
-            return jnp.where(first_row, 0.0, pltpu.roll(x, 1, 0)) + jnp.where(last_row, 0.0, pltpu.roll(x, shape[0] - 1, 0))
-
-        def three(v):
-            for reach in (2, 1, 0):
-                v = {
-                    k: (1.0 - DAMPING) * v[k] + w[k] * ((sources[k] + vertical(v[k])) + (v[k - 1] + v[k + 1]))
-                    for k in range(-reach, reach + 1)
-                }
-            return v[0]
+        for k in range(-2, 3):
+            self.gk[k + 2] = self.shifted(g, k)
+        lane = iota(g.shape, 1)
+
+        def at(ref, k, step=0):
+            return ref[k + 3, p + step : p + step + height, :]
+
+        def put(ref, k, value):
+            ref[k + 3, p : p + height, :] = value
 
         if fresh:
-            left = jnp.sum(g, keepdims=True) * one
+            left = jnp.broadcast_to(jnp.sum(g, keepdims=True) * unit, g.shape)
             v = {k: 0.0 for k in range(-3, 4)}
         else:
             v = self.inner(self.v[top])
             v = {k: self.shifted(v, k) for k in range(-3, 4)}
-            around_v = vertical(v[0]) + (v[-1] + v[1])
-            left = jnp.sum((g - self.inner(self.d[top]) * v[0]) + around_v, keepdims=True) * one
-        left = jnp.broadcast_to(left, shape)
+            put(self.va, 0, v[0])
+            around_v = (at(self.va, 0, -1) + at(self.va, 0, 1)) + (v[-1] + v[1])
+            left = jnp.sum((g - self.inner(self.d[top]) * v[0]) + around_v, keepdims=True) * unit
+            left = jnp.broadcast_to(left, g.shape)
         for k in range(-3, 4):
-            v[k] = v[k] + jnp.where((lane < shape[1] - k) & (lane >= -k), left, 0.0)
+            inside = (lane < g.shape[1] - k) & (lane >= -k)
+            put(self.va, k, v[k] + jnp.where(inside, left, 0.0) if k else v[k] + left)
         for turn in range(COARSE_SWEEPS // 3):
             if turn:
-                v = {k: self.shifted(v, k) for k in range(-3, 4)}
-            v = three(v)
-        p = self.z.p
-        self.v[top][0, 0, p : p + shape[0], :] = v
+                v = self.inner(self.v[top])
+                for k in range(-3, 4):
+                    put(self.va, k, self.shifted(v, k))
+            source, target = self.va, self.vb
+            for reach in (2, 1, 0):
+                for k in range(-reach, reach + 1):
+                    total = self.gk[k + 2] + (at(source, k, -1) + at(source, k, 1))
+                    total = total + (at(source, k - 1) + at(source, k + 1))
+                    value = (1.0 - DAMPING) * at(source, k) + self.wk[k + 2] * total
+                    if reach:
+                        put(target, k, value)
+                    else:
+                        self.v[top][0, 0, p : p + height, :] = value
+                source, target = target, source
 
     def vcycle(self, level, fresh, unit):
         if level == LEVELS:
@@ -423,6 +446,10 @@
                     for r in range(n):
                         ref[s, r, : z.p, :] = zero
                         ref[s, r, z.p + z.coarse_rows :, :] = zero
+        for ref in (self.va, self.vb):
+            for k in range(7):
+                ref[k, : z.p, :] = zero
+                ref[k, z.p + z.coarse_rows :, :] = zero
 
     def turned(self, blocks, k):
         q = self.z.q
@@ -463,28 +490,23 @@
                     value = jnp.where(low, self.turned(upper, k), self.turned(lower, k + 4))
                     target[k // 2, k % 2, (gx + 1) * z.p : (gx + 2) * z.p, group * 128 : (group + 1) * 128] = value
 
-    def spread(self, gx, gy, columns_ref, scratch):
+    def spread(self, gx, gy, columns_ref, scratch, lines):
         z = self.z
         n = 1 << (LEVELS - self.first)
         above = self.first - 1
         columns = z.coarse_columns
         turn = lax.rem(columns + z.q - gy * z.q, columns)
         start = pl.multiple_of(gx * z.p, 8)
-        parts = []
         for s in range(n):
-            line = [pltpu.roll(self.v[0][s, r, pl.ds(start, 3 * z.p), :], turn, 1)[:, :128] for r in range(n)]
-            parts.append(jnp.concatenate(line, axis=1))
-        wide = f32dot_right(jnp.concatenate(parts, axis=0), columns_ref[...])
-        own, halo = z.rows >> above, HALOS[above]
-        inner, outer = (own + halo) // (2 * n), halo // (2 * n)
-        tiles = wide.shape[1] // 128
-        for t in range(tiles):
-            for s in range(n):
-                part = wide[s * 3 * z.p : (s + 1) * 3 * z.p, t * 128 : (t + 1) * 128]
-                for a in range(2):
-                    scratch[t, pl.ds(2 * s + a, inner, stride=2 * n), :] = part[z.p : z.p + inner]
-                    scratch[t, pl.ds(own + halo + 2 * s + a, outer, stride=2 * n), :] = part[z.p - outer : z.p]
-        return jnp.concatenate([scratch[t, : own + 2 * halo, :] for t in range(tiles)], axis=1)
+            for r in range(n):
+                part = pltpu.roll(self.v[0][s, r, pl.ds(start, 3 * z.p), :], turn, 1)[:, :128]
+                lines[r, pl.ds(s, 3 * z.p, stride=n), :] = part
+        own, halo = z.rows >> self.first, HALOS[above]
+        window = slice(n * z.p - 8, n * z.p + own + 8)
+        wide = f32dot_right(jnp.concatenate([lines[r, window, :] for r in range(n)], axis=1), columns_ref[...])
+        doubled = double_rows(scratch, jnp.concatenate([wide[8:], wide[:8]], axis=0))
+        height = doubled.shape[0]
+        return jnp.concatenate([doubled[: 2 * own + halo], doubled[height - halo :]], axis=0)
 
 
 def level_shape(sizes, level):
@@ -492,12 +514,12 @@
     return (n, n, sizes.coarse_rows + 2 * sizes.p, sizes.coarse_columns)
 
 
-def middle_kernel(sizes, at_ref, y_ref, other_ref, c1_ref, d1_ref, w1_ref, v1_ref, w2l_ref, d2l_ref, sc_ref,
+def middle_kernel(sizes, y_ref, other_ref, c1_ref, d1_ref, w1_ref, v1_ref, w2l_ref, d2l_ref, sc_ref,
                   rc1_ref, pc_ref,
                   d3_ref, d4_ref, w3_ref, w4_ref, e1_ref, c2_ref, e2_ref, out_ref,
-                  d2, w2, g2, g3, g4, v2, v3, v4, t2, t3, t4, scratch):
-    gx, gy = at_ref[0], at_ref[1]
-    m = Coarse(sizes, 2, [d2, d3_ref, d4_ref], [w2, w3_ref, w4_ref], [g2, g3, g4], [v2, v3, v4], [t2, t3, t4])
+                  d2, w2, g2, g3, g4, v2, v3, v4, t2, t3, t4, scratch, lines, *coarsest):
+    gx, gy = lax.axis_index("gx"), lax.axis_index("gy")
+    m = Coarse(sizes, 2, [d2, d3_ref, d4_ref], [w2, w3_ref, w4_ref], [g2, g3, g4], [v2, v3, v4], [t2, t3, t4], coarsest)
     m.clear_ends()
     core = lax.rem(gy, 2)
 
@@ -528,7 +550,7 @@
     m.fcycle(2, unit)
     m.vcycle(2, False, unit)
     g, d, w = c1_ref[...], d1_ref[...], w1_ref[...]
-    v = v1_ref[...] + jnp.where(w > 0.0, m.spread(gx, gy, sc_ref, scratch), 0.0)
+    v = v1_ref[...] + jnp.where(w > 0.0, m.spread(gx, gy, sc_ref, scratch, lines), 0.0)
     for turn in range(4):
         v = sweep(v, g, w)
     e1_ref[...] = v
@@ -543,16 +565,16 @@
     pack_one(sizes, gy, pair_rows(scratch, r[: sizes.rows // 4]), scratch, pc_ref, out_ref)
 
 
-def up_kernel(sizes, at_ref, y_ref, d3_ref, d4_ref, w3_ref, w4_ref, c2_ref, w2_ref, e2_ref, c1_ref, w1_ref, e1_ref,
+def up_kernel(sizes, y_ref, d3_ref, d4_ref, w3_ref, w4_ref, c2_ref, w2_ref, e2_ref, c1_ref, w1_ref, e1_ref,
               g0_ref, d0_ref, w0_ref, v0_ref, sc_ref, pc1_ref, pc0_ref,
-              solution_ref, residual_ref, g3, g4, v3, v4, t3, t4, scratch):
-    gx, gy = at_ref[0], at_ref[1]
-    m = Coarse(sizes, 3, [d3_ref, d4_ref], [w3_ref, w4_ref], [g3, g4], [v3, v4], [t3, t4])
+              solution_ref, residual_ref, g3, g4, v3, v4, t3, t4, scratch, lines, *coarsest):
+    gx, gy = lax.axis_index("gx"), lax.axis_index("gy")
+    m = Coarse(sizes, 3, [d3_ref, d4_ref], [w3_ref, w4_ref], [g3, g4], [v3, v4], [t3, t4], coarsest)
     m.clear_ends()
     m.take_one(y_ref, g3)
     m.vcycle(3, True, m.unit())
     g, w = c2_ref[...], w2_ref[...]
-    v = e2_ref[...] + jnp.where(w > 0.0, m.spread(gx, gy, sc_ref, scratch), 0.0)
+    v = e2_ref[...] + jnp.where(w > 0.0, m.spread(gx, gy, sc_ref, scratch, lines), 0.0)
     for turn in range(2):
         v = sweep(v, g, w)
     own = sizes.rows // 2
@@ -573,7 +595,7 @@
     return [pl.BlockSpec(memory_space=pltpu.VMEM)] * count
 
 
-def call(kernel, sizes, outs, scratch, *operands):
+def call(kernel, sizes, outs, scratch, *operands, inputs=None, semaphores=()):
     shapes = [jax.ShapeDtypeStruct(shape, jnp.float32) for shape in outs]
     used = sum(4 * int(np.prod(shape)) for shape in list(outs) + list(scratch))
     used += sum(x.size * x.dtype.itemsize for x in operands)
@@ -581,9 +603,9 @@
         lambda *refs: kernel(sizes, *refs),
         name=kernel.__name__,
         out_shape=shapes,
-        in_specs=[pl.BlockSpec(memory_space=pltpu.SMEM)] + vmem(len(operands) - 1),
+        in_specs=vmem(len(operands)) if inputs is None else inputs,
         out_specs=vmem(len(outs)),
-        scratch_shapes=[pltpu.VMEM(shape, jnp.float32) for shape in scratch],
+        scratch_shapes=[pltpu.VMEM(shape, jnp.float32) for shape in scratch] + list(semaphores),
         compiler_params=pltpu.CompilerParams(vmem_limit_bytes=used + used // 4 + (4 << 20)),
     )(*operands)
 
@@ -618,34 +640,31 @@
     nx, ny = lax.axis_size("gx"), lax.axis_size("gy")
     rows, columns = right_side.shape
     z = Sizes(rows, columns, nx, ny)
-    at = jnp.stack([lax.axis_index("gx"), lax.axis_index("gy")]).astype(jnp.int32)
-    even = lax.axis_index("gx") % 2 == 0
-
-    def strips(start):
-        return jnp.stack([lax.dynamic_slice(x, (start, 0), (HALO, columns)) for x in (right_side, shift)])
-
-    last = rows - HALO
-    rows_a, rows_b = swaps(strips(jnp.where(even, last, 0)), strips(jnp.where(even, 0, last)), "gx", "gy")
+    first, second = call(
+        rows_kernel, z, [(2, HALO, columns)] * 2, [], right_side, shift,
+        inputs=[pl.BlockSpec(memory_space=pl.ANY)] * 2, semaphores=[pltpu.SemaphoreType.DMA((4,))])
+    rows_a, rows_b = swaps(first, second, "gx", "gy")
     ext = [(z.ext_rows[l], z.ext_columns[l]) for l in range(3)]
     strip = (z.ext_rows[0], 128)
-    first, second = call(strip_kernel, z, [strip] * 2, [], at, right_side, shift, rows_a, rows_b)
+    first, second = call(strip_kernel, z, [strip] * 2, [], right_side, shift, rows_a, rows_b)
     columns_a, columns_b = swaps(first, second, "gy", "gx")
     rc0, rc1 = z.restrict_columns(0), z.restrict_columns(1)
     tiles = (ext[0][1] // 128, ext[0][0], 128)
     g0, d0, w0, v0, c1, d1, w1, v1, d2, w2, packed = call(
         down_kernel, z, [(rows + 2 * NEAR, ext[0][1])] * 4 + [ext[1]] * 4 + [ext[2]] * 2 + [(nx * ny // 2 * 4 * z.p, 128)], [tiles],
-        at, right_side, shift, rows_a, rows_b, columns_a, columns_b, rc0, rc1, z.pack_pair())
+        right_side, shift, rows_a, rows_b, columns_a, columns_b, rc0, rc1, z.pack_pair())
     y, other = gather_by_core(packed, nx, ny)
     slabs = [level_shape(z, level) for level in (2, 3, 4)]
+    coarsest = [(7,) + slabs[2][2:]] * 2 + [(5, z.coarse_rows, z.coarse_columns)] * 2
     d3, d4, w3, w4, e1, c2, e2, packed = call(
         middle_kernel, z, slabs[1:] * 2 + [ext[1], ext[2], ext[2], (nx * ny * 4, 128)],
-        [slabs[0]] * 2 + slabs * 3 + [tiles],
-        at, y, other, c1, d1, w1, v1, w2, d2, z.spread_columns(2),
+        [slabs[0]] * 2 + slabs * 3 + [tiles, (4, 12 * z.p, 128)] + coarsest,
+        y, other, c1, d1, w1, v1, w2, d2, z.spread_columns(2),
         rc1, z.pack_single())
     y = gather(packed)
     return call(
-        up_kernel, z, [(rows, columns)] * 2, slabs[1:] * 3 + [tiles],
-        at, y, d3, d4, w3, w4, c2, w2, e2, c1, w1, e1, g0, d0, w0, v0,
+        up_kernel, z, [(rows, columns)] * 2, slabs[1:] * 3 + [tiles, (2, 6 * z.p, 128)] + coarsest,
+        y, d3, d4, w3, w4, c2, w2, e2, c1, w1, e1, g0, d0, w0, v0,
         z.spread_columns(3), rc1.T, rc0.T)
 
 

time: 53 us -> 51.9 us (0.979)
  Pallas kernels: 11.2 us -> 9.18 us
  local copies, waits for them, and re-layouts: 0.91 us -> 1.84 us
    pallas_call x4 -> x5, Pallas kernels: 11.2 us -> 9.18 us  [call(): pl.pallas_call(lambda *refs: kernel(sizes, *refs), name=kernel.__name__,...]
    unnamed x20 -> x24, local copies, waits for them, and re-layouts: 0.05 us -> 1.84 us
    another operation x1 -> x0, local copies, waits for them, and re-layouts: 0.86 us -> none  [strips(): jnp.stack([lax.dynamic_slice(x, (start, 0), (HALO, columns)) for x in (ri...]
where the time goes in v6:
time: 51.9 us; the launch traced here: 51.6 us
  blocking collectives  26.8 us (52%)
  Pallas kernels  9.18 us (18%)
  waiting for transfers between devices  6.65 us (13%)
  starting transfers between devices  6.39 us (12%)
  local copies, waits for them, and re-layouts  1.84 us (4%)
  between operations  0.71 us (1%)
    all_to_all x1, blocking collectives, gather_by_core(): lax.all_to_all(copies, ('gx', 'gy'), 0, 0, tiled=True, axis_index_groups=...  17.1 us
    all_to_all x1, blocking collectives, gather(): return lax.all_to_all(copies, ('gx', 'gy'), 0, 0, tiled=True)  9.75 us
    pallas_call x5, Pallas kernels, call(): pl.pallas_call(lambda *refs: kernel(sizes, *refs), name=kernel.__name__,...  9.18 us
    ppermute x2, starting transfers between devices, swaps(): lax.ppermute(second, ('gx', 'gy'), pairs)  3.19 us
    ppermute x2, starting transfers between devices, swaps(): lax.ppermute(first, axis, [(i, i ^ 1) for i in range(count)])  3.19 us
    ppermute x2, waiting for transfers between devices, swaps(): lax.ppermute(second, ('gx', 'gy'), pairs)  2.68 us
    ppermute x2, waiting for transfers between devices, swaps(): lax.ppermute(first, axis, [(i, i ^ 1) for i in range(count)])  2.43 us
    unnamed x24, local copies, waits for them, and re-layouts  1.84 us
  transfers between devices with their start and end apart: 5, of which 3 were waited for; matrix products, arithmetic and copies ran while one was open for 0% of the time, Pallas kernels for 0%

profile of v6, /device:TPU:0, one launch (start us, length us, event | category | flops | bytes accessed | tf_op | source)
XLA Modules:
  0.0 51.6 jit_solution(9738174392743011207)
XLA Ops:
  0.6 0.0 copy-start
  0.6 0.9 %copy-done = f32[128,256]{1,0:T(8,128)S(1)} copy-done((f32[128,256]{1,0:T(8,128)S(1)}, f32[128,256]{1,0:T(8,128)}, u32[]{:S(2)}) %copy-start) | copy-done | bytes 131096
  1.5 0.9 %copy-done.2 = f32[128,256]{1,0:T(8,128)S(1)} copy-done((f32[128,256]{1,0:T(8,128)S(1)}, f32[128,256]{1,0:T(8,128)}, u32[]{:S(2)}) %copy-start.2) | copy-done | bytes 131096
  2.4 0.2 rows_kernel.1
  2.7 3.1 %collective-permute-start = (f32[2,40,256]{2,1,0:T(8,128)S(1)}, f32[2,40,256]{2,1,0:T(8,128)S(1)}, u32[]{:S(2)}, u32[]{:S(2)}) collective-permute-start(f32[2,40,256]{2,1,0:T(8,128)S(1)} %get-tuple-element.25), channel_id=1, source_target_pairs={{0,8},{8,0},{16,24},{24,16},{1,9},{9,1},{17,25},{25,17},{2,10},{10... | collective-permute-start | bytes 245768 | tf_op jit(solution)/shard_map/ppermute | solution.py:625
  5.8 0.0 collective-permute-start.1
  5.8 2.4 %collective-permute-done.refs_2_ = f32[2,40,256]{2,1,0:T(8,128)S(1)} collective-permute-done((f32[2,40,256]{2,1,0:T(8,128)S(1)}, f32[2,40,256]{2,1,0:T(8,128)S(1)}, u32[]{:S(2)}, u32[]{:S(2)}) %collective-permute-start) | collective-permute-done | bytes 81952 | tf_op jit(solution)/shard_map/ppermute | solution.py:625
  8.2 0.0 collective-permute-done.1.refs_3_
  8.3 0.0 copy-done.1
  8.3 0.0 copy-done.3
  8.3 0.1 strip_kernel.1
  8.4 0.1 collective-permute-start.2
  8.5 3.2 %collective-permute-start.3 = (f32[208,128]{1,0:T(8,128)S(1)}, f32[208,128]{1,0:T(8,128)S(1)}, u32[]{:S(2)}, u32[]{:S(2)}) collective-permute-start(f32[208,128]{1,0:T(8,128)S(1)} %get-tuple-element.28), channel_id=1, source_target_pairs={{0,8},{1,2},{2,1},{3,4},{4,3},{5,6},{6,5},{7,15},{8,0},{9,10},{10,... | collective-permute-start | bytes 319496 | tf_op jit(solution)/shard_map/ppermute | solution.py:625
  11.7 0.0 collective-permute-done.2.refs_4_
  11.7 2.7 %collective-permute-done.3.refs_5_ = f32[208,128]{1,0:T(8,128)S(1)} collective-permute-done((f32[208,128]{1,0:T(8,128)S(1)}, f32[208,128]{1,0:T(8,128)S(1)}, u32[]{:S(2)}, u32[]{:S(2)}) %collective-permute-start.3) | collective-permute-done | bytes 106528 | tf_op jit(solution)/shard_map/ppermute | solution.py:625
  14.3 0.0 copy-done.4
  14.3 0.0 copy-done.6
  14.3 0.0 copy-done.10
  14.4 1.5 %down_kernel.1 = (f32[144,384]{1,0:T(8,128)S(1)}, f32[144,384]{1,0:T(8,128)S(1)}, f32[144,384]{1,0:T(8,128)S(1)}, f32[144,384]{1,0:T(8,128)S(1)}, f32[96,256]{1,...) custom-call(f32[128,256]{1,0:T(8,128)S(1)} %copy-done.1, ...), custom_call_target="tpu_custom_call" | custom-call | tf_op jit(solution)/shard_map/down_kernel/pallas_call | solution.py:602
  15.9 0.0 copy-start.5
  15.9 0.0 copy-start.11
  15.9 17.1 %all_to_all.22 = f32[16,32,128]{2,1,0:T(8,128)S(1)} all-to-all(f32[16,32,128]{2,1,0:T(8,128)S(1)} %bitcast.6), channel_id=1, replica_groups={{0,2,4,6,8,10,12,14,16,18,20,22,24,26,28,30},{1,3,5,7,9,11,13,15,17,19,..., dimensions={0} | all-to-all | bytes 524288 | tf_op jit(solution)/shard_map/all_to_all | solution.py:635
  33.0 0.0 collective-permute-start.4
  33.0 1.5 %collective-permute-done.4.refs_1_ = f32[512,128]{1,0:T(8,128)S(1)} collective-permute-done((f32[512,128]{1,0:T(8,128)S(1)}, f32[512,128]{1,0:T(8,128)S(1)}, u32[]{:S(2)}, u32[]{:S(2)}) %collective-permute-start.4) | collective-permute-done | bytes 262176 | tf_op jit(solution)/shard_map/ppermute | solution.py:636
  34.6 0.0 copy-done.5
  34.6 0.0 copy-done.11
  34.6 4.6 %middle_kernel.1 = (f32[2,2,48,128]{3,2,1,0:T(8,128)S(1)}, f32[1,1,48,128]{3,2,1,0:T(8,128)S(1)}, f32[2,2,48,128]{3,2,1,0:T(8,128)S(1)}, f32[1,1,48,128]{3,2,1,0...) custom-call(f32[512,128]{1,0:T(8,128)S(1)} %bitcast.5, ...), custom_call_target="tpu_custom_call" | custom-call | tf_op jit(solution)/shard_map/middle_kernel/pallas_call | solution.py:602
  39.2 9.7 %all_to_all.23 = f32[32,4,128]{2,1,0:T(4,128)S(1)} all-to-all(f32[32,4,128]{2,1,0:T(4,128)S(1)} %bitcast.8), channel_id=1, replica_groups=mesh['gx'=4,'gy'=8] {'gx','gy'}, dimensions={0} | all-to-all | bytes 131072 | tf_op jit(solution)/shard_map/all_to_all | solution.py:629
  48.9 0.0 copy-done.7
  48.9 0.0 copy-done.8
  48.9 0.0 copy-done.9
  48.9 2.7 %up_kernel.1 = (f32[128,256]{1,0:T(8,128)}, f32[128,256]{1,0:T(8,128)}) custom-call(f32[128,128]{1,0:T(8,128)S(1)} %bitcast.7, f32[2,2,48,128]{3,2,1,0:T(8,128)S(1)} %get-tuple-element.37.refs_1_, f32[1,1,48,128]{3,2,1,0:T(8,128)S(1)} %get-tuple-element.38.refs_2_, f32[2,2,48,128]{3,2,1,0:T(8,128)S(1)} %get-tuple-element.39.refs_3_, ...), custom_call_target="tpu_custom_call" | custom-call | tf_op jit(solution)/shard_map/up_kernel/pallas_call | solution.py:602
  (9 shorter events, 0.0 us)
Async XLA Ops:
  0.6 0.9 %copy-start = (f32[128,256]{1,0:T(8,128)S(1)}, f32[128,256]{1,0:T(8,128)}, u32[]{:S(2)}) copy-start(f32[128,256]{1,0:T(8,128)} %refs_0_.5) | copy-start | bytes 393220
  1.5 0.9 %copy-start.2 = (f32[128,256]{1,0:T(8,128)S(1)}, f32[128,256]{1,0:T(8,128)}, u32[]{:S(2)}) copy-start(f32[128,256]{1,0:T(8,128)} %refs_1_.5) | copy-start | bytes 393220
  2.4 5.8 %copy-start.1 = (f32[128,256]{1,0:T(8,128)S(1)}, f32[128,256]{1,0:T(8,128)}, u32[]{:S(2)}) copy-start(f32[128,256]{1,0:T(8,128)} %refs_0_.5) | copy-start | bytes 393220
  2.4 5.8 %copy-start.3 = (f32[128,256]{1,0:T(8,128)S(1)}, f32[128,256]{1,0:T(8,128)}, u32[]{:S(2)}) copy-start(f32[128,256]{1,0:T(8,128)} %refs_1_.5) | copy-start | bytes 393220
  2.7 5.6 %collective-permute-start = (f32[2,40,256]{2,1,0:T(8,128)S(1)}, f32[2,40,256]{2,1,0:T(8,128)S(1)}, u32[]{:S(2)}, u32[]{:S(2)}) collective-permute-start(f32[2,40,256]{2,1,0:T(8,128)S(1)} %get-tuple-element.25), channel_id=1, source_target_pairs={{0,8},{8,0},{16,24},{24,16},{1,9},{9,1},{17,25},{25,17},{2,10},{10... | collective-permute-start | bytes 245768 | tf_op jit(solution)/shard_map/ppermute | solution.py:625
  5.8 8.5 %copy-start.4 = (bf16[256,128]{1,0:T(8,128)(2,1)S(1)}, bf16[256,128]{1,0:T(8,128)(2,1)}, u32[]{:S(2)}) copy-start(bf16[256,128]{1,0:T(8,128)(2,1)} %constant.17.clone.refs_7_.refs_9_) | copy-start | bytes 196612
  5.8 8.5 %copy-start.6 = (bf16[384,256]{1,0:T(8,128)(2,1)S(1)}, bf16[384,256]{1,0:T(8,128)(2,1)}, u32[]{:S(2)}) copy-start(bf16[384,256]{1,0:T(8,128)(2,1)} %constant.16.clone.refs_6_) | copy-start | bytes 589828
  5.8 8.5 %copy-start.10 = (bf16[128,128]{1,0:T(8,128)(2,1)S(1)}, bf16[128,128]{1,0:T(8,128)(2,1)}, u32[]{:S(2)}) copy-start(bf16[128,128]{1,0:T(8,128)(2,1)} %constant.18.clone.refs_8_) | copy-start | bytes 98308
  5.8 2.4 %collective-permute-start.1 = (f32[2,40,256]{2,1,0:T(8,128)S(1)}, f32[2,40,256]{2,1,0:T(8,128)S(1)}, u32[]{:S(2)}, u32[]{:S(2)}) collective-permute-start(f32[2,40,256]{2,1,0:T(8,128)S(1)} %get-tuple-element.26), channel_id=1, source_target_pairs={{0,1},{1,0},{2,3},{3,2},{4,5},{5,4},{6,7},{7,6},{8,16},{9,17},{10,... | collective-permute-start | bytes 245768 | tf_op jit(solution)/shard_map/ppermute | solution.py:625
  8.4 3.3 %collective-permute-start.2 = (f32[208,128]{1,0:T(8,128)S(1)}, f32[208,128]{1,0:T(8,128)S(1)}, u32[]{:S(2)}, u32[]{:S(2)}) collective-permute-start(f32[208,128]{1,0:T(8,128)S(1)} %get-tuple-element.27), channel_id=1, source_target_pairs={{0,1},{1,0},{2,3},{3,2},{4,5},{5,4},{6,7},{7,6},{8,9},{9,8},{10,11... | collective-permute-start | bytes 319496 | tf_op jit(solution)/shard_map/ppermute | solution.py:625
  8.5 5.9 %collective-permute-start.3 = (f32[208,128]{1,0:T(8,128)S(1)}, f32[208,128]{1,0:T(8,128)S(1)}, u32[]{:S(2)}, u32[]{:S(2)}) collective-permute-start(f32[208,128]{1,0:T(8,128)S(1)} %get-tuple-element.28), channel_id=1, source_target_pairs={{0,8},{1,2},{2,1},{3,4},{4,3},{5,6},{6,5},{7,15},{8,0},{9,10},{10,... | collective-permute-start | bytes 319496 | tf_op jit(solution)/shard_map/ppermute | solution.py:625
  15.9 18.7 %copy-start.5 = (bf16[512,256]{1,0:T(8,128)(2,1)S(1)}, bf16[512,256]{1,0:T(8,128)(2,1)}, u32[]{:S(2)}) copy-start(bf16[512,256]{1,0:T(8,128)(2,1)} %constant.19.clone.refs_8_) | copy-start | bytes 786436
  15.9 18.7 %copy-start.11 = (bf16[128,128]{1,0:T(8,128)(2,1)S(1)}, bf16[128,128]{1,0:T(8,128)(2,1)}, u32[]{:S(2)}) copy-start(bf16[128,128]{1,0:T(8,128)(2,1)} %constant.20.clone.refs_10_) | copy-start | bytes 98308
  33.0 1.5 %collective-permute-start.4 = (f32[512,128]{1,0:T(8,128)S(1)}, f32[512,128]{1,0:T(8,128)S(1)}, u32[]{:S(2)}, u32[]{:S(2)}) collective-permute-start(f32[512,128]{1,0:T(8,128)S(1)} %bitcast.4), channel_id=1, source_target_pairs={{0,1},{1,0},{2,3},{3,2},{4,5},{5,4},{6,7},{7,6},{8,9},{9,8},{10,11... | collective-permute-start | bytes 786440 | tf_op jit(solution)/shard_map/ppermute | solution.py:636
  34.6 14.3 %copy-start.7 = (bf16[256,384]{1,0:T(8,128)(2,1)S(1)}, bf16[256,384]{1,0:T(8,128)(2,1)}, u32[]{:S(2)}) copy-start(bf16[256,384]{1,0:T(8,128)(2,1)} %constant.23.clone.refs_17_) | copy-start | bytes 589828
  39.2 9.8 %copy-start.8 = (bf16[128,256]{1,0:T(8,128)(2,1)S(1)}, bf16[128,256]{1,0:T(8,128)(2,1)}, u32[]{:S(2)}) copy-start(bf16[128,256]{1,0:T(8,128)(2,1)} %constant.22.clone.refs_16_) | copy-start | bytes 196612
  39.2 9.8 %copy-start.9 = (bf16[256,128]{1,0:T(8,128)(2,1)S(1)}, bf16[256,128]{1,0:T(8,128)(2,1)}, u32[]{:S(2)}) copy-start(bf16[256,128]{1,0:T(8,128)(2,1)} %constant.21.clone.refs_15_) | copy-start | bytes 196612

commit v7 on v6

--- a/solution.py
+++ b/solution.py
@@ -169,19 +169,42 @@
         copy.wait()
 
 
+def strip_rows(sizes):
+    groups = 128 // HALO
+    return groups, -(-2 * sizes.ext_rows[0] // (8 * groups)) * 8
+
+
+def fold(sizes, strip, step):
+    groups, height = strip_rows(sizes)
+    lane = iota((height, 128), 1)
+    lane = lane if step > 0 else 127 - lane
+    out = strip[:height]
+    for k in range(1, groups):
+        part = strip[k * height : (k + 1) * height]
+        part = pltpu.roll(part, k * step % 128, 1)
+        if part.shape[0] < height:
+            part = jnp.concatenate([part, jnp.zeros((height - part.shape[0], 128), jnp.float32)], axis=0)
+        out = jnp.where(lane >= k * HALO, part, out)
+    return out
+
+
+def unfold(sizes, packed, step):
+    groups, _ = strip_rows(sizes)
+    parts = [packed] + [pltpu.roll(packed, -k * step % 128, 1) for k in range(1, groups)]
+    rows = sizes.ext_rows[0]
+    out = jnp.concatenate(parts, axis=0)
+    return out[:rows], out[rows : 2 * rows]
+
+
 def strip_kernel(sizes, g_ref, s_ref, rows_a_ref, rows_b_ref, first_ref, second_ref):
     last = sizes.columns - 128
     even = lax.rem(lax.axis_index("gy"), 2) == 0
     below, above = sides(lax.axis_index("gx"), rows_a_ref, rows_b_ref)
-    start = 0
-    for g, s in ((g_ref[...], s_ref[...]), (below[0], below[1]), (above[0], above[1])):
-        rows = slice(start, start + g.shape[0])
-        start += g.shape[0]
-        lane = iota((g.shape[0], 128), 1)
-        left = jnp.where(lane < HALO, g[:, :128], pltpu.roll(s[:, :128], HALO, 1))
-        right = jnp.where(lane >= 128 - HALO, g[:, last:], pltpu.roll(s[:, last:], 128 - HALO, 1))
-        first_ref[rows, :] = jnp.where(even, right, left)
-        second_ref[rows, :] = jnp.where(even, left, right)
+    fields = (g_ref[...], below[0], above[0], s_ref[...], below[1], above[1])
+    left = fold(sizes, jnp.concatenate([x[:, :128] for x in fields], axis=0), HALO)
+    right = fold(sizes, jnp.concatenate([x[:, last:] for x in fields], axis=0), -HALO)
+    first_ref[...] = jnp.where(even, right, left)
+    second_ref[...] = jnp.where(even, left, right)
 
 
 def coefficients(sizes, level, gx, gy, sigma):
@@ -197,8 +220,9 @@
     lane = iota((rows, 128), 1)
     below, above = sides(gx, rows_a_ref, rows_b_ref)
     from_right, from_left = sides(gy, columns_a_ref, columns_b_ref)
-    g = jnp.where(lane < HALO, from_right, from_left)
-    sigma = jnp.where(lane < HALO, pltpu.roll(from_right, 128 - HALO, 1), pltpu.roll(from_left, HALO, 1))
+    from_right, from_left = unfold(sizes, from_right, HALO), unfold(sizes, from_left, -HALO)
+    g = jnp.where(lane < HALO, from_right[0], from_left[0])
+    sigma = jnp.where(lane < HALO, from_right[1], from_left[1])
     g = jnp.concatenate([jnp.concatenate([g_ref[...], below[0], above[0]], axis=0), g], axis=1)
     sigma = jnp.concatenate([jnp.concatenate([s_ref[...], below[1], above[1]], axis=0), sigma], axis=1)
     d, w = coefficients(sizes, 0, gx, gy, sigma)
@@ -642,10 +666,10 @@
     z = Sizes(rows, columns, nx, ny)
     first, second = call(
         rows_kernel, z, [(2, HALO, columns)] * 2, [], right_side, shift,
-        inputs=[pl.BlockSpec(memory_space=pl.ANY)] * 2, semaphores=[pltpu.SemaphoreType.DMA((4,))])
+        inputs=[pl.BlockSpec(memory_space=pltpu.HBM)] * 2, semaphores=[pltpu.SemaphoreType.DMA((4,))])
     rows_a, rows_b = swaps(first, second, "gx", "gy")
     ext = [(z.ext_rows[l], z.ext_columns[l]) for l in range(3)]
-    strip = (z.ext_rows[0], 128)
+    strip = (strip_rows(z)[1], 128)
     first, second = call(strip_kernel, z, [strip] * 2, [], right_side, shift, rows_a, rows_b)
     columns_a, columns_b = swaps(first, second, "gy", "gx")
     rc0, rc1 = z.restrict_columns(0), z.restrict_columns(1)

time: 51.9 us -> 51.2 us (0.987)
  no operation moved by 1% of the time
where the time goes in v7:
time: 51.2 us; the launch traced here: 50.9 us
  blocking collectives  26.5 us (52%)
  Pallas kernels  9.2 us (18%)
  starting transfers between devices  6.38 us (12%)
  waiting for transfers between devices  6.3 us (12%)
  local copies, waits for them, and re-layouts  1.84 us (4%)
  between operations  0.72 us (1%)
    all_to_all x1, blocking collectives, gather_by_core(): lax.all_to_all(copies, ('gx', 'gy'), 0, 0, tiled=True, axis_index_groups=...  16.7 us
    all_to_all x1, blocking collectives, gather(): return lax.all_to_all(copies, ('gx', 'gy'), 0, 0, tiled=True)  9.75 us
    pallas_call x5, Pallas kernels, call(): pl.pallas_call(lambda *refs: kernel(sizes, *refs), name=kernel.__name__,...  9.2 us
    ppermute x2, starting transfers between devices, swaps(): lax.ppermute(second, ('gx', 'gy'), pairs)  3.19 us
    ppermute x2, starting transfers between devices, swaps(): lax.ppermute(first, axis, [(i, i ^ 1) for i in range(count)])  3.19 us
    ppermute x2, waiting for transfers between devices, swaps(): lax.ppermute(first, axis, [(i, i ^ 1) for i in range(count)])  2.43 us
    ppermute x2, waiting for transfers between devices, swaps(): lax.ppermute(second, ('gx', 'gy'), pairs)  2.33 us
    unnamed x24, local copies, waits for them, and re-layouts  1.84 us
  transfers between devices with their start and end apart: 5, of which 3 were waited for; matrix products, arithmetic and copies ran while one was open for 0% of the time, Pallas kernels for 0%

profile of v7, /device:TPU:0, one launch (start us, length us, event | category | flops | bytes accessed | tf_op | source)
XLA Modules:
  0.0 50.9 jit_solution(4474655980062476009)
XLA Ops:
  0.6 0.0 copy-start
  0.6 0.9 %copy-done = f32[128,256]{1,0:T(8,128)S(1)} copy-done((f32[128,256]{1,0:T(8,128)S(1)}, f32[128,256]{1,0:T(8,128)}, u32[]{:S(2)}) %copy-start) | copy-done | bytes 131096
  1.5 0.9 %copy-done.2 = f32[128,256]{1,0:T(8,128)S(1)} copy-done((f32[128,256]{1,0:T(8,128)S(1)}, f32[128,256]{1,0:T(8,128)}, u32[]{:S(2)}) %copy-start.2) | copy-done | bytes 131096
  2.4 0.2 rows_kernel.1
  2.7 3.1 %collective-permute-start = (f32[2,40,256]{2,1,0:T(8,128)S(1)}, f32[2,40,256]{2,1,0:T(8,128)S(1)}, u32[]{:S(2)}, u32[]{:S(2)}) collective-permute-start(f32[2,40,256]{2,1,0:T(8,128)S(1)} %get-tuple-element.25), channel_id=1, source_target_pairs={{0,8},{8,0},{16,24},{24,16},{1,9},{9,1},{17,25},{25,17},{2,10},{10... | collective-permute-start | bytes 245768 | tf_op jit(solution)/shard_map/ppermute | solution.py:649
  5.8 0.0 collective-permute-start.1
  5.8 2.4 %collective-permute-done.refs_2_ = f32[2,40,256]{2,1,0:T(8,128)S(1)} collective-permute-done((f32[2,40,256]{2,1,0:T(8,128)S(1)}, f32[2,40,256]{2,1,0:T(8,128)S(1)}, u32[]{:S(2)}, u32[]{:S(2)}) %collective-permute-start) | collective-permute-done | bytes 81952 | tf_op jit(solution)/shard_map/ppermute | solution.py:649
  8.2 0.0 collective-permute-done.1.refs_3_
  8.3 0.0 copy-done.1
  8.3 0.0 copy-done.3
  8.3 0.1 strip_kernel.1
  8.4 0.1 collective-permute-start.2
  8.5 3.2 %collective-permute-start.3 = (f32[144,128]{1,0:T(8,128)S(1)}, f32[144,128]{1,0:T(8,128)S(1)}, u32[]{:S(2)}, u32[]{:S(2)}) collective-permute-start(f32[144,128]{1,0:T(8,128)S(1)} %get-tuple-element.28), channel_id=1, source_target_pairs={{0,8},{1,2},{2,1},{3,4},{4,3},{5,6},{6,5},{7,15},{8,0},{9,10},{10,... | collective-permute-start | bytes 221192 | tf_op jit(solution)/shard_map/ppermute | solution.py:649
  11.7 0.0 collective-permute-done.2.refs_4_
  11.7 2.3 %collective-permute-done.3.refs_5_ = f32[144,128]{1,0:T(8,128)S(1)} collective-permute-done((f32[144,128]{1,0:T(8,128)S(1)}, f32[144,128]{1,0:T(8,128)S(1)}, u32[]{:S(2)}, u32[]{:S(2)}) %collective-permute-start.3) | collective-permute-done | bytes 73760 | tf_op jit(solution)/shard_map/ppermute | solution.py:649
  14.0 0.0 copy-done.5
  14.0 0.0 copy-done.6
  14.0 0.0 copy-done.10
  14.0 1.6 %down_kernel.1 = (f32[144,384]{1,0:T(8,128)S(1)}, f32[144,384]{1,0:T(8,128)S(1)}, f32[144,384]{1,0:T(8,128)S(1)}, f32[144,384]{1,0:T(8,128)S(1)}, f32[96,256]{1,...) custom-call(f32[128,256]{1,0:T(8,128)S(1)} %copy-done.1, ...), custom_call_target="tpu_custom_call" | custom-call | tf_op jit(solution)/shard_map/down_kernel/pallas_call | solution.py:626
  15.6 0.0 copy-start.4
  15.6 0.0 copy-start.11
  15.6 16.7 %all_to_all.22 = f32[16,32,128]{2,1,0:T(8,128)S(1)} all-to-all(f32[16,32,128]{2,1,0:T(8,128)S(1)} %bitcast.6), channel_id=1, replica_groups={{0,2,4,6,8,10,12,14,16,18,20,22,24,26,28,30},{1,3,5,7,9,11,13,15,17,19,..., dimensions={0} | all-to-all | bytes 524288 | tf_op jit(solution)/shard_map/all_to_all | solution.py:659
  32.4 0.0 collective-permute-start.4
  32.4 1.5 %collective-permute-done.4.refs_1_ = f32[512,128]{1,0:T(8,128)S(1)} collective-permute-done((f32[512,128]{1,0:T(8,128)S(1)}, f32[512,128]{1,0:T(8,128)S(1)}, u32[]{:S(2)}, u32[]{:S(2)}) %collective-permute-start.4) | collective-permute-done | bytes 262176 | tf_op jit(solution)/shard_map/ppermute | solution.py:660
  33.9 0.0 copy-done.4
  33.9 0.0 copy-done.11
  33.9 4.6 %middle_kernel.1 = (f32[2,2,48,128]{3,2,1,0:T(8,128)S(1)}, f32[1,1,48,128]{3,2,1,0:T(8,128)S(1)}, f32[2,2,48,128]{3,2,1,0:T(8,128)S(1)}, f32[1,1,48,128]{3,2,1,0...) custom-call(f32[512,128]{1,0:T(8,128)S(1)} %bitcast.5, ...), custom_call_target="tpu_custom_call" | custom-call | tf_op jit(solution)/shard_map/middle_kernel/pallas_call | solution.py:626
  38.5 9.7 %all_to_all.23 = f32[32,4,128]{2,1,0:T(4,128)S(1)} all-to-all(f32[32,4,128]{2,1,0:T(4,128)S(1)} %bitcast.8), channel_id=1, replica_groups=mesh['gx'=4,'gy'=8] {'gx','gy'}, dimensions={0} | all-to-all | bytes 131072 | tf_op jit(solution)/shard_map/all_to_all | solution.py:653
  48.2 0.0 copy-done.7
  48.2 0.0 copy-done.8
  48.2 0.0 copy-done.9
  48.2 2.7 %up_kernel.1 = (f32[128,256]{1,0:T(8,128)}, f32[128,256]{1,0:T(8,128)}) custom-call(f32[128,128]{1,0:T(8,128)S(1)} %bitcast.7, f32[2,2,48,128]{3,2,1,0:T(8,128)S(1)} %get-tuple-element.37.refs_1_, f32[1,1,48,128]{3,2,1,0:T(8,128)S(1)} %get-tuple-element.38.refs_2_, f32[2,2,48,128]{3,2,1,0:T(8,128)S(1)} %get-tuple-element.39.refs_3_, ...), custom_call_target="tpu_custom_call" | custom-call | tf_op jit(solution)/shard_map/up_kernel/pallas_call | solution.py:626
  (9 shorter events, 0.0 us)
Async XLA Ops:
  0.6 0.9 %copy-start = (f32[128,256]{1,0:T(8,128)S(1)}, f32[128,256]{1,0:T(8,128)}, u32[]{:S(2)}) copy-start(f32[128,256]{1,0:T(8,128)} %refs_0_.5) | copy-start | bytes 393220
  1.5 0.9 %copy-start.2 = (f32[128,256]{1,0:T(8,128)S(1)}, f32[128,256]{1,0:T(8,128)}, u32[]{:S(2)}) copy-start(f32[128,256]{1,0:T(8,128)} %refs_1_.5) | copy-start | bytes 393220
  2.4 5.8 %copy-start.1 = (f32[128,256]{1,0:T(8,128)S(1)}, f32[128,256]{1,0:T(8,128)}, u32[]{:S(2)}) copy-start(f32[128,256]{1,0:T(8,128)} %refs_0_.5) | copy-start | bytes 393220
  2.4 5.8 %copy-start.3 = (f32[128,256]{1,0:T(8,128)S(1)}, f32[128,256]{1,0:T(8,128)}, u32[]{:S(2)}) copy-start(f32[128,256]{1,0:T(8,128)} %refs_1_.5) | copy-start | bytes 393220
  2.7 5.6 %collective-permute-start = (f32[2,40,256]{2,1,0:T(8,128)S(1)}, f32[2,40,256]{2,1,0:T(8,128)S(1)}, u32[]{:S(2)}, u32[]{:S(2)}) collective-permute-start(f32[2,40,256]{2,1,0:T(8,128)S(1)} %get-tuple-element.25), channel_id=1, source_target_pairs={{0,8},{8,0},{16,24},{24,16},{1,9},{9,1},{17,25},{25,17},{2,10},{10... | collective-permute-start | bytes 245768 | tf_op jit(solution)/shard_map/ppermute | solution.py:649
  5.8 8.2 %copy-start.5 = (bf16[256,128]{1,0:T(8,128)(2,1)S(1)}, bf16[256,128]{1,0:T(8,128)(2,1)}, u32[]{:S(2)}) copy-start(bf16[256,128]{1,0:T(8,128)(2,1)} %constant.17.clone.refs_7_.refs_9_) | copy-start | bytes 196612
  5.8 8.2 %copy-start.6 = (bf16[384,256]{1,0:T(8,128)(2,1)S(1)}, bf16[384,256]{1,0:T(8,128)(2,1)}, u32[]{:S(2)}) copy-start(bf16[384,256]{1,0:T(8,128)(2,1)} %constant.16.clone.refs_6_) | copy-start | bytes 589828
  5.8 8.2 %copy-start.10 = (bf16[128,128]{1,0:T(8,128)(2,1)S(1)}, bf16[128,128]{1,0:T(8,128)(2,1)}, u32[]{:S(2)}) copy-start(bf16[128,128]{1,0:T(8,128)(2,1)} %constant.18.clone.refs_8_) | copy-start | bytes 98308
  5.8 2.4 %collective-permute-start.1 = (f32[2,40,256]{2,1,0:T(8,128)S(1)}, f32[2,40,256]{2,1,0:T(8,128)S(1)}, u32[]{:S(2)}, u32[]{:S(2)}) collective-permute-start(f32[2,40,256]{2,1,0:T(8,128)S(1)} %get-tuple-element.26), channel_id=1, source_target_pairs={{0,1},{1,0},{2,3},{3,2},{4,5},{5,4},{6,7},{7,6},{8,16},{9,17},{10,... | collective-permute-start | bytes 245768 | tf_op jit(solution)/shard_map/ppermute | solution.py:649
  8.4 3.3 %collective-permute-start.2 = (f32[144,128]{1,0:T(8,128)S(1)}, f32[144,128]{1,0:T(8,128)S(1)}, u32[]{:S(2)}, u32[]{:S(2)}) collective-permute-start(f32[144,128]{1,0:T(8,128)S(1)} %get-tuple-element.27), channel_id=1, source_target_pairs={{0,1},{1,0},{2,3},{3,2},{4,5},{5,4},{6,7},{7,6},{8,9},{9,8},{10,11... | collective-permute-start | bytes 221192 | tf_op jit(solution)/shard_map/ppermute | solution.py:649
  8.5 5.5 %collective-permute-start.3 = (f32[144,128]{1,0:T(8,128)S(1)}, f32[144,128]{1,0:T(8,128)S(1)}, u32[]{:S(2)}, u32[]{:S(2)}) collective-permute-start(f32[144,128]{1,0:T(8,128)S(1)} %get-tuple-element.28), channel_id=1, source_target_pairs={{0,8},{1,2},{2,1},{3,4},{4,3},{5,6},{6,5},{7,15},{8,0},{9,10},{10,... | collective-permute-start | bytes 221192 | tf_op jit(solution)/shard_map/ppermute | solution.py:649
  15.6 18.3 %copy-start.4 = (bf16[512,256]{1,0:T(8,128)(2,1)S(1)}, bf16[512,256]{1,0:T(8,128)(2,1)}, u32[]{:S(2)}) copy-start(bf16[512,256]{1,0:T(8,128)(2,1)} %constant.19.clone.refs_8_) | copy-start | bytes 786436
  15.6 18.3 %copy-start.11 = (bf16[128,128]{1,0:T(8,128)(2,1)S(1)}, bf16[128,128]{1,0:T(8,128)(2,1)}, u32[]{:S(2)}) copy-start(bf16[128,128]{1,0:T(8,128)(2,1)} %constant.20.clone.refs_10_) | copy-start | bytes 98308
  32.4 1.5 %collective-permute-start.4 = (f32[512,128]{1,0:T(8,128)S(1)}, f32[512,128]{1,0:T(8,128)S(1)}, u32[]{:S(2)}, u32[]{:S(2)}) collective-permute-start(f32[512,128]{1,0:T(8,128)S(1)} %bitcast.4), channel_id=1, source_target_pairs={{0,1},{1,0},{2,3},{3,2},{4,5},{5,4},{6,7},{7,6},{8,9},{9,8},{10,11... | collective-permute-start | bytes 786440 | tf_op jit(solution)/shard_map/ppermute | solution.py:660
  33.9 14.3 %copy-start.7 = (bf16[256,384]{1,0:T(8,128)(2,1)S(1)}, bf16[256,384]{1,0:T(8,128)(2,1)}, u32[]{:S(2)}) copy-start(bf16[256,384]{1,0:T(8,128)(2,1)} %constant.23.clone.refs_17_) | copy-start | bytes 589828
  38.5 9.8 %copy-start.8 = (bf16[128,256]{1,0:T(8,128)(2,1)S(1)}, bf16[128,256]{1,0:T(8,128)(2,1)}, u32[]{:S(2)}) copy-start(bf16[128,256]{1,0:T(8,128)(2,1)} %constant.22.clone.refs_16_) | copy-start | bytes 196612
  38.5 9.8 %copy-start.9 = (bf16[256,128]{1,0:T(8,128)(2,1)S(1)}, bf16[256,128]{1,0:T(8,128)(2,1)}, u32[]{:S(2)}) copy-start(bf16[256,128]{1,0:T(8,128)(2,1)} %constant.21.clone.refs_15_) | copy-start | bytes 196612

commit v8 on v7

--- a/solution.py
+++ b/solution.py
@@ -153,20 +153,6 @@
     even = lax.rem(at, 2) == 0
     first, second = first_ref[...], second_ref[...]
     return jnp.where(even, first, second), jnp.where(even, second, first)
-
-
-def rows_kernel(sizes, g_ref, s_ref, first_ref, second_ref, semaphores):
-    even = lax.rem(lax.axis_index("gx"), 2) == 0
-    last = sizes.rows - HALO
-    copies = []
-    for k, (out, start) in enumerate(((first_ref, jnp.where(even, last, 0)), (second_ref, jnp.where(even, 0, last)))):
-        for f, ref in enumerate((g_ref, s_ref)):
-            rows = pl.ds(pl.multiple_of(start, 8), HALO)
-            copies.append(pltpu.make_async_copy(ref.at[rows, :], out.at[f], semaphores.at[2 * k + f]))
-    for copy in copies:
-        copy.start()
-    for copy in copies:
-        copy.wait()
 
 
 def strip_rows(sizes):
@@ -263,7 +249,7 @@
         self.z = sizes
         self.first = first
         self.d, self.w, self.g, self.v, self.t = d_refs, w_refs, g_refs, v_refs, t_refs
-        self.va, self.vb, self.wk, self.gk = coarsest
+        self.va, self.vb, self.wk, self.gk, self.wide_v, self.wide_t, self.wide_w, self.wide_g = coarsest
         lane = iota((sizes.p, sizes.coarse_columns), 1)
         self.first_lane, self.last_lane = lane == 0, lane == sizes.coarse_columns - 1
 
@@ -371,9 +357,9 @@
 
         self.each(level, body)
 
-    def inner(self, ref):
+    def inner(self, ref, s=0, r=0):
         p = self.z.p
-        return ref[0, 0, p : p + self.z.coarse_rows, :]
+        return ref[s, r, p : p + self.z.coarse_rows, :]
 
     def shifted(self, x, k):
         if k == 0:
@@ -390,6 +376,7 @@
         missing = 2.0 * (z.coarse_rows + z.coarse_columns)
         for k in range(-2, 3):
             self.wk[k + 2] = self.shifted(w, k)
+        self.widen(self.w[top - 1], self.wide_w, 1, False)
         return 1.0 / (jnp.sum(d - 4.0, keepdims=True) + missing)
 
     def coarse(self, fresh, unit):
@@ -436,29 +423,87 @@
                         self.v[top][0, 0, p : p + height, :] = value
                 source, target = target, source
 
+    def widen(self, source, target, reach, padded):
+        rows = slice(self.z.p, self.z.p + self.z.coarse_rows) if padded else slice(None)
+        for s in range(2):
+            for k in range(-reach, 2 + reach):
+                target[s, k + reach, rows, :] = self.shifted(self.inner(source, s, k % 2), k // 2)
+
+    def twice(self, restricting):
+        l = LEVELS - 1 - self.first
+        p, height = self.z.p, self.z.coarse_rows
+        rows = slice(p, p + height)
+
+        def at(ref, s, k, step=0):
+            return ref[s, k + 2, p + step : p + step + height, :]
+
+        def beside(ref, s, k):
+            up = at(ref, 0, k) if s else at(ref, 1, k, -1)
+            down = at(ref, 0, k, 1) if s else at(ref, 1, k)
+            return (up + down) + (at(ref, s, k - 1) + at(ref, s, k + 1))
+
+        def swept(ref, s, k):
+            total = self.wide_g[s, k + 1] + beside(ref, s, k)
+            return (1.0 - DAMPING) * at(ref, s, k) + self.wide_w[s, k + 1] * total
+
+        self.widen(self.v[l], self.wide_v, 2, True)
+        for s in range(2):
+            for k in range(-1, 3):
+                self.wide_t[s, k + 2, rows, :] = swept(self.wide_v, s, k)
+        parts = []
+        for s in range(2):
+            for k in range(2):
+                if restricting:
+                    v = at(self.wide_t, s, k)
+                    self.v[l][s, k, rows, :] = v
+                    left = self.wide_g[s, k + 1] - self.inner(self.d[l], s, k) * v
+                    parts.append(left + beside(self.wide_t, s, k))
+                else:
+                    self.v[l][s, k, rows, :] = swept(self.wide_t, s, k)
+        if restricting:
+            self.g[l + 1][0, 0, rows, :] = (parts[0] + parts[1]) + (parts[2] + parts[3])
+
+    def before(self, level, fresh, new_source):
+        l = level - self.first
+        if level < LEVELS - 1:
+            if fresh:
+                self.start(level)
+            else:
+                self.two_sweeps(level)
+            self.restrict(level)
+            return
+        if new_source:
+            self.widen(self.g[l], self.wide_g, 1, False)
+        if fresh:
+            self.first_sweep(level)
+        else:
+            self.sweep(level, self.v[l], self.t[l])
+            self.v[l], self.t[l] = self.t[l], self.v[l]
+        self.twice(True)
+
+    def after(self, level):
+        self.prolong(level)
+        if level < LEVELS - 1:
+            self.two_sweeps(level)
+        else:
+            self.twice(False)
+
     def vcycle(self, level, fresh, unit):
         if level == LEVELS:
             self.coarse(fresh, unit)
             return
-        if fresh:
-            self.start(level)
-        else:
-            self.two_sweeps(level)
-        self.restrict(level)
+        self.before(level, fresh, fresh)
         self.vcycle(level + 1, True, unit)
-        self.prolong(level)
-        self.two_sweeps(level)
+        self.after(level)
 
     def fcycle(self, level, unit):
         if level == LEVELS:
             self.coarse(True, unit)
             return
-        self.start(level)
-        self.restrict(level)
+        self.before(level, True, True)
         self.fcycle(level + 1, unit)
         self.vcycle(level + 1, False, unit)
-        self.prolong(level)
-        self.two_sweeps(level)
+        self.after(level)
 
     def clear_ends(self):
         z = self.z
@@ -470,8 +515,8 @@
                     for r in range(n):
                         ref[s, r, : z.p, :] = zero
                         ref[s, r, z.p + z.coarse_rows :, :] = zero
-        for ref in (self.va, self.vb):
-            for k in range(7):
+        for ref in (self.va, self.vb, self.wide_v.at[0], self.wide_v.at[1], self.wide_t.at[0], self.wide_t.at[1]):
+            for k in range(ref.shape[0]):
                 ref[k, : z.p, :] = zero
                 ref[k, z.p + z.coarse_rows :, :] = zero
 
@@ -619,7 +664,7 @@
     return [pl.BlockSpec(memory_space=pltpu.VMEM)] * count
 
 
-def call(kernel, sizes, outs, scratch, *operands, inputs=None, semaphores=()):
+def call(kernel, sizes, outs, scratch, *operands):
     shapes = [jax.ShapeDtypeStruct(shape, jnp.float32) for shape in outs]
     used = sum(4 * int(np.prod(shape)) for shape in list(outs) + list(scratch))
     used += sum(x.size * x.dtype.itemsize for x in operands)
@@ -627,9 +672,9 @@
         lambda *refs: kernel(sizes, *refs),
         name=kernel.__name__,
         out_shape=shapes,
-        in_specs=vmem(len(operands)) if inputs is None else inputs,
+        in_specs=vmem(len(operands)),
         out_specs=vmem(len(outs)),
-        scratch_shapes=[pltpu.VMEM(shape, jnp.float32) for shape in scratch] + list(semaphores),
+        scratch_shapes=[pltpu.VMEM(shape, jnp.float32) for shape in scratch],
         compiler_params=pltpu.CompilerParams(vmem_limit_bytes=used + used // 4 + (4 << 20)),
     )(*operands)
 
@@ -664,10 +709,13 @@
     nx, ny = lax.axis_size("gx"), lax.axis_size("gy")
     rows, columns = right_side.shape
     z = Sizes(rows, columns, nx, ny)
-    first, second = call(
-        rows_kernel, z, [(2, HALO, columns)] * 2, [], right_side, shift,
-        inputs=[pl.BlockSpec(memory_space=pltpu.HBM)] * 2, semaphores=[pltpu.SemaphoreType.DMA((4,))])
-    rows_a, rows_b = swaps(first, second, "gx", "gy")
+    even = lax.axis_index("gx") % 2 == 0
+    last = rows - HALO
+
+    def strips(start):
+        return jnp.stack([lax.dynamic_slice(x, (start, 0), (HALO, columns)) for x in (right_side, shift)])
+
+    rows_a, rows_b = swaps(strips(jnp.where(even, last, 0)), strips(jnp.where(even, 0, last)), "gx", "gy")
     ext = [(z.ext_rows[l], z.ext_columns[l]) for l in range(3)]
     strip = (strip_rows(z)[1], 128)
     first, second = call(strip_kernel, z, [strip] * 2, [], right_side, shift, rows_a, rows_b)
@@ -679,7 +727,8 @@
         right_side, shift, rows_a, rows_b, columns_a, columns_b, rc0, rc1, z.pack_pair())
     y, other = gather_by_core(packed, nx, ny)
     slabs = [level_shape(z, level) for level in (2, 3, 4)]
-    coarsest = [(7,) + slabs[2][2:]] * 2 + [(5, z.coarse_rows, z.coarse_columns)] * 2
+    padded, plain = slabs[2][2:], (z.coarse_rows, z.coarse_columns)
+    coarsest = [(7,) + padded] * 2 + [(5,) + plain] * 2 + [(2, 6) + padded] * 2 + [(2, 4) + plain] * 2
     d3, d4, w3, w4, e1, c2, e2, packed = call(
         middle_kernel, z, slabs[1:] * 2 + [ext[1], ext[2], ext[2], (nx * ny * 4, 128)],
         [slabs[0]] * 2 + slabs * 3 + [tiles, (4, 12 * z.p, 128)] + coarsest,

time: 51.2 us -> 50 us (0.977)
  local copies, waits for them, and re-layouts: 1.84 us -> 0.91 us
    unnamed x24 -> x20, local copies, waits for them, and re-layouts: 1.84 us -> 0.05 us
    another operation x0 -> x1, local copies, waits for them, and re-layouts: none -> 0.86 us  [strips(): jnp.stack([lax.dynamic_slice(x, (start, 0), (HALO, columns)) for x in (ri...]
    pallas_call x5 -> x4, Pallas kernels: 9.2 us -> 8.82 us  [call(): pl.pallas_call(lambda *refs: kernel(sizes, *refs), name=kernel.__name__,...]
where the time goes in v8:
time: 50 us; the launch traced here: 49.7 us
  blocking collectives  26.5 us (53%)
  Pallas kernels  8.82 us (18%)
  starting transfers between devices  6.55 us (13%)
  waiting for transfers between devices  6.19 us (12%)
  local copies, waits for them, and re-layouts  0.91 us (2%)
  between operations  0.76 us (2%)
    all_to_all x1, blocking collectives, gather_by_core(): lax.all_to_all(copies, ('gx', 'gy'), 0, 0, tiled=True, axis_index_groups=...  16.7 us
    all_to_all x1, blocking collectives, gather(): return lax.all_to_all(copies, ('gx', 'gy'), 0, 0, tiled=True)  9.74 us
    pallas_call x4, Pallas kernels, call(): pl.pallas_call(lambda *refs: kernel(sizes, *refs), name=kernel.__name__,...  8.82 us
    ppermute x2, starting transfers between devices, swaps(): lax.ppermute(second, ('gx', 'gy'), pairs)  3.36 us
    ppermute x2, starting transfers between devices, swaps(): lax.ppermute(first, axis, [(i, i ^ 1) for i in range(count)])  3.19 us
    ppermute x2, waiting for transfers between devices, swaps(): lax.ppermute(second, ('gx', 'gy'), pairs)  2.33 us
    ppermute x2, waiting for transfers between devices, swaps(): lax.ppermute(first, axis, [(i, i ^ 1) for i in range(count)])  2.33 us
    ppermute x1, waiting for transfers between devices, gather_by_core(): return (own, lax.ppermute(own, 'gy', [(j, j ^ 1) for j in range(ny)]))  1.53 us
  transfers between devices with their start and end apart: 5, of which 3 were waited for; matrix products, arithmetic and copies ran while one was open for 0% of the time, Pallas kernels for 0%

profile of v8, /device:TPU:0, one launch (start us, length us, event | category | flops | bytes accessed | tf_op | source)
XLA Modules:
  0.0 49.7 jit_solution(1866534113518119275)
XLA Ops:
  0.6 0.9 %dynamic-slice_bitcast_fusion = (f32[1,40,256]{2,1,0:T(8,128)S(1)}, f32[1,40,256]{2,1,0:T(8,128)S(1)}, f32[1,40,256]{2,1,0:T(8,128)S(1)}, f32[1,40,256]{2,1,0:T(8,128)S(1)}) fusion(f32[128,256]{1,0:T(8,128)} %refs_1_.3, s32[]{:T(128)S(6)} %select_n.20, s32[]{:T(128)S(6)} %select_n.19, f32[128,256]{1,0:T(8,128)} %refs_0_.3), kind=kLoop, calls=%fused_computation.2 | loop fusion | bytes 327688 | tf_op jit(solution)/shard_map/stack | solution.py:716
  1.5 0.0 copy-start
  1.5 0.0 copy-start.1
  1.5 3.1 %collective-permute-start = (f32[2,40,256]{2,1,0:T(8,128)S(1)}, f32[2,40,256]{2,1,0:T(8,128)S(1)}, u32[]{:S(2)}, u32[]{:S(2)}) collective-permute-start(f32[2,40,256]{2,1,0:T(8,128)S(1)} %pad_maximum_fusion), channel_id=1, source_target_pairs={{0,8},{8,0},{16,24},{24,16},{1,9},{9,1},{17,25},{25,17},{2,10},{10... | collective-permute-start | bytes 245768 | tf_op jit(solution)/shard_map/ppermute | solution.py:694
  4.7 0.0 copy-start.4
  4.7 0.0 copy-start.8
  4.7 0.1 collective-permute-start.1
  4.8 2.3 %collective-permute-done.refs_2_ = f32[2,40,256]{2,1,0:T(8,128)S(1)} collective-permute-done((f32[2,40,256]{2,1,0:T(8,128)S(1)}, f32[2,40,256]{2,1,0:T(8,128)S(1)}, u32[]{:S(2)}, u32[]{:S(2)}) %collective-permute-start) | collective-permute-done | bytes 81952 | tf_op jit(solution)/shard_map/ppermute | solution.py:694
  7.1 0.0 collective-permute-done.1.refs_3_
  7.1 0.0 copy-done
  7.1 0.0 copy-done.1
  7.1 0.1 strip_kernel.1
  7.3 0.1 collective-permute-start.2
  7.3 3.3 %collective-permute-start.3 = (f32[144,128]{1,0:T(8,128)S(1)}, f32[144,128]{1,0:T(8,128)S(1)}, u32[]{:S(2)}, u32[]{:S(2)}) collective-permute-start(f32[144,128]{1,0:T(8,128)S(1)} %get-tuple-element.24), channel_id=1, source_target_pairs={{0,8},{1,2},{2,1},{3,4},{4,3},{5,6},{6,5},{7,15},{8,0},{9,10},{10,... | collective-permute-start | bytes 221192 | tf_op jit(solution)/shard_map/ppermute | solution.py:694
  10.6 0.0 collective-permute-done.2.refs_4_
  10.6 2.3 %collective-permute-done.3.refs_5_ = f32[144,128]{1,0:T(8,128)S(1)} collective-permute-done((f32[144,128]{1,0:T(8,128)S(1)}, f32[144,128]{1,0:T(8,128)S(1)}, u32[]{:S(2)}, u32[]{:S(2)}) %collective-permute-start.3) | collective-permute-done | bytes 73760 | tf_op jit(solution)/shard_map/ppermute | solution.py:694
  13.0 0.0 copy-done.3
  13.0 0.0 copy-done.4
  13.0 0.0 copy-done.8
  13.0 1.6 %down_kernel.1 = (f32[144,384]{1,0:T(8,128)S(1)}, f32[144,384]{1,0:T(8,128)S(1)}, f32[144,384]{1,0:T(8,128)S(1)}, f32[144,384]{1,0:T(8,128)S(1)}, f32[96,256]{1,...) custom-call(f32[128,256]{1,0:T(8,128)S(1)} %copy-done, ...), custom_call_target="tpu_custom_call" | custom-call | tf_op jit(solution)/shard_map/down_kernel/pallas_call | solution.py:671
  14.5 0.0 copy-start.2
  14.6 0.0 copy-start.9
  14.6 16.7 %all_to_all.22 = f32[16,32,128]{2,1,0:T(8,128)S(1)} all-to-all(f32[16,32,128]{2,1,0:T(8,128)S(1)} %bitcast.14), channel_id=1, replica_groups={{0,2,4,6,8,10,12,14,16,18,20,22,24,26,28,30},{1,3,5,7,9,11,13,15,17,19,..., dimensions={0} | all-to-all | bytes 524288 | tf_op jit(solution)/shard_map/all_to_all | solution.py:704
  31.3 0.0 collective-permute-start.4
  31.3 1.5 %collective-permute-done.4.refs_1_ = f32[512,128]{1,0:T(8,128)S(1)} collective-permute-done((f32[512,128]{1,0:T(8,128)S(1)}, f32[512,128]{1,0:T(8,128)S(1)}, u32[]{:S(2)}, u32[]{:S(2)}) %collective-permute-start.4) | collective-permute-done | bytes 262176 | tf_op jit(solution)/shard_map/ppermute | solution.py:705
  32.9 0.0 copy-done.2
  32.9 0.0 copy-done.9
  32.9 4.5 %middle_kernel.1 = (f32[2,2,48,128]{3,2,1,0:T(8,128)S(1)}, f32[1,1,48,128]{3,2,1,0:T(8,128)S(1)}, f32[2,2,48,128]{3,2,1,0:T(8,128)S(1)}, f32[1,1,48,128]{3,2,1,0...) custom-call(f32[512,128]{1,0:T(8,128)S(1)} %bitcast.13, ...), custom_call_target="tpu_custom_call" | custom-call | tf_op jit(solution)/shard_map/middle_kernel/pallas_call | solution.py:671
  37.3 9.7 %all_to_all.23 = f32[32,4,128]{2,1,0:T(4,128)S(1)} all-to-all(f32[32,4,128]{2,1,0:T(4,128)S(1)} %bitcast.16), channel_id=1, replica_groups=mesh['gx'=4,'gy'=8] {'gx','gy'}, dimensions={0} | all-to-all | bytes 131072 | tf_op jit(solution)/shard_map/all_to_all | solution.py:698
  47.1 0.0 copy-done.5
  47.1 0.0 copy-done.6
  47.1 2.7 %up_kernel.1 = (f32[128,256]{1,0:T(8,128)}, f32[128,256]{1,0:T(8,128)}) custom-call(f32[128,128]{1,0:T(8,128)S(1)} %bitcast.15, f32[2,2,48,128]{3,2,1,0:T(8,128)S(1)} %get-tuple-element.33.refs_1_, f32[1,1,48,128]{3,2,1,0:T(8,128)S(1)} %get-tuple-element.34.refs_2_, f32[2,2,48,128]{3,2,1,0:T(8,128)S(1)} %get-tuple-element.35.refs_3_, ...), custom_call_target="tpu_custom_call" | custom-call | tf_op jit(solution)/shard_map/up_kernel/pallas_call | solution.py:671
  (7 shorter events, 0.0 us)
Async XLA Ops:
  1.5 5.6 %copy-start = (f32[128,256]{1,0:T(8,128)S(1)}, f32[128,256]{1,0:T(8,128)}, u32[]{:S(2)}) copy-start(f32[128,256]{1,0:T(8,128)} %refs_0_.3) | copy-start | bytes 393220
  1.5 5.6 %copy-start.1 = (f32[128,256]{1,0:T(8,128)S(1)}, f32[128,256]{1,0:T(8,128)}, u32[]{:S(2)}) copy-start(f32[128,256]{1,0:T(8,128)} %refs_1_.3) | copy-start | bytes 393220
  1.5 5.6 %collective-permute-start = (f32[2,40,256]{2,1,0:T(8,128)S(1)}, f32[2,40,256]{2,1,0:T(8,128)S(1)}, u32[]{:S(2)}, u32[]{:S(2)}) collective-permute-start(f32[2,40,256]{2,1,0:T(8,128)S(1)} %pad_maximum_fusion), channel_id=1, source_target_pairs={{0,8},{8,0},{16,24},{24,16},{1,9},{9,1},{17,25},{25,17},{2,10},{10... | collective-permute-start | bytes 245768 | tf_op jit(solution)/shard_map/ppermute | solution.py:694
  4.7 8.3 %copy-start.3 = (bf16[256,128]{1,0:T(8,128)(2,1)S(1)}, bf16[256,128]{1,0:T(8,128)(2,1)}, u32[]{:S(2)}) copy-start(bf16[256,128]{1,0:T(8,128)(2,1)} %constant.41.clone.refs_7_.refs_9_) | copy-start | bytes 196612
  4.7 8.3 %copy-start.4 = (bf16[384,256]{1,0:T(8,128)(2,1)S(1)}, bf16[384,256]{1,0:T(8,128)(2,1)}, u32[]{:S(2)}) copy-start(bf16[384,256]{1,0:T(8,128)(2,1)} %constant.40.clone.refs_6_) | copy-start | bytes 589828
  4.7 8.3 %copy-start.8 = (bf16[128,128]{1,0:T(8,128)(2,1)S(1)}, bf16[128,128]{1,0:T(8,128)(2,1)}, u32[]{:S(2)}) copy-start(bf16[128,128]{1,0:T(8,128)(2,1)} %constant.42.clone.refs_8_) | copy-start | bytes 98308
  4.7 2.4 %collective-permute-start.1 = (f32[2,40,256]{2,1,0:T(8,128)S(1)}, f32[2,40,256]{2,1,0:T(8,128)S(1)}, u32[]{:S(2)}, u32[]{:S(2)}) collective-permute-start(f32[2,40,256]{2,1,0:T(8,128)S(1)} %pad_maximum_fusion.1), channel_id=1, source_target_pairs={{0,1},{1,0},{2,3},{3,2},{4,5},{5,4},{6,7},{7,6},{8,16},{9,17},{10,... | collective-permute-start | bytes 245768 | tf_op jit(solution)/shard_map/ppermute | solution.py:694
  7.3 3.4 %collective-permute-start.2 = (f32[144,128]{1,0:T(8,128)S(1)}, f32[144,128]{1,0:T(8,128)S(1)}, u32[]{:S(2)}, u32[]{:S(2)}) collective-permute-start(f32[144,128]{1,0:T(8,128)S(1)} %get-tuple-element.23), channel_id=1, source_target_pairs={{0,1},{1,0},{2,3},{3,2},{4,5},{5,4},{6,7},{7,6},{8,9},{9,8},{10,11... | collective-permute-start | bytes 221192 | tf_op jit(solution)/shard_map/ppermute | solution.py:694
  7.3 5.6 %collective-permute-start.3 = (f32[144,128]{1,0:T(8,128)S(1)}, f32[144,128]{1,0:T(8,128)S(1)}, u32[]{:S(2)}, u32[]{:S(2)}) collective-permute-start(f32[144,128]{1,0:T(8,128)S(1)} %get-tuple-element.24), channel_id=1, source_target_pairs={{0,8},{1,2},{2,1},{3,4},{4,3},{5,6},{6,5},{7,15},{8,0},{9,10},{10,... | collective-permute-start | bytes 221192 | tf_op jit(solution)/shard_map/ppermute | solution.py:694
  14.5 18.3 %copy-start.2 = (bf16[512,256]{1,0:T(8,128)(2,1)S(1)}, bf16[512,256]{1,0:T(8,128)(2,1)}, u32[]{:S(2)}) copy-start(bf16[512,256]{1,0:T(8,128)(2,1)} %constant.43.clone.refs_8_) | copy-start | bytes 786436
  14.6 18.3 %copy-start.9 = (bf16[128,128]{1,0:T(8,128)(2,1)S(1)}, bf16[128,128]{1,0:T(8,128)(2,1)}, u32[]{:S(2)}) copy-start(bf16[128,128]{1,0:T(8,128)(2,1)} %constant.44.clone.refs_10_) | copy-start | bytes 98308
  31.3 1.5 %collective-permute-start.4 = (f32[512,128]{1,0:T(8,128)S(1)}, f32[512,128]{1,0:T(8,128)S(1)}, u32[]{:S(2)}, u32[]{:S(2)}) collective-permute-start(f32[512,128]{1,0:T(8,128)S(1)} %bitcast.12), channel_id=1, source_target_pairs={{0,1},{1,0},{2,3},{3,2},{4,5},{5,4},{6,7},{7,6},{8,9},{9,8},{10,11... | collective-permute-start | bytes 786440 | tf_op jit(solution)/shard_map/ppermute | solution.py:705
  32.9 14.2 %copy-start.5 = (bf16[256,384]{1,0:T(8,128)(2,1)S(1)}, bf16[256,384]{1,0:T(8,128)(2,1)}, u32[]{:S(2)}) copy-start(bf16[256,384]{1,0:T(8,128)(2,1)} %constant.47.clone.refs_17_) | copy-start | bytes 589828
  37.3 9.8 %copy-start.6 = (bf16[128,256]{1,0:T(8,128)(2,1)S(1)}, bf16[128,256]{1,0:T(8,128)(2,1)}, u32[]{:S(2)}) copy-start(bf16[128,256]{1,0:T(8,128)(2,1)} %constant.46.clone.refs_16_) | copy-start | bytes 196612
  37.3 9.8 %copy-start.7 = (bf16[256,128]{1,0:T(8,128)(2,1)S(1)}, bf16[256,128]{1,0:T(8,128)(2,1)}, u32[]{:S(2)}) copy-start(bf16[256,128]{1,0:T(8,128)(2,1)} %constant.45.clone.refs_15_) | copy-start | bytes 196612

commit v9 on v8

--- a/solution.py
+++ b/solution.py
@@ -64,10 +64,12 @@
         return hit.astype(jnp.bfloat16)
 
     def pack_pair(self):
-        own = self.columns >> 2
-        x = np.arange(2 * own)
-        target = (x // own) * own + (x % own % 4) * self.q + x % own // 4
-        return (target[:, None] == np.arange(2 * own)[None, :]).astype(jnp.bfloat16)
+        width, own = self.ext_columns[1], self.columns >> 1
+        x = np.arange(2 * width)
+        column = x % width // 2
+        target = (x // width) * (own // 2) + (column % 4) * self.q + column // 4
+        hit = (target[:, None] == np.arange(own)[None, :]) & (x % width < own)[:, None]
+        return hit.astype(jnp.bfloat16)
 
     def pack_single(self):
         x = np.arange(self.ext_columns[2])[:, None]
@@ -126,10 +128,8 @@
 
 
 def pack_two(sizes, gy, first, second, scratch, columns_ref, out_ref):
-    own = sizes.columns >> 2
-    both = jnp.where(iota(first.shape, 1) < own, first, pltpu.roll(second, own, 1))
-    rows = both.shape[0]
-    scratch[0, :rows, :] = f32dot_right(both, columns_ref[...])
+    rows = first.shape[0]
+    scratch[0, :rows, :] = f32dot_right(jnp.concatenate([first, second], axis=1), columns_ref[...])
     block = jnp.concatenate([scratch[0, pl.ds(s, sizes.p, stride=4), :] for s in range(4)], axis=0)
     repeat(pltpu.roll(block, lax.rem(gy, 8) * sizes.q, 1), out_ref)
 
@@ -233,15 +233,12 @@
     d1_ref[...] = d
     w1_ref[...] = w
     v1_ref[...] = v
-    half = half // 2
-    both = jnp.concatenate([pair_rows(scratch, r), pair_rows(scratch, sigma)], axis=0)
-    both = f32dot_right(both, rc1_ref[...])
-    g, sigma = both[:half], both[half:]
-    d, w = coefficients(sizes, 2, gx, gy, sigma)
+    own = sizes.rows // 4
+    source, sigma = pair_rows(scratch, r), pair_rows(scratch, sigma)
+    pack_two(sizes, gy, source[:own], sigma[:own], scratch, pc_ref, out_ref)
+    d, w = coefficients(sizes, 2, gx, gy, f32dot_right(sigma, rc1_ref[...]))
     d2_ref[...] = d
     w2_ref[...] = w
-    own = sizes.rows // 4
-    pack_two(sizes, gy, g[:own], sigma[:own], scratch, pc_ref, out_ref)
 
 
 class Coarse:
@@ -249,7 +246,7 @@
         self.z = sizes
         self.first = first
         self.d, self.w, self.g, self.v, self.t = d_refs, w_refs, g_refs, v_refs, t_refs
-        self.va, self.vb, self.wk, self.gk, self.wide_v, self.wide_t, self.wide_w, self.wide_g = coarsest
+        self.va, self.vb, self.wk, self.gk, self.wide_v, self.wide_t, self.wide_w, self.wide_g, self.ones = coarsest
         lane = iota((sizes.p, sizes.coarse_columns), 1)
         self.first_lane, self.last_lane = lane == 0, lane == sizes.coarse_columns - 1
 
@@ -369,7 +366,7 @@
         keep = lane < columns - k if k > 0 else lane >= -k
         return jnp.where(keep, pltpu.roll(x, -k % columns, 1), 0.0)
 
-    def unit(self):
+    def unit(self, build):
         z = self.z
         top = LEVELS - self.first
         d, w = self.inner(self.d[top]), self.inner(self.w[top])
@@ -377,51 +374,58 @@
         for k in range(-2, 3):
             self.wk[k + 2] = self.shifted(w, k)
         self.widen(self.w[top - 1], self.wide_w, 1, False)
+        if build:
+            lane = iota(d.shape, 1)
+            for k in range(-3, 4):
+                self.put_shifted(self.va, k, jnp.where((lane < d.shape[1] - k) & (lane >= -k), 1.0, 0.0))
+            self.ones[...] = self.coarse_sweeps(False, False)
         return 1.0 / (jnp.sum(d - 4.0, keepdims=True) + missing)
+
+    def shifted_at(self, ref, k, step=0):
+        p = self.z.p
+        return ref[k + 3, p + step : p + step + self.z.coarse_rows, :]
+
+    def put_shifted(self, ref, k, value):
+        ref[k + 3, self.z.p : self.z.p + self.z.coarse_rows, :] = value
+
+    def coarse_sweeps(self, from_zero, with_source):
+        at = self.shifted_at
+        for turn in range(COARSE_SWEEPS // 3):
+            if turn:
+                for k in range(-3, 4):
+                    self.put_shifted(self.va, k, self.shifted(value, k))
+            source, target = self.va, self.vb
+            for reach in (2, 1, 0):
+                for k in range(-reach, reach + 1):
+                    if from_zero and not turn and reach == 2:
+                        value = self.wk[k + 2] * self.gk[k + 2]
+                    else:
+                        total = (at(source, k, -1) + at(source, k, 1)) + (at(source, k - 1) + at(source, k + 1))
+                        if with_source:
+                            total = self.gk[k + 2] + total
+                        value = (1.0 - DAMPING) * at(source, k) + self.wk[k + 2] * total
+                    if reach:
+                        self.put_shifted(target, k, value)
+                source, target = target, source
+        return value
 
     def coarse(self, fresh, unit):
         top = LEVELS - self.first
-        p, height = self.z.p, self.z.coarse_rows
         g = self.inner(self.g[top])
         for k in range(-2, 3):
             self.gk[k + 2] = self.shifted(g, k)
-        lane = iota(g.shape, 1)
-
-        def at(ref, k, step=0):
-            return ref[k + 3, p + step : p + step + height, :]
-
-        def put(ref, k, value):
-            ref[k + 3, p : p + height, :] = value
-
         if fresh:
-            left = jnp.broadcast_to(jnp.sum(g, keepdims=True) * unit, g.shape)
-            v = {k: 0.0 for k in range(-3, 4)}
+            left = jnp.sum(g, keepdims=True)
         else:
             v = self.inner(self.v[top])
-            v = {k: self.shifted(v, k) for k in range(-3, 4)}
-            put(self.va, 0, v[0])
-            around_v = (at(self.va, 0, -1) + at(self.va, 0, 1)) + (v[-1] + v[1])
-            left = jnp.sum((g - self.inner(self.d[top]) * v[0]) + around_v, keepdims=True) * unit
-            left = jnp.broadcast_to(left, g.shape)
-        for k in range(-3, 4):
-            inside = (lane < g.shape[1] - k) & (lane >= -k)
-            put(self.va, k, v[k] + jnp.where(inside, left, 0.0) if k else v[k] + left)
-        for turn in range(COARSE_SWEEPS // 3):
-            if turn:
-                v = self.inner(self.v[top])
-                for k in range(-3, 4):
-                    put(self.va, k, self.shifted(v, k))
-            source, target = self.va, self.vb
-            for reach in (2, 1, 0):
-                for k in range(-reach, reach + 1):
-                    total = self.gk[k + 2] + (at(source, k, -1) + at(source, k, 1))
-                    total = total + (at(source, k - 1) + at(source, k + 1))
-                    value = (1.0 - DAMPING) * at(source, k) + self.wk[k + 2] * total
-                    if reach:
-                        put(target, k, value)
-                    else:
-                        self.v[top][0, 0, p : p + height, :] = value
-                source, target = target, source
+            for k in range(-3, 4):
+                self.put_shifted(self.va, k, self.shifted(v, k))
+            at = self.shifted_at
+            beside = (at(self.va, 0, -1) + at(self.va, 0, 1)) + (at(self.va, -1) + at(self.va, 1))
+            left = jnp.sum((g - self.inner(self.d[top]) * v) + beside, keepdims=True)
+        value = self.coarse_sweeps(fresh, True)
+        left = jnp.broadcast_to(left * unit, g.shape)
+        self.v[top][0, 0, self.z.p : self.z.p + self.z.coarse_rows, :] = value + left * self.ones[...]
 
     def widen(self, source, target, reach, padded):
         rows = slice(self.z.p, self.z.p + self.z.coarse_rows) if padded else slice(None)
@@ -585,10 +589,10 @@
 
 def middle_kernel(sizes, y_ref, other_ref, c1_ref, d1_ref, w1_ref, v1_ref, w2l_ref, d2l_ref, sc_ref,
                   rc1_ref, pc_ref,
-                  d3_ref, d4_ref, w3_ref, w4_ref, e1_ref, c2_ref, e2_ref, out_ref,
+                  d3_ref, d4_ref, w3_ref, w4_ref, ones_ref, e1_ref, c2_ref, e2_ref, out_ref,
                   d2, w2, g2, g3, g4, v2, v3, v4, t2, t3, t4, scratch, lines, *coarsest):
     gx, gy = lax.axis_index("gx"), lax.axis_index("gy")
-    m = Coarse(sizes, 2, [d2, d3_ref, d4_ref], [w2, w3_ref, w4_ref], [g2, g3, g4], [v2, v3, v4], [t2, t3, t4], coarsest)
+    m = Coarse(sizes, 2, [d2, d3_ref, d4_ref], [w2, w3_ref, w4_ref], [g2, g3, g4], [v2, v3, v4], [t2, t3, t4], (*coarsest, ones_ref))
     m.clear_ends()
     core = lax.rem(gy, 2)
 
@@ -615,7 +619,7 @@
             m.put(m.w[l], s, r, base, DAMPING / m.at(m.d[l], s, r, base))
 
         m.each(l + 2, body)
-    unit = m.unit()
+    unit = m.unit(True)
     m.fcycle(2, unit)
     m.vcycle(2, False, unit)
     g, d, w = c1_ref[...], d1_ref[...], w1_ref[...]
@@ -634,14 +638,14 @@
     pack_one(sizes, gy, pair_rows(scratch, r[: sizes.rows // 4]), scratch, pc_ref, out_ref)
 
 
-def up_kernel(sizes, y_ref, d3_ref, d4_ref, w3_ref, w4_ref, c2_ref, w2_ref, e2_ref, c1_ref, w1_ref, e1_ref,
+def up_kernel(sizes, y_ref, d3_ref, d4_ref, w3_ref, w4_ref, ones_ref, c2_ref, w2_ref, e2_ref, c1_ref, w1_ref, e1_ref,
               g0_ref, d0_ref, w0_ref, v0_ref, sc_ref, pc1_ref, pc0_ref,
               solution_ref, residual_ref, g3, g4, v3, v4, t3, t4, scratch, lines, *coarsest):
     gx, gy = lax.axis_index("gx"), lax.axis_index("gy")
-    m = Coarse(sizes, 3, [d3_ref, d4_ref], [w3_ref, w4_ref], [g3, g4], [v3, v4], [t3, t4], coarsest)
+    m = Coarse(sizes, 3, [d3_ref, d4_ref], [w3_ref, w4_ref], [g3, g4], [v3, v4], [t3, t4], (*coarsest, ones_ref))
     m.clear_ends()
     m.take_one(y_ref, g3)
-    m.vcycle(3, True, m.unit())
+    m.vcycle(3, True, m.unit(False))
     g, w = c2_ref[...], w2_ref[...]
     v = e2_ref[...] + jnp.where(w > 0.0, m.spread(gx, gy, sc_ref, scratch, lines), 0.0)
     for turn in range(2):
@@ -729,15 +733,15 @@
     slabs = [level_shape(z, level) for level in (2, 3, 4)]
     padded, plain = slabs[2][2:], (z.coarse_rows, z.coarse_columns)
     coarsest = [(7,) + padded] * 2 + [(5,) + plain] * 2 + [(2, 6) + padded] * 2 + [(2, 4) + plain] * 2
-    d3, d4, w3, w4, e1, c2, e2, packed = call(
-        middle_kernel, z, slabs[1:] * 2 + [ext[1], ext[2], ext[2], (nx * ny * 4, 128)],
+    d3, d4, w3, w4, ones, e1, c2, e2, packed = call(
+        middle_kernel, z, slabs[1:] * 2 + [plain, ext[1], ext[2], ext[2], (nx * ny * 4, 128)],
         [slabs[0]] * 2 + slabs * 3 + [tiles, (4, 12 * z.p, 128)] + coarsest,
         y, other, c1, d1, w1, v1, w2, d2, z.spread_columns(2),
         rc1, z.pack_single())
     y = gather(packed)
     return call(
         up_kernel, z, [(rows, columns)] * 2, slabs[1:] * 3 + [tiles, (2, 6 * z.p, 128)] + coarsest,
-        y, d3, d4, w3, w4, c2, w2, e2, c1, w1, e1, g0, d0, w0, v0,
+        y, d3, d4, w3, w4, ones, c2, w2, e2, c1, w1, e1, g0, d0, w0, v0,
         z.spread_columns(3), rc1.T, rc0.T)
 
 

time: 50 us -> 49.6 us (level)
  no operation moved by 1% of the time
where the time goes in v9:
time: 49.6 us; the launch traced here: 49.3 us
  blocking collectives  26.5 us (53%)
  Pallas kernels  8.4 us (17%)
  starting transfers between devices  6.55 us (13%)
  waiting for transfers between devices  6.19 us (12%)
  local copies, waits for them, and re-layouts  0.91 us (2%)
  between operations  0.75 us (2%)
    all_to_all x1, blocking collectives, gather_by_core(): lax.all_to_all(copies, ('gx', 'gy'), 0, 0, tiled=True, axis_index_groups=...  16.7 us
    all_to_all x1, blocking collectives, gather(): return lax.all_to_all(copies, ('gx', 'gy'), 0, 0, tiled=True)  9.74 us
    pallas_call x4, Pallas kernels, call(): pl.pallas_call(lambda *refs: kernel(sizes, *refs), name=kernel.__name__,...  8.4 us
    ppermute x2, starting transfers between devices, swaps(): lax.ppermute(second, ('gx', 'gy'), pairs)  3.36 us
    ppermute x2, starting transfers between devices, swaps(): lax.ppermute(first, axis, [(i, i ^ 1) for i in range(count)])  3.19 us
    ppermute x2, waiting for transfers between devices, swaps(): lax.ppermute(second, ('gx', 'gy'), pairs)  2.33 us
    ppermute x2, waiting for transfers between devices, swaps(): lax.ppermute(first, axis, [(i, i ^ 1) for i in range(count)])  2.33 us
    ppermute x1, waiting for transfers between devices, gather_by_core(): return (own, lax.ppermute(own, 'gy', [(j, j ^ 1) for j in range(ny)]))  1.53 us
  transfers between devices with their start and end apart: 5, of which 3 were waited for; matrix products, arithmetic and copies ran while one was open for 0% of the time, Pallas kernels for 0%

profile of v9, /device:TPU:0, one launch (start us, length us, event | category | flops | bytes accessed | tf_op | source)
XLA Modules:
  0.0 49.3 jit_solution(10261269411874070874)
XLA Ops:
  0.6 0.9 %dynamic-slice_bitcast_fusion = (f32[1,40,256]{2,1,0:T(8,128)S(1)}, f32[1,40,256]{2,1,0:T(8,128)S(1)}, f32[1,40,256]{2,1,0:T(8,128)S(1)}, f32[1,40,256]{2,1,0:T(8,128)S(1)}) fusion(f32[128,256]{1,0:T(8,128)} %refs_1_.3, s32[]{:T(128)S(6)} %select_n.20, s32[]{:T(128)S(6)} %select_n.19, f32[128,256]{1,0:T(8,128)} %refs_0_.3), kind=kLoop, calls=%fused_computation.2 | loop fusion | bytes 327688 | tf_op jit(solution)/shard_map/stack | solution.py:720
  1.5 0.0 copy-start
  1.5 0.0 copy-start.1
  1.5 3.1 %collective-permute-start = (f32[2,40,256]{2,1,0:T(8,128)S(1)}, f32[2,40,256]{2,1,0:T(8,128)S(1)}, u32[]{:S(2)}, u32[]{:S(2)}) collective-permute-start(f32[2,40,256]{2,1,0:T(8,128)S(1)} %pad_maximum_fusion), channel_id=1, source_target_pairs={{0,8},{8,0},{16,24},{24,16},{1,9},{9,1},{17,25},{25,17},{2,10},{10... | collective-permute-start | bytes 245768 | tf_op jit(solution)/shard_map/ppermute | solution.py:698
  4.7 0.0 copy-start.5
  4.7 0.0 copy-start.6
  4.7 0.1 collective-permute-start.1
  4.8 2.3 %collective-permute-done.refs_2_ = f32[2,40,256]{2,1,0:T(8,128)S(1)} collective-permute-done((f32[2,40,256]{2,1,0:T(8,128)S(1)}, f32[2,40,256]{2,1,0:T(8,128)S(1)}, u32[]{:S(2)}, u32[]{:S(2)}) %collective-permute-start) | collective-permute-done | bytes 81952 | tf_op jit(solution)/shard_map/ppermute | solution.py:698
  7.1 0.0 collective-permute-done.1.refs_3_
  7.1 0.0 copy-done
  7.1 0.0 copy-done.1
  7.1 0.1 strip_kernel.1
  7.3 0.1 collective-permute-start.2
  7.3 3.3 %collective-permute-start.3 = (f32[144,128]{1,0:T(8,128)S(1)}, f32[144,128]{1,0:T(8,128)S(1)}, u32[]{:S(2)}, u32[]{:S(2)}) collective-permute-start(f32[144,128]{1,0:T(8,128)S(1)} %get-tuple-element.25), channel_id=1, source_target_pairs={{0,8},{1,2},{2,1},{3,4},{4,3},{5,6},{6,5},{7,15},{8,0},{9,10},{10,... | collective-permute-start | bytes 221192 | tf_op jit(solution)/shard_map/ppermute | solution.py:698
  10.6 0.0 collective-permute-done.2.refs_4_
  10.6 2.3 %collective-permute-done.3.refs_5_ = f32[144,128]{1,0:T(8,128)S(1)} collective-permute-done((f32[144,128]{1,0:T(8,128)S(1)}, f32[144,128]{1,0:T(8,128)S(1)}, u32[]{:S(2)}, u32[]{:S(2)}) %collective-permute-start.3) | collective-permute-done | bytes 73760 | tf_op jit(solution)/shard_map/ppermute | solution.py:698
  13.0 0.0 copy-done.3
  13.0 0.0 copy-done.5
  13.0 0.0 copy-done.6
  13.0 1.3 %down_kernel.1 = (f32[144,384]{1,0:T(8,128)S(1)}, f32[144,384]{1,0:T(8,128)S(1)}, f32[144,384]{1,0:T(8,128)S(1)}, f32[144,384]{1,0:T(8,128)S(1)}, f32[96,256]{1,...) custom-call(f32[128,256]{1,0:T(8,128)S(1)} %copy-done, ...), custom_call_target="tpu_custom_call" | custom-call | tf_op jit(solution)/shard_map/down_kernel/pallas_call | solution.py:675
  14.3 0.0 copy-start.2
  14.3 0.0 copy-start.9
  14.4 16.7 %all_to_all.22 = f32[16,32,128]{2,1,0:T(8,128)S(1)} all-to-all(f32[16,32,128]{2,1,0:T(8,128)S(1)} %bitcast.14), channel_id=1, replica_groups={{0,2,4,6,8,10,12,14,16,18,20,22,24,26,28,30},{1,3,5,7,9,11,13,15,17,19,..., dimensions={0} | all-to-all | bytes 524288 | tf_op jit(solution)/shard_map/all_to_all | solution.py:708
  31.1 0.0 collective-permute-start.4
  31.1 1.5 %collective-permute-done.4.refs_1_ = f32[512,128]{1,0:T(8,128)S(1)} collective-permute-done((f32[512,128]{1,0:T(8,128)S(1)}, f32[512,128]{1,0:T(8,128)S(1)}, u32[]{:S(2)}, u32[]{:S(2)}) %collective-permute-start.4) | collective-permute-done | bytes 262176 | tf_op jit(solution)/shard_map/ppermute | solution.py:709
  32.6 0.0 copy-done.2
  32.6 0.0 copy-done.9
  32.7 4.3 %middle_kernel.1 = (f32[2,2,48,128]{3,2,1,0:T(8,128)S(1)}, f32[1,1,48,128]{3,2,1,0:T(8,128)S(1)}, f32[2,2,48,128]{3,2,1,0:T(8,128)S(1)}, f32[1,1,48,128]{3,2,1,0...) custom-call(f32[512,128]{1,0:T(8,128)S(1)} %bitcast.13, ...), custom_call_target="tpu_custom_call" | custom-call | tf_op jit(solution)/shard_map/middle_kernel/pallas_call | solution.py:675
  37.0 9.7 %all_to_all.23 = f32[32,4,128]{2,1,0:T(4,128)S(1)} all-to-all(f32[32,4,128]{2,1,0:T(4,128)S(1)} %bitcast.16), channel_id=1, replica_groups=mesh['gx'=4,'gy'=8] {'gx','gy'}, dimensions={0} | all-to-all | bytes 131072 | tf_op jit(solution)/shard_map/all_to_all | solution.py:702
  46.7 0.0 copy-done.4
  46.7 0.0 copy-done.7
  46.7 2.6 %up_kernel.1 = (f32[128,256]{1,0:T(8,128)}, f32[128,256]{1,0:T(8,128)}) custom-call(f32[128,128]{1,0:T(8,128)S(1)} %bitcast.15, f32[2,2,48,128]{3,2,1,0:T(8,128)S(1)} %get-tuple-element.34.refs_1_, f32[1,1,48,128]{3,2,1,0:T(8,128)S(1)} %get-tuple-element.35.refs_2_, f32[2,2,48,128]{3,2,1,0:T(8,128)S(1)} %get-tuple-element.36.refs_3_, ...), custom_call_target="tpu_custom_call" | custom-call | tf_op jit(solution)/shard_map/up_kernel/pallas_call | solution.py:675
  (7 shorter events, 0.0 us)
Async XLA Ops:
  1.5 5.6 %copy-start = (f32[128,256]{1,0:T(8,128)S(1)}, f32[128,256]{1,0:T(8,128)}, u32[]{:S(2)}) copy-start(f32[128,256]{1,0:T(8,128)} %refs_0_.3) | copy-start | bytes 393220
  1.5 5.6 %copy-start.1 = (f32[128,256]{1,0:T(8,128)S(1)}, f32[128,256]{1,0:T(8,128)}, u32[]{:S(2)}) copy-start(f32[128,256]{1,0:T(8,128)} %refs_1_.3) | copy-start | bytes 393220
  1.5 5.6 %collective-permute-start = (f32[2,40,256]{2,1,0:T(8,128)S(1)}, f32[2,40,256]{2,1,0:T(8,128)S(1)}, u32[]{:S(2)}, u32[]{:S(2)}) collective-permute-start(f32[2,40,256]{2,1,0:T(8,128)S(1)} %pad_maximum_fusion), channel_id=1, source_target_pairs={{0,8},{8,0},{16,24},{24,16},{1,9},{9,1},{17,25},{25,17},{2,10},{10... | collective-permute-start | bytes 245768 | tf_op jit(solution)/shard_map/ppermute | solution.py:698
  4.7 8.3 %copy-start.3 = (bf16[256,128]{1,0:T(8,128)(2,1)S(1)}, bf16[256,128]{1,0:T(8,128)(2,1)}, u32[]{:S(2)}) copy-start(bf16[256,128]{1,0:T(8,128)(2,1)} %constant.41.clone.refs_7_.refs_9_) | copy-start | bytes 196612
  4.7 8.3 %copy-start.5 = (bf16[384,256]{1,0:T(8,128)(2,1)S(1)}, bf16[384,256]{1,0:T(8,128)(2,1)}, u32[]{:S(2)}) copy-start(bf16[384,256]{1,0:T(8,128)(2,1)} %constant.40.clone.refs_6_) | copy-start | bytes 589828
  4.7 8.3 %copy-start.6 = (bf16[512,128]{1,0:T(8,128)(2,1)S(1)}, bf16[512,128]{1,0:T(8,128)(2,1)}, u32[]{:S(2)}) copy-start(bf16[512,128]{1,0:T(8,128)(2,1)} %constant.42.clone.refs_8_) | copy-start | bytes 393220
  4.7 2.4 %collective-permute-start.1 = (f32[2,40,256]{2,1,0:T(8,128)S(1)}, f32[2,40,256]{2,1,0:T(8,128)S(1)}, u32[]{:S(2)}, u32[]{:S(2)}) collective-permute-start(f32[2,40,256]{2,1,0:T(8,128)S(1)} %pad_maximum_fusion.1), channel_id=1, source_target_pairs={{0,1},{1,0},{2,3},{3,2},{4,5},{5,4},{6,7},{7,6},{8,16},{9,17},{10,... | collective-permute-start | bytes 245768 | tf_op jit(solution)/shard_map/ppermute | solution.py:698
  7.3 3.4 %collective-permute-start.2 = (f32[144,128]{1,0:T(8,128)S(1)}, f32[144,128]{1,0:T(8,128)S(1)}, u32[]{:S(2)}, u32[]{:S(2)}) collective-permute-start(f32[144,128]{1,0:T(8,128)S(1)} %get-tuple-element.24), channel_id=1, source_target_pairs={{0,1},{1,0},{2,3},{3,2},{4,5},{5,4},{6,7},{7,6},{8,9},{9,8},{10,11... | collective-permute-start | bytes 221192 | tf_op jit(solution)/shard_map/ppermute | solution.py:698
  7.3 5.6 %collective-permute-start.3 = (f32[144,128]{1,0:T(8,128)S(1)}, f32[144,128]{1,0:T(8,128)S(1)}, u32[]{:S(2)}, u32[]{:S(2)}) collective-permute-start(f32[144,128]{1,0:T(8,128)S(1)} %get-tuple-element.25), channel_id=1, source_target_pairs={{0,8},{1,2},{2,1},{3,4},{4,3},{5,6},{6,5},{7,15},{8,0},{9,10},{10,... | collective-permute-start | bytes 221192 | tf_op jit(solution)/shard_map/ppermute | solution.py:698
  14.3 18.3 %copy-start.2 = (bf16[512,256]{1,0:T(8,128)(2,1)S(1)}, bf16[512,256]{1,0:T(8,128)(2,1)}, u32[]{:S(2)}) copy-start(bf16[512,256]{1,0:T(8,128)(2,1)} %constant.43.clone.refs_8_) | copy-start | bytes 786436
  14.3 18.3 %copy-start.9 = (bf16[128,128]{1,0:T(8,128)(2,1)S(1)}, bf16[128,128]{1,0:T(8,128)(2,1)}, u32[]{:S(2)}) copy-start(bf16[128,128]{1,0:T(8,128)(2,1)} %constant.44.clone.refs_10_) | copy-start | bytes 98308
  31.1 1.5 %collective-permute-start.4 = (f32[512,128]{1,0:T(8,128)S(1)}, f32[512,128]{1,0:T(8,128)S(1)}, u32[]{:S(2)}, u32[]{:S(2)}) collective-permute-start(f32[512,128]{1,0:T(8,128)S(1)} %bitcast.12), channel_id=1, source_target_pairs={{0,1},{1,0},{2,3},{3,2},{4,5},{5,4},{6,7},{7,6},{8,9},{9,8},{10,11... | collective-permute-start | bytes 786440 | tf_op jit(solution)/shard_map/ppermute | solution.py:709
  32.6 14.1 %copy-start.4 = (bf16[256,384]{1,0:T(8,128)(2,1)S(1)}, bf16[256,384]{1,0:T(8,128)(2,1)}, u32[]{:S(2)}) copy-start(bf16[256,384]{1,0:T(8,128)(2,1)} %constant.47.clone.refs_18_) | copy-start | bytes 589828
  36.9 9.8 %copy-start.7 = (bf16[128,256]{1,0:T(8,128)(2,1)S(1)}, bf16[128,256]{1,0:T(8,128)(2,1)}, u32[]{:S(2)}) copy-start(bf16[128,256]{1,0:T(8,128)(2,1)} %constant.46.clone.refs_17_) | copy-start | bytes 196612
  37.0 9.8 %copy-start.8 = (bf16[256,128]{1,0:T(8,128)(2,1)S(1)}, bf16[256,128]{1,0:T(8,128)(2,1)}, u32[]{:S(2)}) copy-start(bf16[256,128]{1,0:T(8,128)(2,1)} %constant.45.clone.refs_16_) | copy-start | bytes 196612

commit v10 on v9

--- a/solution.py
+++ b/solution.py
@@ -624,7 +624,7 @@
     m.vcycle(2, False, unit)
     g, d, w = c1_ref[...], d1_ref[...], w1_ref[...]
     v = v1_ref[...] + jnp.where(w > 0.0, m.spread(gx, gy, sc_ref, scratch, lines), 0.0)
-    for turn in range(4):
+    for _ in range(4):
         v = sweep(v, g, w)
     e1_ref[...] = v
     r = g - d * v + around(v)
@@ -648,16 +648,16 @@
     m.vcycle(3, True, m.unit(False))
     g, w = c2_ref[...], w2_ref[...]
     v = e2_ref[...] + jnp.where(w > 0.0, m.spread(gx, gy, sc_ref, scratch, lines), 0.0)
-    for turn in range(2):
+    for _ in range(2):
         v = sweep(v, g, w)
     own = sizes.rows // 2
     g, w = near(c1_ref, own), near(w1_ref, own)
     v = near(e1_ref, own) + near(double_rows(scratch, f32dot_right(v, pc1_ref[...])), own)
-    for turn in range(2):
+    for _ in range(2):
         v = sweep(v, g, w)
     g, d, w = g0_ref[...], d0_ref[...], w0_ref[...]
     v = v0_ref[...] + near(double_rows(scratch, f32dot_right(v, pc0_ref[...])), sizes.rows)
-    for turn in range(2):
+    for _ in range(2):
         v = sweep(v, g, w)
     r = g - d * v + around(v)
     solution_ref[...] = v[: sizes.rows, : sizes.columns]
@@ -674,7 +674,6 @@
     used += sum(x.size * x.dtype.itemsize for x in operands)
     return pl.pallas_call(
         lambda *refs: kernel(sizes, *refs),
-        name=kernel.__name__,
         out_shape=shapes,
         in_specs=vmem(len(operands)),
         out_specs=vmem(len(outs)),
@@ -695,7 +694,8 @@
         return place * ny + gy if axis == "gx" else gx * ny + place
 
     pairs = [(gx * ny + gy, target(gx, gy)) for gx in range(nx) for gy in range(ny)]
-    return lax.ppermute(first, axis, [(i, i ^ 1) for i in range(count)]), lax.ppermute(second, ("gx", "gy"), pairs)
+    other = lax.ppermute(second, ("gx", "gy"), pairs)
+    return lax.ppermute(first, axis, [(i, i ^ 1) for i in range(count)]), other
 
 
 def gather(copies):
@@ -716,10 +716,13 @@
     even = lax.axis_index("gx") % 2 == 0
     last = rows - HALO
 
-    def strips(start):
-        return jnp.stack([lax.dynamic_slice(x, (start, 0), (HALO, columns)) for x in (right_side, shift)])
-
-    rows_a, rows_b = swaps(strips(jnp.where(even, last, 0)), strips(jnp.where(even, 0, last)), "gx", "gy")
+    def strips(start, fields):
+        return jnp.stack([lax.dynamic_slice(x, (start, 0), (HALO, columns)) for x in fields])
+
+    fields = (right_side, shift)
+    later = lax.optimization_barrier(fields)
+    rows_a, rows_b = swaps(
+        strips(jnp.where(even, last, 0), later), strips(jnp.where(even, 0, last), fields), "gx", "gy")
     ext = [(z.ext_rows[l], z.ext_columns[l]) for l in range(3)]
     strip = (strip_rows(z)[1], 128)
     first, second = call(strip_kernel, z, [strip] * 2, [], right_side, shift, rows_a, rows_b)

time: 49.6 us -> 49.4 us (level)
  blocking collectives: 26.5 us -> 25.9 us
    ppermute x2, starting transfers between devices: 3.19 us -> 4.27 us  [swaps(): lax.ppermute(first, axis, [(i, i ^ 1) for i in range(count)])]
    ppermute x2, starting transfers between devices: 3.36 us -> 2.64 us  [swaps(): other = lax.ppermute(second, ('gx', 'gy'), pairs)]
    all_to_all x1, blocking collectives: 16.7 us -> 16.2 us  [gather_by_core(): lax.all_to_all(copies, ('gx', 'gy'), 0, 0, tiled=True, axis_index_groups=...]
where the time goes in v10:
time: 49.4 us; the launch traced here: 49.2 us
  blocking collectives  25.9 us (52%)
  Pallas kernels  8.4 us (17%)
  starting transfers between devices  6.92 us (14%)
  waiting for transfers between devices  6.28 us (13%)
  local copies, waits for them, and re-layouts  0.91 us (2%)
  between operations  0.75 us (2%)
    all_to_all x1, blocking collectives, gather_by_core(): lax.all_to_all(copies, ('gx', 'gy'), 0, 0, tiled=True, axis_index_groups=...  16.2 us
    all_to_all x1, blocking collectives, gather(): return lax.all_to_all(copies, ('gx', 'gy'), 0, 0, tiled=True)  9.74 us
    pallas_call x4, Pallas kernels, call(): pl.pallas_call(lambda *refs: kernel(sizes, *refs), out_shape=shapes, in_s...  8.4 us
    ppermute x2, starting transfers between devices, swaps(): lax.ppermute(first, axis, [(i, i ^ 1) for i in range(count)])  4.27 us
    ppermute x2, starting transfers between devices, swaps(): other = lax.ppermute(second, ('gx', 'gy'), pairs)  2.64 us
    ppermute x2, waiting for transfers between devices, swaps(): lax.ppermute(first, axis, [(i, i ^ 1) for i in range(count)])  2.42 us
    ppermute x2, waiting for transfers between devices, swaps(): other = lax.ppermute(second, ('gx', 'gy'), pairs)  2.33 us
    ppermute x1, waiting for transfers between devices, gather_by_core(): return (own, lax.ppermute(own, 'gy', [(j, j ^ 1) for j in range(ny)]))  1.53 us
  transfers between devices with their start and end apart: 5, of which 3 were waited for; matrix products, arithmetic and copies ran while one was open for 0% of the time, Pallas kernels for 0%

profile of v10, /device:TPU:0, one launch (start us, length us, event | category | flops | bytes accessed | tf_op | source)
XLA Modules:
  0.0 49.2 jit_solution(15921425882476069468)
XLA Ops:
  0.6 0.0 copy-start
  0.7 0.0 copy-start.1
  0.7 0.9 %dynamic-slice_bitcast_fusion = (f32[1,40,256]{2,1,0:T(8,128)S(1)}, f32[1,40,256]{2,1,0:T(8,128)S(1)}) fusion(f32[128,256]{1,0:T(8,128)} %refs_1_.3, s32[]{:T(128)S(6)} %select_n.20, f32[128,256]{1,0:T(8,128)} %refs_0_.3), kind=kLoop, calls=%fused_computation.2 | loop fusion | bytes 163844 | tf_op jit(solution)/shard_map/stack | solution.py:720
  1.5 0.6 %collective-permute-start.1 = (f32[2,40,256]{2,1,0:T(8,128)S(1)}, f32[2,40,256]{2,1,0:T(8,128)S(1)}, u32[]{:S(2)}, u32[]{:S(2)}) collective-permute-start(f32[2,40,256]{2,1,0:T(8,128)S(1)} %pad_maximum_fusion.1), channel_id=1, source_target_pairs={{0,1},{1,0},{2,3},{3,2},{4,5},{5,4},{6,7},{7,6},{8,16},{9,17},{10,... | collective-permute-start | bytes 245768 | tf_op jit(solution)/shard_map/ppermute | solution.py:697
  2.1 0.0 copy-done
  2.1 0.0 copy-done.1
  2.1 0.0 copy-start.3
  2.1 0.0 copy-start.5
  2.1 0.0 copy-start.6
  2.2 4.2 %collective-permute-start = (f32[2,40,256]{2,1,0:T(8,128)S(1)}, f32[2,40,256]{2,1,0:T(8,128)S(1)}, u32[]{:S(2)}, u32[]{:S(2)}) collective-permute-start(f32[2,40,256]{2,1,0:T(8,128)S(1)} %pad_maximum_fusion), channel_id=1, source_target_pairs={{0,8},{8,0},{16,24},{24,16},{1,9},{9,1},{17,25},{25,17},{2,10},{10... | collective-permute-start | bytes 245768 | tf_op jit(solution)/shard_map/ppermute | solution.py:698
  6.4 0.0 collective-permute-done.1.refs_3_
  6.4 2.4 %collective-permute-done.refs_2_ = f32[2,40,256]{2,1,0:T(8,128)S(1)} collective-permute-done((f32[2,40,256]{2,1,0:T(8,128)S(1)}, f32[2,40,256]{2,1,0:T(8,128)S(1)}, u32[]{:S(2)}, u32[]{:S(2)}) %collective-permute-start) | collective-permute-done | bytes 81952 | tf_op jit(solution)/shard_map/ppermute | solution.py:698
  8.8 0.1 shard_map.113
  8.9 0.1 collective-permute-start.2
  9.0 2.1 %collective-permute-start.3 = (f32[144,128]{1,0:T(8,128)S(1)}, f32[144,128]{1,0:T(8,128)S(1)}, u32[]{:S(2)}, u32[]{:S(2)}) collective-permute-start(f32[144,128]{1,0:T(8,128)S(1)} %get-tuple-element.29), channel_id=1, source_target_pairs={{0,8},{1,2},{2,1},{3,4},{4,3},{5,6},{6,5},{7,15},{8,0},{9,10},{10,... | collective-permute-start | bytes 221192 | tf_op jit(solution)/shard_map/ppermute | solution.py:697
  11.1 0.0 collective-permute-done.2.refs_4_
  11.1 2.3 %collective-permute-done.3.refs_5_ = f32[144,128]{1,0:T(8,128)S(1)} collective-permute-done((f32[144,128]{1,0:T(8,128)S(1)}, f32[144,128]{1,0:T(8,128)S(1)}, u32[]{:S(2)}, u32[]{:S(2)}) %collective-permute-start.3) | collective-permute-done | bytes 73760 | tf_op jit(solution)/shard_map/ppermute | solution.py:697
  13.4 0.0 copy-done.3
  13.4 0.0 copy-done.5
  13.4 0.0 copy-done.6
  13.4 1.4 %shard_map.114 = (f32[144,384]{1,0:T(8,128)S(1)}, f32[144,384]{1,0:T(8,128)S(1)}, f32[144,384]{1,0:T(8,128)S(1)}, f32[144,384]{1,0:T(8,128)S(1)}, f32[96,256]{1,...) custom-call(f32[128,256]{1,0:T(8,128)S(1)} %copy-done, ...), custom_call_target="tpu_custom_call" | custom-call | tf_op jit(solution)/shard_map/pallas_call | solution.py:675
  14.8 0.0 copy-start.2
  14.8 0.0 copy-start.9
  14.8 16.2 %all_to_all.22 = f32[16,32,128]{2,1,0:T(8,128)S(1)} all-to-all(f32[16,32,128]{2,1,0:T(8,128)S(1)} %bitcast.14), channel_id=1, replica_groups={{0,2,4,6,8,10,12,14,16,18,20,22,24,26,28,30},{1,3,5,7,9,11,13,15,17,19,..., dimensions={0} | all-to-all | bytes 524288 | tf_op jit(solution)/shard_map/all_to_all | solution.py:708
  31.0 0.0 collective-permute-start.4
  31.0 1.5 %collective-permute-done.4.refs_1_ = f32[512,128]{1,0:T(8,128)S(1)} collective-permute-done((f32[512,128]{1,0:T(8,128)S(1)}, f32[512,128]{1,0:T(8,128)S(1)}, u32[]{:S(2)}, u32[]{:S(2)}) %collective-permute-start.4) | collective-permute-done | bytes 262176 | tf_op jit(solution)/shard_map/ppermute | solution.py:709
  32.5 0.0 copy-done.2
  32.5 0.0 copy-done.9
  32.5 4.3 %shard_map.115 = (f32[2,2,48,128]{3,2,1,0:T(8,128)S(1)}, f32[1,1,48,128]{3,2,1,0:T(8,128)S(1)}, f32[2,2,48,128]{3,2,1,0:T(8,128)S(1)}, f32[1,1,48,128]{3,2,1,0:T...) custom-call(f32[512,128]{1,0:T(8,128)S(1)} %bitcast.13, ...), custom_call_target="tpu_custom_call" | custom-call | tf_op jit(solution)/shard_map/pallas_call | solution.py:675
  36.8 9.7 %all_to_all.23 = f32[32,4,128]{2,1,0:T(4,128)S(1)} all-to-all(f32[32,4,128]{2,1,0:T(4,128)S(1)} %bitcast.16), channel_id=1, replica_groups=mesh['gx'=4,'gy'=8] {'gx','gy'}, dimensions={0} | all-to-all | bytes 131072 | tf_op jit(solution)/shard_map/all_to_all | solution.py:702
  46.6 0.0 copy-done.7
  46.6 2.6 %shard_map.116 = (f32[128,256]{1,0:T(8,128)}, f32[128,256]{1,0:T(8,128)}) custom-call(f32[128,128]{1,0:T(8,128)S(1)} %bitcast.15, f32[2,2,48,128]{3,2,1,0:T(8,128)S(1)} %get-tuple-element.38.refs_1_, f32[1,1,48,128]{3,2,1,0:T(8,128)S(1)} %get-tuple-element.39.refs_2_, f32[2,2,48,128]{3,2,1,0:T(8,128)S(1)} %get-tuple-element.40.refs_3_, ...), custom_call_target="tpu_custom_call" | custom-call | tf_op jit(solution)/shard_map/pallas_call | solution.py:675
  (8 shorter events, 0.0 us)
Async XLA Ops:
  0.6 1.4 %copy-start = (f32[128,256]{1,0:T(8,128)S(1)}, f32[128,256]{1,0:T(8,128)}, u32[]{:S(2)}) copy-start(f32[128,256]{1,0:T(8,128)} %refs_0_.3) | copy-start | bytes 393220
  0.7 1.4 %copy-start.1 = (f32[128,256]{1,0:T(8,128)S(1)}, f32[128,256]{1,0:T(8,128)}, u32[]{:S(2)}) copy-start(f32[128,256]{1,0:T(8,128)} %refs_1_.3) | copy-start | bytes 393220
  1.5 4.8 %collective-permute-start.1 = (f32[2,40,256]{2,1,0:T(8,128)S(1)}, f32[2,40,256]{2,1,0:T(8,128)S(1)}, u32[]{:S(2)}, u32[]{:S(2)}) collective-permute-start(f32[2,40,256]{2,1,0:T(8,128)S(1)} %pad_maximum_fusion.1), channel_id=1, source_target_pairs={{0,1},{1,0},{2,3},{3,2},{4,5},{5,4},{6,7},{7,6},{8,16},{9,17},{10,... | collective-permute-start | bytes 245768 | tf_op jit(solution)/shard_map/ppermute | solution.py:697
  2.1 11.3 %copy-start.3 = (bf16[256,128]{1,0:T(8,128)(2,1)S(1)}, bf16[256,128]{1,0:T(8,128)(2,1)}, u32[]{:S(2)}) copy-start(bf16[256,128]{1,0:T(8,128)(2,1)} %constant.41.clone.refs_7_.refs_9_) | copy-start | bytes 196612
  2.1 11.3 %copy-start.5 = (bf16[384,256]{1,0:T(8,128)(2,1)S(1)}, bf16[384,256]{1,0:T(8,128)(2,1)}, u32[]{:S(2)}) copy-start(bf16[384,256]{1,0:T(8,128)(2,1)} %constant.40.clone.refs_6_) | copy-start | bytes 589828
  2.1 11.3 %copy-start.6 = (bf16[512,128]{1,0:T(8,128)(2,1)S(1)}, bf16[512,128]{1,0:T(8,128)(2,1)}, u32[]{:S(2)}) copy-start(bf16[512,128]{1,0:T(8,128)(2,1)} %constant.42.clone.refs_8_) | copy-start | bytes 393220
  2.2 6.6 %collective-permute-start = (f32[2,40,256]{2,1,0:T(8,128)S(1)}, f32[2,40,256]{2,1,0:T(8,128)S(1)}, u32[]{:S(2)}, u32[]{:S(2)}) collective-permute-start(f32[2,40,256]{2,1,0:T(8,128)S(1)} %pad_maximum_fusion), channel_id=1, source_target_pairs={{0,8},{8,0},{16,24},{24,16},{1,9},{9,1},{17,25},{25,17},{2,10},{10... | collective-permute-start | bytes 245768 | tf_op jit(solution)/shard_map/ppermute | solution.py:698
  8.9 2.2 %collective-permute-start.2 = (f32[144,128]{1,0:T(8,128)S(1)}, f32[144,128]{1,0:T(8,128)S(1)}, u32[]{:S(2)}, u32[]{:S(2)}) collective-permute-start(f32[144,128]{1,0:T(8,128)S(1)} %get-tuple-element.28), channel_id=1, source_target_pairs={{0,1},{1,0},{2,3},{3,2},{4,5},{5,4},{6,7},{7,6},{8,9},{9,8},{10,11... | collective-permute-start | bytes 221192 | tf_op jit(solution)/shard_map/ppermute | solution.py:698
  9.0 4.4 %collective-permute-start.3 = (f32[144,128]{1,0:T(8,128)S(1)}, f32[144,128]{1,0:T(8,128)S(1)}, u32[]{:S(2)}, u32[]{:S(2)}) collective-permute-start(f32[144,128]{1,0:T(8,128)S(1)} %get-tuple-element.29), channel_id=1, source_target_pairs={{0,8},{1,2},{2,1},{3,4},{4,3},{5,6},{6,5},{7,15},{8,0},{9,10},{10,... | collective-permute-start | bytes 221192 | tf_op jit(solution)/shard_map/ppermute | solution.py:697
  14.8 17.7 %copy-start.2 = (bf16[512,256]{1,0:T(8,128)(2,1)S(1)}, bf16[512,256]{1,0:T(8,128)(2,1)}, u32[]{:S(2)}) copy-start(bf16[512,256]{1,0:T(8,128)(2,1)} %constant.43.clone.refs_8_) | copy-start | bytes 786436
  14.8 17.7 %copy-start.9 = (bf16[128,128]{1,0:T(8,128)(2,1)S(1)}, bf16[128,128]{1,0:T(8,128)(2,1)}, u32[]{:S(2)}) copy-start(bf16[128,128]{1,0:T(8,128)(2,1)} %constant.44.clone.refs_10_) | copy-start | bytes 98308
  31.0 1.5 %collective-permute-start.4 = (f32[512,128]{1,0:T(8,128)S(1)}, f32[512,128]{1,0:T(8,128)S(1)}, u32[]{:S(2)}, u32[]{:S(2)}) collective-permute-start(f32[512,128]{1,0:T(8,128)S(1)} %bitcast.12), channel_id=1, source_target_pairs={{0,1},{1,0},{2,3},{3,2},{4,5},{5,4},{6,7},{7,6},{8,9},{9,8},{10,11... | collective-permute-start | bytes 786440 | tf_op jit(solution)/shard_map/ppermute | solution.py:709
  32.5 14.1 %copy-start.4 = (bf16[256,384]{1,0:T(8,128)(2,1)S(1)}, bf16[256,384]{1,0:T(8,128)(2,1)}, u32[]{:S(2)}) copy-start(bf16[256,384]{1,0:T(8,128)(2,1)} %constant.47.clone.refs_18_) | copy-start | bytes 589828
  36.8 9.8 %copy-start.7 = (bf16[128,256]{1,0:T(8,128)(2,1)S(1)}, bf16[128,256]{1,0:T(8,128)(2,1)}, u32[]{:S(2)}) copy-start(bf16[128,256]{1,0:T(8,128)(2,1)} %constant.46.clone.refs_17_) | copy-start | bytes 196612
  36.8 9.8 %copy-start.8 = (bf16[256,128]{1,0:T(8,128)(2,1)S(1)}, bf16[256,128]{1,0:T(8,128)(2,1)}, u32[]{:S(2)}) copy-start(bf16[256,128]{1,0:T(8,128)(2,1)} %constant.45.clone.refs_16_) | copy-start | bytes 196612

commit v11 on v10

--- a/solution.py
+++ b/solution.py
@@ -25,6 +25,14 @@
     return (out[2 * rows :] + out[rows : 2 * rows]) + out[:rows]
 
 
+def restrict_right(values, onehot):
+    high = values.astype(jnp.bfloat16)
+    middle = (values - high.astype(jnp.float32)).astype(jnp.bfloat16)
+    rows = values.shape[0]
+    out = jnp.dot(jnp.concatenate([high, middle], axis=0), onehot, preferred_element_type=jnp.float32)
+    return out[rows:] + out[:rows]
+
+
 def around(v):
     rows, columns = v.shape
     up = pltpu.roll(v, 1, 0)
@@ -129,14 +137,14 @@
 
 def pack_two(sizes, gy, first, second, scratch, columns_ref, out_ref):
     rows = first.shape[0]
-    scratch[0, :rows, :] = f32dot_right(jnp.concatenate([first, second], axis=1), columns_ref[...])
+    scratch[0, :rows, :] = restrict_right(jnp.concatenate([first, second], axis=1), columns_ref[...])
     block = jnp.concatenate([scratch[0, pl.ds(s, sizes.p, stride=4), :] for s in range(4)], axis=0)
     repeat(pltpu.roll(block, lax.rem(gy, 8) * sizes.q, 1), out_ref)
 
 
 def pack_one(sizes, gy, values, scratch, columns_ref, out_ref):
     rows = values.shape[0]
-    scratch[0, :rows, :] = f32dot_right(values, columns_ref[...])
+    scratch[0, :rows, :] = restrict_right(values, columns_ref[...])
     part = iota((4, 128), 1) // (2 * sizes.q)
     block = scratch[0, pl.ds(0, 4, stride=2), :]
     for k in range(1, 4):
@@ -222,7 +230,7 @@
     for values in (r, sigma):
         pairs = pair_rows(scratch, values)
         both += [pairs[: own + halo], pairs[pairs.shape[0] - halo :]]
-    both = f32dot_right(jnp.concatenate(both, axis=0), rc0_ref[...])
+    both = restrict_right(jnp.concatenate(both, axis=0), rc0_ref[...])
     half = own + 2 * halo
     g, sigma = both[:half], both[half:]
     d, w = coefficients(sizes, 1, gx, gy, sigma)
@@ -236,7 +244,7 @@
     own = sizes.rows // 4
     source, sigma = pair_rows(scratch, r), pair_rows(scratch, sigma)
     pack_two(sizes, gy, source[:own], sigma[:own], scratch, pc_ref, out_ref)
-    d, w = coefficients(sizes, 2, gx, gy, f32dot_right(sigma, rc1_ref[...]))
+    d, w = coefficients(sizes, 2, gx, gy, restrict_right(sigma, rc1_ref[...]))
     d2_ref[...] = d
     w2_ref[...] = w
 
@@ -628,7 +636,7 @@
         v = sweep(v, g, w)
     e1_ref[...] = v
     r = g - d * v + around(v)
-    g = f32dot_right(pair_rows(scratch, r), rc1_ref[...])
+    g = restrict_right(pair_rows(scratch, r), rc1_ref[...])
     d, w = d2l_ref[...], w2l_ref[...]
     v = w * g
     v = sweep(v, g, w)
@@ -722,7 +730,7 @@
     fields = (right_side, shift)
     later = lax.optimization_barrier(fields)
     rows_a, rows_b = swaps(
-        strips(jnp.where(even, last, 0), later), strips(jnp.where(even, 0, last), fields), "gx", "gy")
+        strips(jnp.where(even, last, 0), fields), strips(jnp.where(even, 0, last), later), "gx", "gy")
     ext = [(z.ext_rows[l], z.ext_columns[l]) for l in range(3)]
     strip = (strip_rows(z)[1], 128)
     first, second = call(strip_kernel, z, [strip] * 2, [], right_side, shift, rows_a, rows_b)

time: 49.4 us -> 49.4 us (level)
  blocking collectives: 25.9 us -> 26.5 us
    ppermute x2, starting transfers between devices: 4.27 us -> 3.19 us  [swaps(): lax.ppermute(first, axis, [(i, i ^ 1) for i in range(count)])]
    ppermute x2, starting transfers between devices: 2.64 us -> 3.4 us  [swaps(): other = lax.ppermute(second, ('gx', 'gy'), pairs)]
    all_to_all x1, blocking collectives: 16.2 us -> 16.7 us  [gather_by_core(): lax.all_to_all(copies, ('gx', 'gy'), 0, 0, tiled=True, axis_index_groups=...]
where the time goes in v11:
time: 49.4 us; the launch traced here: 49.2 us
  blocking collectives  26.5 us (54%)
  Pallas kernels  8.29 us (17%)
  starting transfers between devices  6.59 us (13%)
  waiting for transfers between devices  6.16 us (12%)
  local copies, waits for them, and re-layouts  0.91 us (2%)
  between operations  0.76 us (2%)
    all_to_all x1, blocking collectives, gather_by_core(): lax.all_to_all(copies, ('gx', 'gy'), 0, 0, tiled=True, axis_index_groups=...  16.7 us
    all_to_all x1, blocking collectives, gather(): return lax.all_to_all(copies, ('gx', 'gy'), 0, 0, tiled=True)  9.74 us
    pallas_call x4, Pallas kernels, call(): pl.pallas_call(lambda *refs: kernel(sizes, *refs), out_shape=shapes, in_s...  8.29 us
    ppermute x2, starting transfers between devices, swaps(): other = lax.ppermute(second, ('gx', 'gy'), pairs)  3.4 us
    ppermute x2, starting transfers between devices, swaps(): lax.ppermute(first, axis, [(i, i ^ 1) for i in range(count)])  3.19 us
    ppermute x2, waiting for transfers between devices, swaps(): other = lax.ppermute(second, ('gx', 'gy'), pairs)  2.33 us
    ppermute x2, waiting for transfers between devices, swaps(): lax.ppermute(first, axis, [(i, i ^ 1) for i in range(count)])  2.3 us
    ppermute x1, waiting for transfers between devices, gather_by_core(): return (own, lax.ppermute(own, 'gy', [(j, j ^ 1) for j in range(ny)]))  1.53 us
  transfers between devices with their start and end apart: 5, of which 3 were waited for; matrix products, arithmetic and copies ran while one was open for 0% of the time, Pallas kernels for 0%

profile of v11, /device:TPU:0, one launch (start us, length us, event | category | flops | bytes accessed | tf_op | source)
XLA Modules:
  0.0 49.2 jit_solution(15981710777832492987)
XLA Ops:
  0.6 0.0 copy-start
  0.7 0.0 copy-start.1
  0.7 0.9 %dynamic-slice_bitcast_fusion.2 = (f32[1,40,256]{2,1,0:T(8,128)S(1)}, f32[1,40,256]{2,1,0:T(8,128)S(1)}) fusion(f32[128,256]{1,0:T(8,128)} %refs_1_.3, s32[]{:T(128)S(6)} %select_n.19, f32[128,256]{1,0:T(8,128)} %refs_0_.3), kind=kLoop, calls=%fused_computation.4 | loop fusion | bytes 163844 | tf_op jit(solution)/shard_map/stack | solution.py:728
  1.5 3.1 %collective-permute-start = (f32[2,40,256]{2,1,0:T(8,128)S(1)}, f32[2,40,256]{2,1,0:T(8,128)S(1)}, u32[]{:S(2)}, u32[]{:S(2)}) collective-permute-start(f32[2,40,256]{2,1,0:T(8,128)S(1)} %pad_maximum_fusion), channel_id=1, source_target_pairs={{0,8},{8,0},{16,24},{24,16},{1,9},{9,1},{17,25},{25,17},{2,10},{10... | collective-permute-start | bytes 245768 | tf_op jit(solution)/shard_map/ppermute | solution.py:706
  4.6 0.0 copy-done
  4.6 0.0 copy-done.1
  4.7 0.0 copy-start.3
  4.7 0.0 copy-start.5
  4.7 0.0 copy-start.6
  4.7 0.1 collective-permute-start.1
  4.8 2.3 %collective-permute-done.refs_2_ = f32[2,40,256]{2,1,0:T(8,128)S(1)} collective-permute-done((f32[2,40,256]{2,1,0:T(8,128)S(1)}, f32[2,40,256]{2,1,0:T(8,128)S(1)}, u32[]{:S(2)}, u32[]{:S(2)}) %collective-permute-start) | collective-permute-done | bytes 81952 | tf_op jit(solution)/shard_map/ppermute | solution.py:706
  7.1 0.0 collective-permute-done.1.refs_3_
  7.1 0.1 shard_map.113
  7.2 0.1 collective-permute-start.2
  7.3 3.3 %collective-permute-start.3 = (f32[144,128]{1,0:T(8,128)S(1)}, f32[144,128]{1,0:T(8,128)S(1)}, u32[]{:S(2)}, u32[]{:S(2)}) collective-permute-start(f32[144,128]{1,0:T(8,128)S(1)} %get-tuple-element.29), channel_id=1, source_target_pairs={{0,8},{1,2},{2,1},{3,4},{4,3},{5,6},{6,5},{7,15},{8,0},{9,10},{10,... | collective-permute-start | bytes 221192 | tf_op jit(solution)/shard_map/ppermute | solution.py:705
  10.6 0.0 collective-permute-done.2.refs_4_
  10.6 2.3 %collective-permute-done.3.refs_5_ = f32[144,128]{1,0:T(8,128)S(1)} collective-permute-done((f32[144,128]{1,0:T(8,128)S(1)}, f32[144,128]{1,0:T(8,128)S(1)}, u32[]{:S(2)}, u32[]{:S(2)}) %collective-permute-start.3) | collective-permute-done | bytes 73760 | tf_op jit(solution)/shard_map/ppermute | solution.py:705
  13.0 0.0 copy-done.3
  13.0 0.0 copy-done.5
  13.0 0.0 copy-done.6
  13.0 1.3 %shard_map.114 = (f32[144,384]{1,0:T(8,128)S(1)}, f32[144,384]{1,0:T(8,128)S(1)}, f32[144,384]{1,0:T(8,128)S(1)}, f32[144,384]{1,0:T(8,128)S(1)}, f32[96,256]{1,...) custom-call(f32[128,256]{1,0:T(8,128)S(1)} %copy-done, ...), custom_call_target="tpu_custom_call" | custom-call | tf_op jit(solution)/shard_map/pallas_call | solution.py:683
  14.2 0.0 copy-start.2
  14.3 0.0 copy-start.9
  14.3 16.7 %all_to_all.22 = f32[16,32,128]{2,1,0:T(8,128)S(1)} all-to-all(f32[16,32,128]{2,1,0:T(8,128)S(1)} %bitcast.14), channel_id=1, replica_groups={{0,2,4,6,8,10,12,14,16,18,20,22,24,26,28,30},{1,3,5,7,9,11,13,15,17,19,..., dimensions={0} | all-to-all | bytes 524288 | tf_op jit(solution)/shard_map/all_to_all | solution.py:716
  31.0 0.0 collective-permute-start.4
  31.0 1.5 %collective-permute-done.4.refs_1_ = f32[512,128]{1,0:T(8,128)S(1)} collective-permute-done((f32[512,128]{1,0:T(8,128)S(1)}, f32[512,128]{1,0:T(8,128)S(1)}, u32[]{:S(2)}, u32[]{:S(2)}) %collective-permute-start.4) | collective-permute-done | bytes 262176 | tf_op jit(solution)/shard_map/ppermute | solution.py:717
  32.5 0.0 copy-done.2
  32.6 0.0 copy-done.9
  32.6 4.3 %shard_map.115 = (f32[2,2,48,128]{3,2,1,0:T(8,128)S(1)}, f32[1,1,48,128]{3,2,1,0:T(8,128)S(1)}, f32[2,2,48,128]{3,2,1,0:T(8,128)S(1)}, f32[1,1,48,128]{3,2,1,0:T...) custom-call(f32[512,128]{1,0:T(8,128)S(1)} %bitcast.13, ...), custom_call_target="tpu_custom_call" | custom-call | tf_op jit(solution)/shard_map/pallas_call | solution.py:683
  36.8 9.7 %all_to_all.23 = f32[32,4,128]{2,1,0:T(4,128)S(1)} all-to-all(f32[32,4,128]{2,1,0:T(4,128)S(1)} %bitcast.16), channel_id=1, replica_groups=mesh['gx'=4,'gy'=8] {'gx','gy'}, dimensions={0} | all-to-all | bytes 131072 | tf_op jit(solution)/shard_map/all_to_all | solution.py:710
  46.6 0.0 copy-done.4
  46.6 2.6 %shard_map.116 = (f32[128,256]{1,0:T(8,128)}, f32[128,256]{1,0:T(8,128)}) custom-call(f32[128,128]{1,0:T(8,128)S(1)} %bitcast.15, f32[2,2,48,128]{3,2,1,0:T(8,128)S(1)} %get-tuple-element.38.refs_1_, f32[1,1,48,128]{3,2,1,0:T(8,128)S(1)} %get-tuple-element.39.refs_2_, f32[2,2,48,128]{3,2,1,0:T(8,128)S(1)} %get-tuple-element.40.refs_3_, ...), custom_call_target="tpu_custom_call" | custom-call | tf_op jit(solution)/shard_map/pallas_call | solution.py:683
  (8 shorter events, 0.0 us)
Async XLA Ops:
  0.6 4.0 %copy-start = (f32[128,256]{1,0:T(8,128)S(1)}, f32[128,256]{1,0:T(8,128)}, u32[]{:S(2)}) copy-start(f32[128,256]{1,0:T(8,128)} %refs_0_.3) | copy-start | bytes 393220
  0.7 4.0 %copy-start.1 = (f32[128,256]{1,0:T(8,128)S(1)}, f32[128,256]{1,0:T(8,128)}, u32[]{:S(2)}) copy-start(f32[128,256]{1,0:T(8,128)} %refs_1_.3) | copy-start | bytes 393220
  1.5 5.6 %collective-permute-start = (f32[2,40,256]{2,1,0:T(8,128)S(1)}, f32[2,40,256]{2,1,0:T(8,128)S(1)}, u32[]{:S(2)}, u32[]{:S(2)}) collective-permute-start(f32[2,40,256]{2,1,0:T(8,128)S(1)} %pad_maximum_fusion), channel_id=1, source_target_pairs={{0,8},{8,0},{16,24},{24,16},{1,9},{9,1},{17,25},{25,17},{2,10},{10... | collective-permute-start | bytes 245768 | tf_op jit(solution)/shard_map/ppermute | solution.py:706
  4.7 8.3 %copy-start.3 = (bf16[256,128]{1,0:T(8,128)(2,1)S(1)}, bf16[256,128]{1,0:T(8,128)(2,1)}, u32[]{:S(2)}) copy-start(bf16[256,128]{1,0:T(8,128)(2,1)} %constant.41.clone.refs_7_.refs_9_) | copy-start | bytes 196612
  4.7 8.3 %copy-start.5 = (bf16[384,256]{1,0:T(8,128)(2,1)S(1)}, bf16[384,256]{1,0:T(8,128)(2,1)}, u32[]{:S(2)}) copy-start(bf16[384,256]{1,0:T(8,128)(2,1)} %constant.40.clone.refs_6_) | copy-start | bytes 589828
  4.7 8.3 %copy-start.6 = (bf16[512,128]{1,0:T(8,128)(2,1)S(1)}, bf16[512,128]{1,0:T(8,128)(2,1)}, u32[]{:S(2)}) copy-start(bf16[512,128]{1,0:T(8,128)(2,1)} %constant.42.clone.refs_8_) | copy-start | bytes 393220
  4.7 2.4 %collective-permute-start.1 = (f32[2,40,256]{2,1,0:T(8,128)S(1)}, f32[2,40,256]{2,1,0:T(8,128)S(1)}, u32[]{:S(2)}, u32[]{:S(2)}) collective-permute-start(f32[2,40,256]{2,1,0:T(8,128)S(1)} %pad_maximum_fusion.1), channel_id=1, source_target_pairs={{0,1},{1,0},{2,3},{3,2},{4,5},{5,4},{6,7},{7,6},{8,16},{9,17},{10,... | collective-permute-start | bytes 245768 | tf_op jit(solution)/shard_map/ppermute | solution.py:705
  7.2 3.4 %collective-permute-start.2 = (f32[144,128]{1,0:T(8,128)S(1)}, f32[144,128]{1,0:T(8,128)S(1)}, u32[]{:S(2)}, u32[]{:S(2)}) collective-permute-start(f32[144,128]{1,0:T(8,128)S(1)} %get-tuple-element.28), channel_id=1, source_target_pairs={{0,1},{1,0},{2,3},{3,2},{4,5},{5,4},{6,7},{7,6},{8,9},{9,8},{10,11... | collective-permute-start | bytes 221192 | tf_op jit(solution)/shard_map/ppermute | solution.py:706
  7.3 5.7 %collective-permute-start.3 = (f32[144,128]{1,0:T(8,128)S(1)}, f32[144,128]{1,0:T(8,128)S(1)}, u32[]{:S(2)}, u32[]{:S(2)}) collective-permute-start(f32[144,128]{1,0:T(8,128)S(1)} %get-tuple-element.29), channel_id=1, source_target_pairs={{0,8},{1,2},{2,1},{3,4},{4,3},{5,6},{6,5},{7,15},{8,0},{9,10},{10,... | collective-permute-start | bytes 221192 | tf_op jit(solution)/shard_map/ppermute | solution.py:705
  14.2 18.3 %copy-start.2 = (bf16[512,256]{1,0:T(8,128)(2,1)S(1)}, bf16[512,256]{1,0:T(8,128)(2,1)}, u32[]{:S(2)}) copy-start(bf16[512,256]{1,0:T(8,128)(2,1)} %constant.43.clone.refs_8_) | copy-start | bytes 786436
  14.3 18.3 %copy-start.9 = (bf16[128,128]{1,0:T(8,128)(2,1)S(1)}, bf16[128,128]{1,0:T(8,128)(2,1)}, u32[]{:S(2)}) copy-start(bf16[128,128]{1,0:T(8,128)(2,1)} %constant.44.clone.refs_10_) | copy-start | bytes 98308
  31.0 1.5 %collective-permute-start.4 = (f32[512,128]{1,0:T(8,128)S(1)}, f32[512,128]{1,0:T(8,128)S(1)}, u32[]{:S(2)}, u32[]{:S(2)}) collective-permute-start(f32[512,128]{1,0:T(8,128)S(1)} %bitcast.12), channel_id=1, source_target_pairs={{0,1},{1,0},{2,3},{3,2},{4,5},{5,4},{6,7},{7,6},{8,9},{9,8},{10,11... | collective-permute-start | bytes 786440 | tf_op jit(solution)/shard_map/ppermute | solution.py:717
  32.6 14.0 %copy-start.4 = (bf16[256,384]{1,0:T(8,128)(2,1)S(1)}, bf16[256,384]{1,0:T(8,128)(2,1)}, u32[]{:S(2)}) copy-start(bf16[256,384]{1,0:T(8,128)(2,1)} %constant.47.clone.refs_18_) | copy-start | bytes 589828
  36.8 9.7 %copy-start.7 = (bf16[128,256]{1,0:T(8,128)(2,1)S(1)}, bf16[128,256]{1,0:T(8,128)(2,1)}, u32[]{:S(2)}) copy-start(bf16[128,256]{1,0:T(8,128)(2,1)} %constant.46.clone.refs_17_) | copy-start | bytes 196612
  36.8 9.7 %copy-start.8 = (bf16[256,128]{1,0:T(8,128)(2,1)S(1)}, bf16[256,128]{1,0:T(8,128)(2,1)}, u32[]{:S(2)}) copy-start(bf16[256,128]{1,0:T(8,128)(2,1)} %constant.45.clone.refs_16_) | copy-start | bytes 196612

commit v12 on v10

--- a/solution.py
+++ b/solution.py
@@ -716,13 +716,10 @@
     even = lax.axis_index("gx") % 2 == 0
     last = rows - HALO
 
-    def strips(start, fields):
-        return jnp.stack([lax.dynamic_slice(x, (start, 0), (HALO, columns)) for x in fields])
-
-    fields = (right_side, shift)
-    later = lax.optimization_barrier(fields)
-    rows_a, rows_b = swaps(
-        strips(jnp.where(even, last, 0), later), strips(jnp.where(even, 0, last), fields), "gx", "gy")
+    def strips(start):
+        return jnp.stack([lax.dynamic_slice(x, (start, 0), (HALO, columns)) for x in (right_side, shift)])
+
+    rows_a, rows_b = swaps(strips(jnp.where(even, last, 0)), strips(jnp.where(even, 0, last)), "gx", "gy")
     ext = [(z.ext_rows[l], z.ext_columns[l]) for l in range(3)]
     strip = (strip_rows(z)[1], 128)
     first, second = call(strip_kernel, z, [strip] * 2, [], right_side, shift, rows_a, rows_b)

time: 49.4 us -> 49.6 us (level)
  blocking collectives: 25.9 us -> 26.5 us
    ppermute x2, starting transfers between devices: 4.27 us -> 3.19 us  [swaps(): lax.ppermute(first, axis, [(i, i ^ 1) for i in range(count)])]
    ppermute x2, starting transfers between devices: 2.64 us -> 3.36 us  [swaps(): other = lax.ppermute(second, ('gx', 'gy'), pairs)]
    all_to_all x1, blocking collectives: 16.2 us -> 16.7 us  [gather_by_core(): lax.all_to_all(copies, ('gx', 'gy'), 0, 0, tiled=True, axis_index_groups=...]
where the time goes in v12:
time: 49.6 us; the launch traced here: 49.3 us
  blocking collectives  26.5 us (53%)
  Pallas kernels  8.4 us (17%)
  starting transfers between devices  6.55 us (13%)
  waiting for transfers between devices  6.19 us (12%)
  local copies, waits for them, and re-layouts  0.91 us (2%)
  between operations  0.75 us (2%)
    all_to_all x1, blocking collectives, gather_by_core(): lax.all_to_all(copies, ('gx', 'gy'), 0, 0, tiled=True, axis_index_groups=...  16.7 us
    all_to_all x1, blocking collectives, gather(): return lax.all_to_all(copies, ('gx', 'gy'), 0, 0, tiled=True)  9.74 us
    pallas_call x4, Pallas kernels, call(): pl.pallas_call(lambda *refs: kernel(sizes, *refs), out_shape=shapes, in_s...  8.4 us
    ppermute x2, starting transfers between devices, swaps(): other = lax.ppermute(second, ('gx', 'gy'), pairs)  3.36 us
    ppermute x2, starting transfers between devices, swaps(): lax.ppermute(first, axis, [(i, i ^ 1) for i in range(count)])  3.19 us
    ppermute x2, waiting for transfers between devices, swaps(): other = lax.ppermute(second, ('gx', 'gy'), pairs)  2.33 us
    ppermute x2, waiting for transfers between devices, swaps(): lax.ppermute(first, axis, [(i, i ^ 1) for i in range(count)])  2.33 us
    ppermute x1, waiting for transfers between devices, gather_by_core(): return (own, lax.ppermute(own, 'gy', [(j, j ^ 1) for j in range(ny)]))  1.53 us
  transfers between devices with their start and end apart: 5, of which 3 were waited for; matrix products, arithmetic and copies ran while one was open for 0% of the time, Pallas kernels for 0%

profile of v12, /device:TPU:0, one launch (start us, length us, event | category | flops | bytes accessed | tf_op | source)
XLA Modules:
  0.0 49.3 jit_solution(10261269411874070874)
XLA Ops:
  0.6 0.9 %dynamic-slice_bitcast_fusion = (f32[1,40,256]{2,1,0:T(8,128)S(1)}, f32[1,40,256]{2,1,0:T(8,128)S(1)}, f32[1,40,256]{2,1,0:T(8,128)S(1)}, f32[1,40,256]{2,1,0:T(8,128)S(1)}) fusion(f32[128,256]{1,0:T(8,128)} %refs_1_.3, s32[]{:T(128)S(6)} %select_n.20, s32[]{:T(128)S(6)} %select_n.19, f32[128,256]{1,0:T(8,128)} %refs_0_.3), kind=kLoop, calls=%fused_computation.2 | loop fusion | bytes 327688 | tf_op jit(solution)/shard_map/stack | solution.py:720
  1.5 0.0 copy-start
  1.5 0.0 copy-start.1
  1.5 3.1 %collective-permute-start = (f32[2,40,256]{2,1,0:T(8,128)S(1)}, f32[2,40,256]{2,1,0:T(8,128)S(1)}, u32[]{:S(2)}, u32[]{:S(2)}) collective-permute-start(f32[2,40,256]{2,1,0:T(8,128)S(1)} %pad_maximum_fusion), channel_id=1, source_target_pairs={{0,8},{8,0},{16,24},{24,16},{1,9},{9,1},{17,25},{25,17},{2,10},{10... | collective-permute-start | bytes 245768 | tf_op jit(solution)/shard_map/ppermute | solution.py:698
  4.7 0.0 copy-start.5
  4.7 0.0 copy-start.6
  4.7 0.1 collective-permute-start.1
  4.8 2.3 %collective-permute-done.refs_2_ = f32[2,40,256]{2,1,0:T(8,128)S(1)} collective-permute-done((f32[2,40,256]{2,1,0:T(8,128)S(1)}, f32[2,40,256]{2,1,0:T(8,128)S(1)}, u32[]{:S(2)}, u32[]{:S(2)}) %collective-permute-start) | collective-permute-done | bytes 81952 | tf_op jit(solution)/shard_map/ppermute | solution.py:698
  7.1 0.0 collective-permute-done.1.refs_3_
  7.1 0.0 copy-done
  7.1 0.0 copy-done.1
  7.1 0.1 shard_map.113
  7.3 0.1 collective-permute-start.2
  7.3 3.3 %collective-permute-start.3 = (f32[144,128]{1,0:T(8,128)S(1)}, f32[144,128]{1,0:T(8,128)S(1)}, u32[]{:S(2)}, u32[]{:S(2)}) collective-permute-start(f32[144,128]{1,0:T(8,128)S(1)} %get-tuple-element.25), channel_id=1, source_target_pairs={{0,8},{1,2},{2,1},{3,4},{4,3},{5,6},{6,5},{7,15},{8,0},{9,10},{10,... | collective-permute-start | bytes 221192 | tf_op jit(solution)/shard_map/ppermute | solution.py:697
  10.6 0.0 collective-permute-done.2.refs_4_
  10.6 2.3 %collective-permute-done.3.refs_5_ = f32[144,128]{1,0:T(8,128)S(1)} collective-permute-done((f32[144,128]{1,0:T(8,128)S(1)}, f32[144,128]{1,0:T(8,128)S(1)}, u32[]{:S(2)}, u32[]{:S(2)}) %collective-permute-start.3) | collective-permute-done | bytes 73760 | tf_op jit(solution)/shard_map/ppermute | solution.py:697
  13.0 0.0 copy-done.3
  13.0 0.0 copy-done.5
  13.0 0.0 copy-done.6
  13.0 1.3 %shard_map.114 = (f32[144,384]{1,0:T(8,128)S(1)}, f32[144,384]{1,0:T(8,128)S(1)}, f32[144,384]{1,0:T(8,128)S(1)}, f32[144,384]{1,0:T(8,128)S(1)}, f32[96,256]{1,...) custom-call(f32[128,256]{1,0:T(8,128)S(1)} %copy-done, ...), custom_call_target="tpu_custom_call" | custom-call | tf_op jit(solution)/shard_map/pallas_call | solution.py:675
  14.3 0.0 copy-start.2
  14.3 0.0 copy-start.9
  14.4 16.7 %all_to_all.22 = f32[16,32,128]{2,1,0:T(8,128)S(1)} all-to-all(f32[16,32,128]{2,1,0:T(8,128)S(1)} %bitcast.14), channel_id=1, replica_groups={{0,2,4,6,8,10,12,14,16,18,20,22,24,26,28,30},{1,3,5,7,9,11,13,15,17,19,..., dimensions={0} | all-to-all | bytes 524288 | tf_op jit(solution)/shard_map/all_to_all | solution.py:708
  31.1 0.0 collective-permute-start.4
  31.1 1.5 %collective-permute-done.4.refs_1_ = f32[512,128]{1,0:T(8,128)S(1)} collective-permute-done((f32[512,128]{1,0:T(8,128)S(1)}, f32[512,128]{1,0:T(8,128)S(1)}, u32[]{:S(2)}, u32[]{:S(2)}) %collective-permute-start.4) | collective-permute-done | bytes 262176 | tf_op jit(solution)/shard_map/ppermute | solution.py:709
  32.6 0.0 copy-done.2
  32.6 0.0 copy-done.9
  32.7 4.3 %shard_map.115 = (f32[2,2,48,128]{3,2,1,0:T(8,128)S(1)}, f32[1,1,48,128]{3,2,1,0:T(8,128)S(1)}, f32[2,2,48,128]{3,2,1,0:T(8,128)S(1)}, f32[1,1,48,128]{3,2,1,0:T...) custom-call(f32[512,128]{1,0:T(8,128)S(1)} %bitcast.13, ...), custom_call_target="tpu_custom_call" | custom-call | tf_op jit(solution)/shard_map/pallas_call | solution.py:675
  37.0 9.7 %all_to_all.23 = f32[32,4,128]{2,1,0:T(4,128)S(1)} all-to-all(f32[32,4,128]{2,1,0:T(4,128)S(1)} %bitcast.16), channel_id=1, replica_groups=mesh['gx'=4,'gy'=8] {'gx','gy'}, dimensions={0} | all-to-all | bytes 131072 | tf_op jit(solution)/shard_map/all_to_all | solution.py:702
  46.7 0.0 copy-done.4
  46.7 0.0 copy-done.7
  46.7 2.6 %shard_map.116 = (f32[128,256]{1,0:T(8,128)}, f32[128,256]{1,0:T(8,128)}) custom-call(f32[128,128]{1,0:T(8,128)S(1)} %bitcast.15, f32[2,2,48,128]{3,2,1,0:T(8,128)S(1)} %get-tuple-element.34.refs_1_, f32[1,1,48,128]{3,2,1,0:T(8,128)S(1)} %get-tuple-element.35.refs_2_, f32[2,2,48,128]{3,2,1,0:T(8,128)S(1)} %get-tuple-element.36.refs_3_, ...), custom_call_target="tpu_custom_call" | custom-call | tf_op jit(solution)/shard_map/pallas_call | solution.py:675
  (7 shorter events, 0.0 us)
Async XLA Ops:
  1.5 5.6 %copy-start = (f32[128,256]{1,0:T(8,128)S(1)}, f32[128,256]{1,0:T(8,128)}, u32[]{:S(2)}) copy-start(f32[128,256]{1,0:T(8,128)} %refs_0_.3) | copy-start | bytes 393220
  1.5 5.6 %copy-start.1 = (f32[128,256]{1,0:T(8,128)S(1)}, f32[128,256]{1,0:T(8,128)}, u32[]{:S(2)}) copy-start(f32[128,256]{1,0:T(8,128)} %refs_1_.3) | copy-start | bytes 393220
  1.5 5.6 %collective-permute-start = (f32[2,40,256]{2,1,0:T(8,128)S(1)}, f32[2,40,256]{2,1,0:T(8,128)S(1)}, u32[]{:S(2)}, u32[]{:S(2)}) collective-permute-start(f32[2,40,256]{2,1,0:T(8,128)S(1)} %pad_maximum_fusion), channel_id=1, source_target_pairs={{0,8},{8,0},{16,24},{24,16},{1,9},{9,1},{17,25},{25,17},{2,10},{10... | collective-permute-start | bytes 245768 | tf_op jit(solution)/shard_map/ppermute | solution.py:698
  4.7 8.3 %copy-start.3 = (bf16[256,128]{1,0:T(8,128)(2,1)S(1)}, bf16[256,128]{1,0:T(8,128)(2,1)}, u32[]{:S(2)}) copy-start(bf16[256,128]{1,0:T(8,128)(2,1)} %constant.41.clone.refs_7_.refs_9_) | copy-start | bytes 196612
  4.7 8.3 %copy-start.5 = (bf16[384,256]{1,0:T(8,128)(2,1)S(1)}, bf16[384,256]{1,0:T(8,128)(2,1)}, u32[]{:S(2)}) copy-start(bf16[384,256]{1,0:T(8,128)(2,1)} %constant.40.clone.refs_6_) | copy-start | bytes 589828
  4.7 8.3 %copy-start.6 = (bf16[512,128]{1,0:T(8,128)(2,1)S(1)}, bf16[512,128]{1,0:T(8,128)(2,1)}, u32[]{:S(2)}) copy-start(bf16[512,128]{1,0:T(8,128)(2,1)} %constant.42.clone.refs_8_) | copy-start | bytes 393220
  4.7 2.4 %collective-permute-start.1 = (f32[2,40,256]{2,1,0:T(8,128)S(1)}, f32[2,40,256]{2,1,0:T(8,128)S(1)}, u32[]{:S(2)}, u32[]{:S(2)}) collective-permute-start(f32[2,40,256]{2,1,0:T(8,128)S(1)} %pad_maximum_fusion.1), channel_id=1, source_target_pairs={{0,1},{1,0},{2,3},{3,2},{4,5},{5,4},{6,7},{7,6},{8,16},{9,17},{10,... | collective-permute-start | bytes 245768 | tf_op jit(solution)/shard_map/ppermute | solution.py:697
  7.3 3.4 %collective-permute-start.2 = (f32[144,128]{1,0:T(8,128)S(1)}, f32[144,128]{1,0:T(8,128)S(1)}, u32[]{:S(2)}, u32[]{:S(2)}) collective-permute-start(f32[144,128]{1,0:T(8,128)S(1)} %get-tuple-element.24), channel_id=1, source_target_pairs={{0,1},{1,0},{2,3},{3,2},{4,5},{5,4},{6,7},{7,6},{8,9},{9,8},{10,11... | collective-permute-start | bytes 221192 | tf_op jit(solution)/shard_map/ppermute | solution.py:698
  7.3 5.6 %collective-permute-start.3 = (f32[144,128]{1,0:T(8,128)S(1)}, f32[144,128]{1,0:T(8,128)S(1)}, u32[]{:S(2)}, u32[]{:S(2)}) collective-permute-start(f32[144,128]{1,0:T(8,128)S(1)} %get-tuple-element.25), channel_id=1, source_target_pairs={{0,8},{1,2},{2,1},{3,4},{4,3},{5,6},{6,5},{7,15},{8,0},{9,10},{10,... | collective-permute-start | bytes 221192 | tf_op jit(solution)/shard_map/ppermute | solution.py:697
  14.3 18.3 %copy-start.2 = (bf16[512,256]{1,0:T(8,128)(2,1)S(1)}, bf16[512,256]{1,0:T(8,128)(2,1)}, u32[]{:S(2)}) copy-start(bf16[512,256]{1,0:T(8,128)(2,1)} %constant.43.clone.refs_8_) | copy-start | bytes 786436
  14.3 18.3 %copy-start.9 = (bf16[128,128]{1,0:T(8,128)(2,1)S(1)}, bf16[128,128]{1,0:T(8,128)(2,1)}, u32[]{:S(2)}) copy-start(bf16[128,128]{1,0:T(8,128)(2,1)} %constant.44.clone.refs_10_) | copy-start | bytes 98308
  31.1 1.5 %collective-permute-start.4 = (f32[512,128]{1,0:T(8,128)S(1)}, f32[512,128]{1,0:T(8,128)S(1)}, u32[]{:S(2)}, u32[]{:S(2)}) collective-permute-start(f32[512,128]{1,0:T(8,128)S(1)} %bitcast.12), channel_id=1, source_target_pairs={{0,1},{1,0},{2,3},{3,2},{4,5},{5,4},{6,7},{7,6},{8,9},{9,8},{10,11... | collective-permute-start | bytes 786440 | tf_op jit(solution)/shard_map/ppermute | solution.py:709
  32.6 14.1 %copy-start.4 = (bf16[256,384]{1,0:T(8,128)(2,1)S(1)}, bf16[256,384]{1,0:T(8,128)(2,1)}, u32[]{:S(2)}) copy-start(bf16[256,384]{1,0:T(8,128)(2,1)} %constant.47.clone.refs_18_) | copy-start | bytes 589828
  36.9 9.8 %copy-start.7 = (bf16[128,256]{1,0:T(8,128)(2,1)S(1)}, bf16[128,256]{1,0:T(8,128)(2,1)}, u32[]{:S(2)}) copy-start(bf16[128,256]{1,0:T(8,128)(2,1)} %constant.46.clone.refs_17_) | copy-start | bytes 196612
  37.0 9.8 %copy-start.8 = (bf16[256,128]{1,0:T(8,128)(2,1)S(1)}, bf16[256,128]{1,0:T(8,128)(2,1)}, u32[]{:S(2)}) copy-start(bf16[256,128]{1,0:T(8,128)(2,1)} %constant.45.clone.refs_16_) | copy-start | bytes 196612
